TPU v7x, 128 devices: a whole 4x4x4 slice. The times are simulated.
128 devices in a mesh: replica: 1, data: 2 (over core), table: 64 (over z, y, x).
Axes of the slice: x: 4, y: 4, z: 4, core: 2. Of those that a mesh axis runs over, the one named last changes fastest.
Arguments:
- tokens: bfloat16 [65536, 1024], P(('replica', 'data', 'table'))
- grad_out: bfloat16 [65536, 1024], P(('replica', 'data', 'table'))
- table_u: bfloat16 [16384, 1024], P(('replica', 'table'))
- table_v: bfloat16 [16384, 1024], P(('replica', 'table'))
- wanted_ids: int32 [128, 8192], P(('replica', 'data', 'table'))
- pick_idx: int32 [65536, 8, 16], P(('replica', 'data', 'table'))
- gate_val: float32 [65536, 8, 16], P(('replica', 'data', 'table'))
Outputs:
- output 1: bfloat16 [65536, 1024], P(('replica', 'data', 'table'))
- output 2: bfloat16 [65536, 1024], P(('replica', 'data', 'table'))
- output 3: bfloat16 [16384, 1024], P(('replica', 'table'))
- output 4: bfloat16 [16384, 1024], P(('replica', 'table'))
All inputs are finite; a program needn't handle non-finite values.
Results may differ from a plain program's by a relative error of at most 0.00769059.
Values are sent between devices in bfloat16 or wider.
A program may use at most 1 GiB of HBM per device.

v0:
```python
import math
import jax
import jax.numpy as jnp
from jax import lax
from jax.sharding import PartitionSpec as P, NamedSharding


def gelu_pair(pre_act):
    cdf_val = 0.5 * (1.0 + lax.erf(pre_act * 0.7071067811865476))
    pdf_val = jnp.exp(-0.5 * pre_act * pre_act) * 0.3989422804014327
    return pre_act * cdf_val, cdf_val + pre_act * pdf_val


def token_pass(tok_loc, dy_loc, rows_u, rows_v, pick_loc, gate_loc):
    tok_local, width = tok_loc.shape
    sel_tok = pick_loc.shape[1] * pick_loc.shape[2]
    block_len = math.gcd(tok_local, max(1, 8192 // sel_tok))
    num_blocks = tok_local // block_len
    inputs = (tok_loc.reshape(num_blocks, block_len, width), dy_loc.reshape(num_blocks, block_len, width), pick_loc.reshape(num_blocks, block_len, sel_tok), gate_loc.reshape(num_blocks, block_len, sel_tok))

    def body(acc_pair, block_in):
        acc_u, acc_v = acc_pair
        x_blk, dy_blk, pick_blk, gate_blk = block_in
        sel_u = jnp.take(rows_u, pick_blk, axis=0, mode='clip')
        sel_v = jnp.take(rows_v, pick_blk, axis=0, mode='clip')
        pre_act = jnp.einsum('bsd,bd->bs', sel_u, x_blk, preferred_element_type=jnp.float32)
        act_val, slope_val = gelu_pair(pre_act)
        weight = gate_blk * act_val
        y_blk = jnp.einsum('bs,bsd->bd', weight, sel_v, preferred_element_type=jnp.float32)
        v_dot_dy = jnp.einsum('bsd,bd->bs', sel_v, dy_blk, preferred_element_type=jnp.float32)
        coef_sel = gate_blk * slope_val * v_dot_dy
        dx_blk = jnp.einsum('bs,bsd->bd', coef_sel, sel_u, preferred_element_type=jnp.float32)
        flat_pick = pick_blk.reshape(-1)
        acc_u = acc_u.at[flat_pick].add((coef_sel[:, :, None] * x_blk[:, None, :]).reshape(-1, width))
        acc_v = acc_v.at[flat_pick].add((weight[:, :, None] * dy_blk[:, None, :]).reshape(-1, width))
        return (acc_u, acc_v), (y_blk.astype(jnp.bfloat16), dx_blk.astype(jnp.bfloat16))

    zero_acc = jnp.zeros((rows_u.shape[0], width), jnp.float32)
    (acc_u, acc_v), (y_st, dx_st) = lax.scan(body, (zero_acc, zero_acc), inputs)
    return y_st.reshape(tok_local, width), dx_st.reshape(tok_local, width), acc_u, acc_v


def solution(mesh):
    table_n = mesh.shape['table']
    tok_spec = P(('replica', 'data', 'table'))
    row_spec = P(('replica', 'table'))

    def device_step(tok_loc, dy_loc, u_loc, v_loc, wanted_loc, pick_loc, gate_loc):
        n_local, width = u_loc.shape
        pool_len = wanted_loc.shape[1] // table_n
        owner_base = jnp.arange(table_n, dtype=jnp.int32)[:, None] * n_local
        requests = wanted_loc.reshape(table_n, pool_len) - owner_base
        asked_rows = lax.all_to_all(requests, 'table', 0, 0, tiled=True)
        sent_u = jnp.take(u_loc, asked_rows, axis=0, mode='clip')
        sent_v = jnp.take(v_loc, asked_rows, axis=0, mode='clip')
        rows_u = lax.all_to_all(sent_u, 'table', 0, 0, tiled=True).reshape(table_n * pool_len, width)
        rows_v = lax.all_to_all(sent_v, 'table', 0, 0, tiled=True).reshape(table_n * pool_len, width)
        y_loc, dx_loc, part_u, part_v = token_pass(tok_loc, dy_loc, rows_u, rows_v, pick_loc, gate_loc)
        back_u = lax.all_to_all(part_u.astype(jnp.bfloat16).reshape(table_n, pool_len, width), 'table', 0, 0, tiled=True)
        back_v = lax.all_to_all(part_v.astype(jnp.bfloat16).reshape(table_n, pool_len, width), 'table', 0, 0, tiled=True)
        flat_rows = asked_rows.reshape(-1)
        grad_u = jnp.zeros((n_local, width), jnp.float32).at[flat_rows].add(back_u.reshape(-1, width).astype(jnp.float32))
        grad_v = jnp.zeros((n_local, width), jnp.float32).at[flat_rows].add(back_v.reshape(-1, width).astype(jnp.float32))
        grad_u = lax.psum(grad_u, 'data')
        grad_v = lax.psum(grad_v, 'data')
        return y_loc, dx_loc, grad_u.astype(jnp.bfloat16), grad_v.astype(jnp.bfloat16)

    return jax.shard_map(device_step, mesh=mesh, in_specs=(tok_spec, tok_spec, row_spec, row_spec, tok_spec, tok_spec, tok_spec), out_specs=(tok_spec, tok_spec, row_spec, row_spec), check_vma=False)
```

profile of v0, /device:TPU:1, one launch (start us, length us, event | category | flops | bytes accessed | tf_op | source)
XLA Modules:
  0.0 3965.7 jit_solution(16904698067206796357)
XLA Ops:
  1.6 20.3 all_to_all.26
  22.5 35.4 gather_fusion.2
  64.0 35.5 gather_fusion.3
  99.4 222.9 %all-to-all-done.1 = bf16[64,128,1024]{2,1,0:T(8,128)(2,1)} async-done(((bf16[64,128,1024]{2,1,0:T(8,128)(2,1)}), bf16[64,128,1024]{2,1,0:T(8,128)(2,1)}, u32[]{:S(2)}, u32[]{:S(2)}) %all-to-all-start.1) | async-done | bytes 16777248 | tf_op jit(solution)/shard_map/all_to_all | solution.py:56
  322.4 29.0 all-to-all-start.2
  352.1 259.8 %all-to-all-done.2 = bf16[64,128,1024]{2,1,0:T(8,128)(2,1)} async-done(((bf16[64,128,1024]{2,1,0:T(8,128)(2,1)}), bf16[64,128,1024]{2,1,0:T(8,128)(2,1)}, u32[]{:S(2)}, u32[]{:S(2)}) %all-to-all-start.2) | async-done | bytes 16777248 | tf_op jit(solution)/shard_map/all_to_all | solution.py:57
  611.9 11.3 broadcast_in_dim.29
  634.4 2680.0 %while.16 = (s32[]{:T(128)}, f32[8192,1024]{1,0:T(8,128)}, f32[8192,1024]{1,0:T(8,128)}, bf16[8,64,1024]{2,1,0:T(8,128)(2,1)}, bf16[8,64,1024]{2,1,0:T(8,128)(2,...) while((s32[]{:T(128)}, f32[8192,1024]{1,0:T(8,128)}, ...), condition=%wide.region_3.4_spmd, body=%wide.region_0.3_spmd.sunk | while | flops 100925440 | bytes 461767616 | solution.py:39
  634.5 48.7 %gather_fusion = bf16[8192,1024]{1,0:T(8,128)(2,1)} fusion(bf16[8192,1024]{1,0:T(8,128)(2,1)} %get-tuple-element.242, s32[8192]{0:T(1024)S(1)} %get-tuple-element.203), kind=kCustom, calls=%fused_computation.clone.1 | custom fusion | bytes 33587200 | tf_op jit(solution)/shard_map/while/body/eval_jaxpr/jit(_take)/gather | solution.py:24
  692.9 48.5 %gather_fusion.1 = bf16[8192,1024]{1,0:T(8,128)(2,1)} fusion(bf16[8192,1024]{1,0:T(8,128)(2,1)} %get-tuple-element.244, s32[8192]{0:T(1024)S(1)} %get-tuple-element.203), kind=kCustom, calls=%fused_computation.1.clone.1 | custom fusion | bytes 33587200 | tf_op jit(solution)/shard_map/while/body/eval_jaxpr/jit(_take)/gather | solution.py:25
  773.2 92.5 %scatter_fusion.1 = f32[8192,1024]{1,0:T(8,128)} fusion(f32[8192,1024]{1,0:T(8,128)} %get-tuple-element.225, s32[8192]{0:T(1024)S(1)} %bitcast.145, f32[8192,1024]{1,0:T(8,128)} %bitcast_multiply_fusion.8), kind=kCustom, calls=%fused_computation.5.clone.1 | custom fusion | flops 8388608 | bytes 100696064 | tf_op jit(solution)/shard_map/while/body/eval_jaxpr/scatter-add | solution.py:35
  876.9 92.6 %scatter_fusion = f32[8192,1024]{1,0:T(8,128)} fusion(f32[8192,1024]{1,0:T(8,128)} %get-tuple-element.224, s32[8192]{0:T(1024)S(1)} %bitcast.146, f32[8192,1024]{1,0:T(8,128)} %bitcast_multiply_fusion.7), kind=kCustom, calls=%fused_computation.4.clone.1 | custom fusion | flops 8388608 | bytes 100696064 | tf_op jit(solution)/shard_map/while/body/eval_jaxpr/scatter-add | solution.py:34
  969.5 48.7 %gather_fusion = bf16[8192,1024]{1,0:T(8,128)(2,1)} fusion(bf16[8192,1024]{1,0:T(8,128)(2,1)} %get-tuple-element.242, s32[8192]{0:T(1024)S(1)} %get-tuple-element.203), kind=kCustom, calls=%fused_computation.clone.1 | custom fusion | bytes 33587200 | tf_op jit(solution)/shard_map/while/body/eval_jaxpr/jit(_take)/gather | solution.py:24
  1027.9 48.5 %gather_fusion.1 = bf16[8192,1024]{1,0:T(8,128)(2,1)} fusion(bf16[8192,1024]{1,0:T(8,128)(2,1)} %get-tuple-element.244, s32[8192]{0:T(1024)S(1)} %get-tuple-element.203), kind=kCustom, calls=%fused_computation.1.clone.1 | custom fusion | bytes 33587200 | tf_op jit(solution)/shard_map/while/body/eval_jaxpr/jit(_take)/gather | solution.py:25
  1108.2 92.5 %scatter_fusion.1 = f32[8192,1024]{1,0:T(8,128)} fusion(f32[8192,1024]{1,0:T(8,128)} %get-tuple-element.225, s32[8192]{0:T(1024)S(1)} %bitcast.145, f32[8192,1024]{1,0:T(8,128)} %bitcast_multiply_fusion.8), kind=kCustom, calls=%fused_computation.5.clone.1 | custom fusion | flops 8388608 | bytes 100696064 | tf_op jit(solution)/shard_map/while/body/eval_jaxpr/scatter-add | solution.py:35
  1211.9 92.6 %scatter_fusion = f32[8192,1024]{1,0:T(8,128)} fusion(f32[8192,1024]{1,0:T(8,128)} %get-tuple-element.224, s32[8192]{0:T(1024)S(1)} %bitcast.146, f32[8192,1024]{1,0:T(8,128)} %bitcast_multiply_fusion.7), kind=kCustom, calls=%fused_computation.4.clone.1 | custom fusion | flops 8388608 | bytes 100696064 | tf_op jit(solution)/shard_map/while/body/eval_jaxpr/scatter-add | solution.py:34
  1304.5 48.7 %gather_fusion = bf16[8192,1024]{1,0:T(8,128)(2,1)} fusion(bf16[8192,1024]{1,0:T(8,128)(2,1)} %get-tuple-element.242, s32[8192]{0:T(1024)S(1)} %get-tuple-element.203), kind=kCustom, calls=%fused_computation.clone.1 | custom fusion | bytes 33587200 | tf_op jit(solution)/shard_map/while/body/eval_jaxpr/jit(_take)/gather | solution.py:24
  1362.9 48.5 %gather_fusion.1 = bf16[8192,1024]{1,0:T(8,128)(2,1)} fusion(bf16[8192,1024]{1,0:T(8,128)(2,1)} %get-tuple-element.244, s32[8192]{0:T(1024)S(1)} %get-tuple-element.203), kind=kCustom, calls=%fused_computation.1.clone.1 | custom fusion | bytes 33587200 | tf_op jit(solution)/shard_map/while/body/eval_jaxpr/jit(_take)/gather | solution.py:25
  1443.2 92.5 %scatter_fusion.1 = f32[8192,1024]{1,0:T(8,128)} fusion(f32[8192,1024]{1,0:T(8,128)} %get-tuple-element.225, s32[8192]{0:T(1024)S(1)} %bitcast.145, f32[8192,1024]{1,0:T(8,128)} %bitcast_multiply_fusion.8), kind=kCustom, calls=%fused_computation.5.clone.1 | custom fusion | flops 8388608 | bytes 100696064 | tf_op jit(solution)/shard_map/while/body/eval_jaxpr/scatter-add | solution.py:35
  1546.9 92.6 %scatter_fusion = f32[8192,1024]{1,0:T(8,128)} fusion(f32[8192,1024]{1,0:T(8,128)} %get-tuple-element.224, s32[8192]{0:T(1024)S(1)} %bitcast.146, f32[8192,1024]{1,0:T(8,128)} %bitcast_multiply_fusion.7), kind=kCustom, calls=%fused_computation.4.clone.1 | custom fusion | flops 8388608 | bytes 100696064 | tf_op jit(solution)/shard_map/while/body/eval_jaxpr/scatter-add | solution.py:34
  1639.5 48.7 %gather_fusion = bf16[8192,1024]{1,0:T(8,128)(2,1)} fusion(bf16[8192,1024]{1,0:T(8,128)(2,1)} %get-tuple-element.242, s32[8192]{0:T(1024)S(1)} %get-tuple-element.203), kind=kCustom, calls=%fused_computation.clone.1 | custom fusion | bytes 33587200 | tf_op jit(solution)/shard_map/while/body/eval_jaxpr/jit(_take)/gather | solution.py:24
  1697.9 48.5 %gather_fusion.1 = bf16[8192,1024]{1,0:T(8,128)(2,1)} fusion(bf16[8192,1024]{1,0:T(8,128)(2,1)} %get-tuple-element.244, s32[8192]{0:T(1024)S(1)} %get-tuple-element.203), kind=kCustom, calls=%fused_computation.1.clone.1 | custom fusion | bytes 33587200 | tf_op jit(solution)/shard_map/while/body/eval_jaxpr/jit(_take)/gather | solution.py:25
  1778.2 92.5 %scatter_fusion.1 = f32[8192,1024]{1,0:T(8,128)} fusion(f32[8192,1024]{1,0:T(8,128)} %get-tuple-element.225, s32[8192]{0:T(1024)S(1)} %bitcast.145, f32[8192,1024]{1,0:T(8,128)} %bitcast_multiply_fusion.8), kind=kCustom, calls=%fused_computation.5.clone.1 | custom fusion | flops 8388608 | bytes 100696064 | tf_op jit(solution)/shard_map/while/body/eval_jaxpr/scatter-add | solution.py:35
  1881.9 92.6 %scatter_fusion = f32[8192,1024]{1,0:T(8,128)} fusion(f32[8192,1024]{1,0:T(8,128)} %get-tuple-element.224, s32[8192]{0:T(1024)S(1)} %bitcast.146, f32[8192,1024]{1,0:T(8,128)} %bitcast_multiply_fusion.7), kind=kCustom, calls=%fused_computation.4.clone.1 | custom fusion | flops 8388608 | bytes 100696064 | tf_op jit(solution)/shard_map/while/body/eval_jaxpr/scatter-add | solution.py:34
  1974.5 48.7 %gather_fusion = bf16[8192,1024]{1,0:T(8,128)(2,1)} fusion(bf16[8192,1024]{1,0:T(8,128)(2,1)} %get-tuple-element.242, s32[8192]{0:T(1024)S(1)} %get-tuple-element.203), kind=kCustom, calls=%fused_computation.clone.1 | custom fusion | bytes 33587200 | tf_op jit(solution)/shard_map/while/body/eval_jaxpr/jit(_take)/gather | solution.py:24
  2032.9 48.5 %gather_fusion.1 = bf16[8192,1024]{1,0:T(8,128)(2,1)} fusion(bf16[8192,1024]{1,0:T(8,128)(2,1)} %get-tuple-element.244, s32[8192]{0:T(1024)S(1)} %get-tuple-element.203), kind=kCustom, calls=%fused_computation.1.clone.1 | custom fusion | bytes 33587200 | tf_op jit(solution)/shard_map/while/body/eval_jaxpr/jit(_take)/gather | solution.py:25
  2113.2 92.5 %scatter_fusion.1 = f32[8192,1024]{1,0:T(8,128)} fusion(f32[8192,1024]{1,0:T(8,128)} %get-tuple-element.225, s32[8192]{0:T(1024)S(1)} %bitcast.145, f32[8192,1024]{1,0:T(8,128)} %bitcast_multiply_fusion.8), kind=kCustom, calls=%fused_computation.5.clone.1 | custom fusion | flops 8388608 | bytes 100696064 | tf_op jit(solution)/shard_map/while/body/eval_jaxpr/scatter-add | solution.py:35
  2216.9 92.6 %scatter_fusion = f32[8192,1024]{1,0:T(8,128)} fusion(f32[8192,1024]{1,0:T(8,128)} %get-tuple-element.224, s32[8192]{0:T(1024)S(1)} %bitcast.146, f32[8192,1024]{1,0:T(8,128)} %bitcast_multiply_fusion.7), kind=kCustom, calls=%fused_computation.4.clone.1 | custom fusion | flops 8388608 | bytes 100696064 | tf_op jit(solution)/shard_map/while/body/eval_jaxpr/scatter-add | solution.py:34
  2309.5 48.7 %gather_fusion = bf16[8192,1024]{1,0:T(8,128)(2,1)} fusion(bf16[8192,1024]{1,0:T(8,128)(2,1)} %get-tuple-element.242, s32[8192]{0:T(1024)S(1)} %get-tuple-element.203), kind=kCustom, calls=%fused_computation.clone.1 | custom fusion | bytes 33587200 | tf_op jit(solution)/shard_map/while/body/eval_jaxpr/jit(_take)/gather | solution.py:24
  2367.9 48.5 %gather_fusion.1 = bf16[8192,1024]{1,0:T(8,128)(2,1)} fusion(bf16[8192,1024]{1,0:T(8,128)(2,1)} %get-tuple-element.244, s32[8192]{0:T(1024)S(1)} %get-tuple-element.203), kind=kCustom, calls=%fused_computation.1.clone.1 | custom fusion | bytes 33587200 | tf_op jit(solution)/shard_map/while/body/eval_jaxpr/jit(_take)/gather | solution.py:25
  2448.2 92.5 %scatter_fusion.1 = f32[8192,1024]{1,0:T(8,128)} fusion(f32[8192,1024]{1,0:T(8,128)} %get-tuple-element.225, s32[8192]{0:T(1024)S(1)} %bitcast.145, f32[8192,1024]{1,0:T(8,128)} %bitcast_multiply_fusion.8), kind=kCustom, calls=%fused_computation.5.clone.1 | custom fusion | flops 8388608 | bytes 100696064 | tf_op jit(solution)/shard_map/while/body/eval_jaxpr/scatter-add | solution.py:35
  2551.9 92.6 %scatter_fusion = f32[8192,1024]{1,0:T(8,128)} fusion(f32[8192,1024]{1,0:T(8,128)} %get-tuple-element.224, s32[8192]{0:T(1024)S(1)} %bitcast.146, f32[8192,1024]{1,0:T(8,128)} %bitcast_multiply_fusion.7), kind=kCustom, calls=%fused_computation.4.clone.1 | custom fusion | flops 8388608 | bytes 100696064 | tf_op jit(solution)/shard_map/while/body/eval_jaxpr/scatter-add | solution.py:34
  2644.5 48.7 %gather_fusion = bf16[8192,1024]{1,0:T(8,128)(2,1)} fusion(bf16[8192,1024]{1,0:T(8,128)(2,1)} %get-tuple-element.242, s32[8192]{0:T(1024)S(1)} %get-tuple-element.203), kind=kCustom, calls=%fused_computation.clone.1 | custom fusion | bytes 33587200 | tf_op jit(solution)/shard_map/while/body/eval_jaxpr/jit(_take)/gather | solution.py:24
  2702.9 48.5 %gather_fusion.1 = bf16[8192,1024]{1,0:T(8,128)(2,1)} fusion(bf16[8192,1024]{1,0:T(8,128)(2,1)} %get-tuple-element.244, s32[8192]{0:T(1024)S(1)} %get-tuple-element.203), kind=kCustom, calls=%fused_computation.1.clone.1 | custom fusion | bytes 33587200 | tf_op jit(solution)/shard_map/while/body/eval_jaxpr/jit(_take)/gather | solution.py:25
  2783.2 92.5 %scatter_fusion.1 = f32[8192,1024]{1,0:T(8,128)} fusion(f32[8192,1024]{1,0:T(8,128)} %get-tuple-element.225, s32[8192]{0:T(1024)S(1)} %bitcast.145, f32[8192,1024]{1,0:T(8,128)} %bitcast_multiply_fusion.8), kind=kCustom, calls=%fused_computation.5.clone.1 | custom fusion | flops 8388608 | bytes 100696064 | tf_op jit(solution)/shard_map/while/body/eval_jaxpr/scatter-add | solution.py:35
  2886.9 92.6 %scatter_fusion = f32[8192,1024]{1,0:T(8,128)} fusion(f32[8192,1024]{1,0:T(8,128)} %get-tuple-element.224, s32[8192]{0:T(1024)S(1)} %bitcast.146, f32[8192,1024]{1,0:T(8,128)} %bitcast_multiply_fusion.7), kind=kCustom, calls=%fused_computation.4.clone.1 | custom fusion | flops 8388608 | bytes 100696064 | tf_op jit(solution)/shard_map/while/body/eval_jaxpr/scatter-add | solution.py:34
  2979.5 48.7 %gather_fusion = bf16[8192,1024]{1,0:T(8,128)(2,1)} fusion(bf16[8192,1024]{1,0:T(8,128)(2,1)} %get-tuple-element.242, s32[8192]{0:T(1024)S(1)} %get-tuple-element.203), kind=kCustom, calls=%fused_computation.clone.1 | custom fusion | bytes 33587200 | tf_op jit(solution)/shard_map/while/body/eval_jaxpr/jit(_take)/gather | solution.py:24
  3037.9 48.5 %gather_fusion.1 = bf16[8192,1024]{1,0:T(8,128)(2,1)} fusion(bf16[8192,1024]{1,0:T(8,128)(2,1)} %get-tuple-element.244, s32[8192]{0:T(1024)S(1)} %get-tuple-element.203), kind=kCustom, calls=%fused_computation.1.clone.1 | custom fusion | bytes 33587200 | tf_op jit(solution)/shard_map/while/body/eval_jaxpr/jit(_take)/gather | solution.py:25
  3118.2 92.5 %scatter_fusion.1 = f32[8192,1024]{1,0:T(8,128)} fusion(f32[8192,1024]{1,0:T(8,128)} %get-tuple-element.225, s32[8192]{0:T(1024)S(1)} %bitcast.145, f32[8192,1024]{1,0:T(8,128)} %bitcast_multiply_fusion.8), kind=kCustom, calls=%fused_computation.5.clone.1 | custom fusion | flops 8388608 | bytes 100696064 | tf_op jit(solution)/shard_map/while/body/eval_jaxpr/scatter-add | solution.py:35
  3221.9 92.6 %scatter_fusion = f32[8192,1024]{1,0:T(8,128)} fusion(f32[8192,1024]{1,0:T(8,128)} %get-tuple-element.224, s32[8192]{0:T(1024)S(1)} %bitcast.146, f32[8192,1024]{1,0:T(8,128)} %bitcast_multiply_fusion.7), kind=kCustom, calls=%fused_computation.4.clone.1 | custom fusion | flops 8388608 | bytes 100696064 | tf_op jit(solution)/shard_map/while/body/eval_jaxpr/scatter-add | solution.py:34
  3314.4 17.5 convert_element_type.50
  3332.0 18.3 all-to-all-start.4
  3350.3 17.5 convert_element_type.46
  3367.8 246.7 %all-to-all-done.4 = bf16[64,128,1024]{2,1,0:T(8,128)(2,1)} async-done(((bf16[64,128,1024]{2,1,0:T(8,128)(2,1)}), bf16[64,128,1024]{2,1,0:T(8,128)(2,1)}, u32[]{:S(2)}, u32[]{:S(2)}) %all-to-all-start.4) | async-done | bytes 16777248 | tf_op jit(solution)/shard_map/all_to_all | solution.py:60
  3620.5 68.8 %scatter_custom_fusion.3 = f32[256,1024]{1,0:T(8,128)S(1)} fusion(s32[8192]{0:T(1024)S(1)} %bitcast.153, bf16[8192,1024]{1,0:T(8,128)(2,1)} %bitcast.45, f32[]{:T(128)} %constant.9.clone.1), kind=kCustom, calls=%fused_computation.36 | custom fusion | flops 16777216 | bytes 17825796 | tf_op jit(solution)/shard_map/scatter-add | solution.py:63
  3689.3 184.7 %all-to-all-done.3 = bf16[64,128,1024]{2,1,0:T(8,128)(2,1)} async-done(((bf16[64,128,1024]{2,1,0:T(8,128)(2,1)}), bf16[64,128,1024]{2,1,0:T(8,128)(2,1)}, u32[]{:S(2)}, u32[]{:S(2)}) %all-to-all-start.3) | async-done | bytes 16777248 | tf_op jit(solution)/shard_map/all_to_all | solution.py:59
  3874.1 68.7 %scatter_custom_fusion.2 = f32[256,1024]{1,0:T(8,128)S(1)} fusion(s32[8192]{0:T(1024)S(1)} %bitcast.154, bf16[8192,1024]{1,0:T(8,128)(2,1)} %bitcast.44, f32[]{:T(128)} %constant.9.clone.1), kind=kCustom, calls=%fused_computation.38 | custom fusion | flops 16777216 | bytes 17825796 | tf_op jit(solution)/shard_map/scatter-add | solution.py:62
  3942.8 22.8 all-reduce.2
  (307 shorter events, 445.7 us)
Async XLA Ops:
  58.0 264.4 %all-to-all-start.1 = ((bf16[64,128,1024]{2,1,0:T(8,128)(2,1)}), bf16[64,128,1024]{2,1,0:T(8,128)(2,1)}, u32[]{:S(2)}, u32[]{:S(2)}) async-start(bf16[64,128,1024]{2,1,0:T(8,128)(2,1)} %bitcast.140), calls=%async_computation.1 | async-start | bytes 33554432 | tf_op jit(solution)/shard_map/all_to_all | solution.py:56
  322.4 289.5 %all-to-all-start.2 = ((bf16[64,128,1024]{2,1,0:T(8,128)(2,1)}), bf16[64,128,1024]{2,1,0:T(8,128)(2,1)}, u32[]{:S(2)}, u32[]{:S(2)}) async-start(bf16[64,128,1024]{2,1,0:T(8,128)(2,1)} %bitcast.137), calls=%async_computation.2 | async-start | bytes 33554432 | tf_op jit(solution)/shard_map/all_to_all | solution.py:57
  634.4 116.1 %copy-start.8 = (f32[8,64,128]{2,1,0:T(8,128)}, f32[8,64,128]{2,1,0:T(8,128)S(1)}, u32[]{:S(2)}) copy-start(f32[8,64,128]{2,1,0:T(8,128)S(1)} %get-tuple-element.241) | copy-start | bytes 786436 | tf_op jit(solution)/shard_map/while
  773.1 92.6 %copy-start.3 = (f32[64,1024]{1,0:T(8,128)S(1)}, f32[64,1024]{1,0:T(8,128)}, u32[]{:S(2)}) copy-start(f32[64,1024]{1,0:T(8,128)} %get-tuple-element.202) | copy-start | bytes 786436 | tf_op jit(solution)/shard_map/while
  773.2 92.6 %copy-start.5 = (f32[64,128]{1,0:T(8,128)S(1)}, f32[64,128]{1,0:T(8,128)}, u32[]{:S(2)}) copy-start(f32[64,128]{1,0:T(8,128)} %copy-done.4) | copy-start | bytes 98308 | tf_op jit(solution)/shard_map/while
  876.9 92.6 %copy-start.7 = (s32[8,64,128]{2,1,0:T(8,128)S(1)}, s32[8,64,128]{2,1,0:T(8,128)}, u32[]{:S(2)}) copy-start(s32[8,64,128]{2,1,0:T(8,128)} %copy-done.6) | copy-start | bytes 786436 | tf_op jit(solution)/shard_map/while
  876.9 92.6 %copy-start.9 = (f32[8,64,128]{2,1,0:T(8,128)S(1)}, f32[8,64,128]{2,1,0:T(8,128)}, u32[]{:S(2)}) copy-start(f32[8,64,128]{2,1,0:T(8,128)} %copy-done.8) | copy-start | bytes 786436 | tf_op jit(solution)/shard_map/while
  969.4 48.8 %copy-start.6 = (s32[8,64,128]{2,1,0:T(8,128)}, s32[8,64,128]{2,1,0:T(8,128)S(1)}, u32[]{:S(2)}) copy-start(s32[8,64,128]{2,1,0:T(8,128)S(1)} %get-tuple-element.240) | copy-start | bytes 786436 | tf_op jit(solution)/shard_map/while
  969.4 116.1 %copy-start.8 = (f32[8,64,128]{2,1,0:T(8,128)}, f32[8,64,128]{2,1,0:T(8,128)S(1)}, u32[]{:S(2)}) copy-start(f32[8,64,128]{2,1,0:T(8,128)S(1)} %get-tuple-element.241) | copy-start | bytes 786436 | tf_op jit(solution)/shard_map/while
  1108.1 92.6 %copy-start.3 = (f32[64,1024]{1,0:T(8,128)S(1)}, f32[64,1024]{1,0:T(8,128)}, u32[]{:S(2)}) copy-start(f32[64,1024]{1,0:T(8,128)} %get-tuple-element.202) | copy-start | bytes 786436 | tf_op jit(solution)/shard_map/while
  1108.2 92.6 %copy-start.5 = (f32[64,128]{1,0:T(8,128)S(1)}, f32[64,128]{1,0:T(8,128)}, u32[]{:S(2)}) copy-start(f32[64,128]{1,0:T(8,128)} %copy-done.4) | copy-start | bytes 98308 | tf_op jit(solution)/shard_map/while
  1211.9 92.6 %copy-start.7 = (s32[8,64,128]{2,1,0:T(8,128)S(1)}, s32[8,64,128]{2,1,0:T(8,128)}, u32[]{:S(2)}) copy-start(s32[8,64,128]{2,1,0:T(8,128)} %copy-done.6) | copy-start | bytes 786436 | tf_op jit(solution)/shard_map/while
  1211.9 92.6 %copy-start.9 = (f32[8,64,128]{2,1,0:T(8,128)S(1)}, f32[8,64,128]{2,1,0:T(8,128)}, u32[]{:S(2)}) copy-start(f32[8,64,128]{2,1,0:T(8,128)} %copy-done.8) | copy-start | bytes 786436 | tf_op jit(solution)/shard_map/while
  1304.4 116.1 %copy-start.8 = (f32[8,64,128]{2,1,0:T(8,128)}, f32[8,64,128]{2,1,0:T(8,128)S(1)}, u32[]{:S(2)}) copy-start(f32[8,64,128]{2,1,0:T(8,128)S(1)} %get-tuple-element.241) | copy-start | bytes 786436 | tf_op jit(solution)/shard_map/while
  1443.2 92.6 %copy-start.3 = (f32[64,1024]{1,0:T(8,128)S(1)}, f32[64,1024]{1,0:T(8,128)}, u32[]{:S(2)}) copy-start(f32[64,1024]{1,0:T(8,128)} %get-tuple-element.202) | copy-start | bytes 786436 | tf_op jit(solution)/shard_map/while
  1443.2 92.6 %copy-start.5 = (f32[64,128]{1,0:T(8,128)S(1)}, f32[64,128]{1,0:T(8,128)}, u32[]{:S(2)}) copy-start(f32[64,128]{1,0:T(8,128)} %copy-done.4) | copy-start | bytes 98308 | tf_op jit(solution)/shard_map/while
  1546.9 92.6 %copy-start.7 = (s32[8,64,128]{2,1,0:T(8,128)S(1)}, s32[8,64,128]{2,1,0:T(8,128)}, u32[]{:S(2)}) copy-start(s32[8,64,128]{2,1,0:T(8,128)} %copy-done.6) | copy-start | bytes 786436 | tf_op jit(solution)/shard_map/while
  1546.9 92.6 %copy-start.9 = (f32[8,64,128]{2,1,0:T(8,128)S(1)}, f32[8,64,128]{2,1,0:T(8,128)}, u32[]{:S(2)}) copy-start(f32[8,64,128]{2,1,0:T(8,128)} %copy-done.8) | copy-start | bytes 786436 | tf_op jit(solution)/shard_map/while
  1639.4 48.8 %copy-start.6 = (s32[8,64,128]{2,1,0:T(8,128)}, s32[8,64,128]{2,1,0:T(8,128)S(1)}, u32[]{:S(2)}) copy-start(s32[8,64,128]{2,1,0:T(8,128)S(1)} %get-tuple-element.240) | copy-start | bytes 786436 | tf_op jit(solution)/shard_map/while
  1639.4 116.1 %copy-start.8 = (f32[8,64,128]{2,1,0:T(8,128)}, f32[8,64,128]{2,1,0:T(8,128)S(1)}, u32[]{:S(2)}) copy-start(f32[8,64,128]{2,1,0:T(8,128)S(1)} %get-tuple-element.241) | copy-start | bytes 786436 | tf_op jit(solution)/shard_map/while
  1778.2 92.6 %copy-start.3 = (f32[64,1024]{1,0:T(8,128)S(1)}, f32[64,1024]{1,0:T(8,128)}, u32[]{:S(2)}) copy-start(f32[64,1024]{1,0:T(8,128)} %get-tuple-element.202) | copy-start | bytes 786436 | tf_op jit(solution)/shard_map/while
  1778.2 92.6 %copy-start.5 = (f32[64,128]{1,0:T(8,128)S(1)}, f32[64,128]{1,0:T(8,128)}, u32[]{:S(2)}) copy-start(f32[64,128]{1,0:T(8,128)} %copy-done.4) | copy-start | bytes 98308 | tf_op jit(solution)/shard_map/while
  1881.9 92.6 %copy-start.7 = (s32[8,64,128]{2,1,0:T(8,128)S(1)}, s32[8,64,128]{2,1,0:T(8,128)}, u32[]{:S(2)}) copy-start(s32[8,64,128]{2,1,0:T(8,128)} %copy-done.6) | copy-start | bytes 786436 | tf_op jit(solution)/shard_map/while
  1881.9 92.6 %copy-start.9 = (f32[8,64,128]{2,1,0:T(8,128)S(1)}, f32[8,64,128]{2,1,0:T(8,128)}, u32[]{:S(2)}) copy-start(f32[8,64,128]{2,1,0:T(8,128)} %copy-done.8) | copy-start | bytes 786436 | tf_op jit(solution)/shard_map/while
  1974.4 48.8 %copy-start.6 = (s32[8,64,128]{2,1,0:T(8,128)}, s32[8,64,128]{2,1,0:T(8,128)S(1)}, u32[]{:S(2)}) copy-start(s32[8,64,128]{2,1,0:T(8,128)S(1)} %get-tuple-element.240) | copy-start | bytes 786436 | tf_op jit(solution)/shard_map/while
  1974.4 116.1 %copy-start.8 = (f32[8,64,128]{2,1,0:T(8,128)}, f32[8,64,128]{2,1,0:T(8,128)S(1)}, u32[]{:S(2)}) copy-start(f32[8,64,128]{2,1,0:T(8,128)S(1)} %get-tuple-element.241) | copy-start | bytes 786436 | tf_op jit(solution)/shard_map/while
  2113.2 92.6 %copy-start.3 = (f32[64,1024]{1,0:T(8,128)S(1)}, f32[64,1024]{1,0:T(8,128)}, u32[]{:S(2)}) copy-start(f32[64,1024]{1,0:T(8,128)} %get-tuple-element.202) | copy-start | bytes 786436 | tf_op jit(solution)/shard_map/while
  2113.2 92.6 %copy-start.5 = (f32[64,128]{1,0:T(8,128)S(1)}, f32[64,128]{1,0:T(8,128)}, u32[]{:S(2)}) copy-start(f32[64,128]{1,0:T(8,128)} %copy-done.4) | copy-start | bytes 98308 | tf_op jit(solution)/shard_map/while
  2216.9 92.6 %copy-start.7 = (s32[8,64,128]{2,1,0:T(8,128)S(1)}, s32[8,64,128]{2,1,0:T(8,128)}, u32[]{:S(2)}) copy-start(s32[8,64,128]{2,1,0:T(8,128)} %copy-done.6) | copy-start | bytes 786436 | tf_op jit(solution)/shard_map/while
  2216.9 92.6 %copy-start.9 = (f32[8,64,128]{2,1,0:T(8,128)S(1)}, f32[8,64,128]{2,1,0:T(8,128)}, u32[]{:S(2)}) copy-start(f32[8,64,128]{2,1,0:T(8,128)} %copy-done.8) | copy-start | bytes 786436 | tf_op jit(solution)/shard_map/while
  2309.4 116.1 %copy-start.8 = (f32[8,64,128]{2,1,0:T(8,128)}, f32[8,64,128]{2,1,0:T(8,128)S(1)}, u32[]{:S(2)}) copy-start(f32[8,64,128]{2,1,0:T(8,128)S(1)} %get-tuple-element.241) | copy-start | bytes 786436 | tf_op jit(solution)/shard_map/while
  2448.2 92.6 %copy-start.3 = (f32[64,1024]{1,0:T(8,128)S(1)}, f32[64,1024]{1,0:T(8,128)}, u32[]{:S(2)}) copy-start(f32[64,1024]{1,0:T(8,128)} %get-tuple-element.202) | copy-start | bytes 786436 | tf_op jit(solution)/shard_map/while
  2448.2 92.6 %copy-start.5 = (f32[64,128]{1,0:T(8,128)S(1)}, f32[64,128]{1,0:T(8,128)}, u32[]{:S(2)}) copy-start(f32[64,128]{1,0:T(8,128)} %copy-done.4) | copy-start | bytes 98308 | tf_op jit(solution)/shard_map/while
  2551.9 92.6 %copy-start.7 = (s32[8,64,128]{2,1,0:T(8,128)S(1)}, s32[8,64,128]{2,1,0:T(8,128)}, u32[]{:S(2)}) copy-start(s32[8,64,128]{2,1,0:T(8,128)} %copy-done.6) | copy-start | bytes 786436 | tf_op jit(solution)/shard_map/while
  2551.9 92.6 %copy-start.9 = (f32[8,64,128]{2,1,0:T(8,128)S(1)}, f32[8,64,128]{2,1,0:T(8,128)}, u32[]{:S(2)}) copy-start(f32[8,64,128]{2,1,0:T(8,128)} %copy-done.8) | copy-start | bytes 786436 | tf_op jit(solution)/shard_map/while
  2644.4 116.1 %copy-start.8 = (f32[8,64,128]{2,1,0:T(8,128)}, f32[8,64,128]{2,1,0:T(8,128)S(1)}, u32[]{:S(2)}) copy-start(f32[8,64,128]{2,1,0:T(8,128)S(1)} %get-tuple-element.241) | copy-start | bytes 786436 | tf_op jit(solution)/shard_map/while
  2783.2 92.6 %copy-start.3 = (f32[64,1024]{1,0:T(8,128)S(1)}, f32[64,1024]{1,0:T(8,128)}, u32[]{:S(2)}) copy-start(f32[64,1024]{1,0:T(8,128)} %get-tuple-element.202) | copy-start | bytes 786436 | tf_op jit(solution)/shard_map/while
  2783.2 92.6 %copy-start.5 = (f32[64,128]{1,0:T(8,128)S(1)}, f32[64,128]{1,0:T(8,128)}, u32[]{:S(2)}) copy-start(f32[64,128]{1,0:T(8,128)} %copy-done.4) | copy-start | bytes 98308 | tf_op jit(solution)/shard_map/while
  2886.9 92.6 %copy-start.7 = (s32[8,64,128]{2,1,0:T(8,128)S(1)}, s32[8,64,128]{2,1,0:T(8,128)}, u32[]{:S(2)}) copy-start(s32[8,64,128]{2,1,0:T(8,128)} %copy-done.6) | copy-start | bytes 786436 | tf_op jit(solution)/shard_map/while
  2886.9 92.6 %copy-start.9 = (f32[8,64,128]{2,1,0:T(8,128)S(1)}, f32[8,64,128]{2,1,0:T(8,128)}, u32[]{:S(2)}) copy-start(f32[8,64,128]{2,1,0:T(8,128)} %copy-done.8) | copy-start | bytes 786436 | tf_op jit(solution)/shard_map/while
  2979.4 116.1 %copy-start.8 = (f32[8,64,128]{2,1,0:T(8,128)}, f32[8,64,128]{2,1,0:T(8,128)S(1)}, u32[]{:S(2)}) copy-start(f32[8,64,128]{2,1,0:T(8,128)S(1)} %get-tuple-element.241) | copy-start | bytes 786436 | tf_op jit(solution)/shard_map/while
  3118.2 92.6 %copy-start.3 = (f32[64,1024]{1,0:T(8,128)S(1)}, f32[64,1024]{1,0:T(8,128)}, u32[]{:S(2)}) copy-start(f32[64,1024]{1,0:T(8,128)} %get-tuple-element.202) | copy-start | bytes 786436 | tf_op jit(solution)/shard_map/while
  3118.2 92.6 %copy-start.5 = (f32[64,128]{1,0:T(8,128)S(1)}, f32[64,128]{1,0:T(8,128)}, u32[]{:S(2)}) copy-start(f32[64,128]{1,0:T(8,128)} %copy-done.4) | copy-start | bytes 98308 | tf_op jit(solution)/shard_map/while
  3221.9 92.6 %copy-start.7 = (s32[8,64,128]{2,1,0:T(8,128)S(1)}, s32[8,64,128]{2,1,0:T(8,128)}, u32[]{:S(2)}) copy-start(s32[8,64,128]{2,1,0:T(8,128)} %copy-done.6) | copy-start | bytes 786436 | tf_op jit(solution)/shard_map/while
  3221.9 92.6 %copy-start.9 = (f32[8,64,128]{2,1,0:T(8,128)S(1)}, f32[8,64,128]{2,1,0:T(8,128)}, u32[]{:S(2)}) copy-start(f32[8,64,128]{2,1,0:T(8,128)} %copy-done.8) | copy-start | bytes 786436 | tf_op jit(solution)/shard_map/while
  3332.0 282.5 %all-to-all-start.4 = ((bf16[64,128,1024]{2,1,0:T(8,128)(2,1)}), bf16[64,128,1024]{2,1,0:T(8,128)(2,1)}, u32[]{:S(2)}, u32[]{:S(2)}) async-start(bf16[64,128,1024]{2,1,0:T(8,128)(2,1)} %bitcast.139), calls=%async_computation.4 | async-start | bytes 33554432 | tf_op jit(solution)/shard_map/all_to_all | solution.py:60
  3614.5 259.6 %all-to-all-start.3 = ((bf16[64,128,1024]{2,1,0:T(8,128)(2,1)}), bf16[64,128,1024]{2,1,0:T(8,128)(2,1)}, u32[]{:S(2)}, u32[]{:S(2)}) async-start(bf16[64,128,1024]{2,1,0:T(8,128)(2,1)} %bitcast.138), calls=%async_computation.3 | async-start | bytes 33554432 | tf_op jit(solution)/shard_map/all_to_all | solution.py:59
  3620.5 345.1 %copy-start.1 = (bf16[256,1024]{1,0:T(8,128)(2,1)S(1)}, bf16[256,1024]{1,0:T(8,128)(2,1)}, u32[]{:S(2)}) copy-start(bf16[256,1024]{1,0:T(8,128)(2,1)} %param.11) | copy-start | bytes 1572868
  (51 other events, 883.0 us)
where the time goes:
time: 3980 us; the launch traced here: 3970 us
  other arithmetic  1850 us (46%)
  waiting for transfers between devices  914 us (23%)
  local copies, waits for them, and re-layouts  880 us (22%)
  matrix products  214 us (5%)
  starting transfers between devices  59.2 us (1%)
  blocking collectives  43.1 us (1%)
    scatter-add x8, other arithmetic, body(): acc_u.at[flat_pick]  740 us
    scatter-add x8, other arithmetic, body(): acc_v.at[flat_pick]  740 us
    gather x8, local copies, waits for them, and re-layouts, body(): sel_u = jnp.take(rows_u, pick_blk, axis=0, mode='clip')  390 us
    gather x8, local copies, waits for them, and re-layouts, body(): sel_v = jnp.take(rows_v, pick_blk, axis=0, mode='clip')  388 us
    all_to_all x1, waiting for transfers between devices, device_step(): lax.all_to_all(sent_v, 'table', 0, 0, tiled=True)  260 us
    all_to_all x1, waiting for transfers between devices, device_step(): lax.all_to_all(part_v.astype(jnp.bfloat16).reshape(table_n, pool_len, wid...  247 us
    all_to_all x1, waiting for transfers between devices, device_step(): lax.all_to_all(sent_u, 'table', 0, 0, tiled=True)  223 us
    all_to_all x1, waiting for transfers between devices, device_step(): lax.all_to_all(part_u.astype(jnp.bfloat16).reshape(table_n, pool_len, wid...  185 us
  transfers between devices with their start and end apart: 4, of which 4 were waited for; matrix products, arithmetic and copies ran while one was open for 3% of the time, Pallas kernels for 0%

commit v1 on v0

v1 whole, which is shorter than its diff:
```python
import functools
import jax
import jax.numpy as jnp
from jax import lax
from jax.experimental import pallas as pl
from jax.experimental.pallas import tpu as pltpu
from jax.sharding import PartitionSpec as P

F32 = jnp.float32
BF16 = jnp.bfloat16
SIDE = 4
OWN_STEP = 4
VMEM_LIMIT = 60 * 1024 * 1024
B_CALLS = 4
OUT_CALLS = 8
ROW_CUTS = (0, 48, 88, 128)
AXIS_ORDERS = ((2, 1, 0), (1, 0, 2), (0, 2, 1))


def split3(val):
    one = val.astype(BF16)
    rest = val - one.astype(F32)
    two = rest.astype(BF16)
    rest = rest - two.astype(F32)
    return one, two, rest.astype(BF16)


def dot_nn(lhs, rhs):
    return lax.dot_general(lhs, rhs, (((1,), (0,)), ((), ())), preferred_element_type=F32)


def dot_nt(lhs, rhs):
    return lax.dot_general(lhs, rhs, (((1,), (1,)), ((), ())), preferred_element_type=F32)


def swap_fields(val):
    return val ^ ((val & 21) << 1)


def gate_kernel(n_own, pick_ref, gate_ref, out_ref, tile_ref):
    sel = pick_ref.shape[1]
    iota_own = lax.broadcasted_iota(jnp.int32, (n_own, sel), 0)
    iota_lo = lax.broadcasted_iota(jnp.int32, (128, sel), 0)

    def body(grp, carry):
        base = pl.multiple_of(grp * 8, 8)
        pick = pick_ref[pl.ds(base, 8), :]
        hi = pick >> 7
        lo = pick & 127
        parts = [piece.astype(F32) for piece in split3(gate_ref[pl.ds(base, 8), :])]
        for j in range(8):
            mask = iota_own == hi[j:j + 1, :]
            left = jnp.concatenate([jnp.where(mask, piece[j:j + 1, :], 0.0).astype(BF16) for piece in parts], axis=0)
            right = jnp.where(iota_lo == lo[j:j + 1, :], 1.0, 0.0).astype(BF16)
            res = dot_nt(left, right)
            tile_ref[j * n_own:(j + 1) * n_own, :] = res[:n_own] + res[n_own:2 * n_own] + res[2 * n_own:]
        for o in range(n_own):
            out_ref[pl.ds(base, 8), o * 128:(o + 1) * 128] = tile_ref[pl.ds(o, 8, stride=n_own), :]
        return carry

    lax.fori_loop(0, pick_ref.shape[0] // 8, body, 0)


def gate_matrix(pick_rel, gate, n_own):
    tok, sel = pick_rel.shape
    blk = max(8, tok // 4)
    return pl.pallas_call(
        functools.partial(gate_kernel, n_own),
        grid=(tok // blk,),
        in_specs=[pl.BlockSpec((blk, sel), lambda i: (i, 0)), pl.BlockSpec((blk, sel), lambda i: (i, 0))],
        out_specs=pl.BlockSpec((blk, n_own * 128), lambda i: (i, 0)),
        out_shape=jax.ShapeDtypeStruct((tok, n_own * 128), F32),
        scratch_shapes=[pltpu.VMEM((8 * n_own, 128), F32)],
        compiler_params=pltpu.CompilerParams(vmem_limit_bytes=VMEM_LIMIT),
        cost_estimate=pl.CostEstimate(flops=2 * tok * 256 * 256 * 192, bytes_accessed=tok * n_own * 512, transcendentals=0),
        name="gate_matrix",
    )(pick_rel, gate)


def select_rows(xoff_ref, tab_ref, idsb_ref, sel_ref):
    n_rows = tab_ref.shape[0] // OWN_STEP
    iota = lax.broadcasted_iota(jnp.int32, (128, 128), 1)
    for j in range(OWN_STEP):
        ids = idsb_ref[j * 128:(j + 1) * 128, :]
        hot = jnp.concatenate([jnp.where(ids == iota + 128 * h, 1.0, 0.0).astype(BF16) for h in range(n_rows // 128)], axis=1)
        start = pl.multiple_of(xoff_ref[j] * n_rows, n_rows)
        sel_ref[j * 128:(j + 1) * 128, :] = dot_nn(hot, tab_ref[pl.ds(start, n_rows), :]).astype(BF16)


def place_rows(blk, grad_t, ids_ref, keep_ref, send_ref):
    iota = lax.broadcasted_iota(jnp.int32, (256, 128), 0)
    grad_b = grad_t.astype(BF16)
    for j in range(OWN_STEP):
        hot = jnp.where(iota == ids_ref[pl.ds(blk * OWN_STEP + j, 1), :], 1.0, 0.0).astype(BF16)
        rows = dot_nt(hot, grad_b[:, j * 128:(j + 1) * 128]).astype(BF16)
        keep_ref[j * 128:(j + 1) * 128, :] = rows[:128]
        k = swap_fields(j)
        send_ref[k * 128:(k + 1) * 128, :] = rows[128:]


def first_kernel(ublk_ref, xoff_ref, tok_ref, dyt_ref, tab_ref, idsb_ref, ids_ref, gate_ref, w_ref, slope_ref, sel_ref, keep_ref, send_ref):
    select_rows(xoff_ref, tab_ref, idsb_ref, sel_ref)
    pre = dot_nt(tok_ref[...], sel_ref[...])
    gate = gate_ref[...]
    cdf = 0.5 * (1.0 + lax.erf(pre * 0.7071067811865476))
    pdf = jnp.exp(-0.5 * pre * pre) * 0.3989422804014327
    live = gate != 0.0
    w = jnp.where(live, gate * (pre * cdf), 0.0)
    w_ref[...] = w
    slope_ref[...] = jnp.where(live, gate * (cdf + pre * pdf), 0.0)
    one, two, three = split3(w)
    dyt = dyt_ref[...]
    grad_t = dot_nn(dyt, one) + dot_nn(dyt, two) + dot_nn(dyt, three)
    place_rows(pl.program_id(0), grad_t, ids_ref, keep_ref, send_ref)


def first_pass(ublk, xoff, tok, dyt, table, idsb, ids_flip, gate):
    n_tok, width = tok.shape
    n_list = gate.shape[1]
    cols = OWN_STEP * 128
    steps = n_list // cols
    trows = table.shape[0] // steps
    row_blk = pl.BlockSpec((cols, width), lambda i, u, x: (i, 0))
    mat_blk = pl.BlockSpec((n_tok, cols), lambda i, u, x: (0, i))
    return pl.pallas_call(
        first_kernel,
        grid_spec=pltpu.PrefetchScalarGridSpec(
            num_scalar_prefetch=2,
            grid=(steps,),
            in_specs=[
                pl.BlockSpec((n_tok, width), lambda i, u, x: (0, 0)),
                pl.BlockSpec((width, n_tok), lambda i, u, x: (0, 0)),
                pl.BlockSpec((trows, width), lambda i, u, x: (u[i], 0)),
                pl.BlockSpec((cols, 128), lambda i, u, x: (i, 0)),
                pl.BlockSpec(ids_flip.shape, lambda i, u, x: (0, 0)),
                mat_blk,
            ],
            out_specs=[mat_blk, mat_blk, row_blk, row_blk, pl.BlockSpec((cols, width), lambda i, u, x: (swap_fields(i), 0))],
        ),
        out_shape=[
            jax.ShapeDtypeStruct((n_tok, n_list), F32),
            jax.ShapeDtypeStruct((n_tok, n_list), F32),
            jax.ShapeDtypeStruct((n_list, width), BF16),
            jax.ShapeDtypeStruct((n_list, width), BF16),
            jax.ShapeDtypeStruct((n_list, width), BF16),
        ],
        compiler_params=pltpu.CompilerParams(vmem_limit_bytes=VMEM_LIMIT),
        cost_estimate=pl.CostEstimate(flops=11 * n_tok * n_list * width, bytes_accessed=n_list * (width * 10 + n_tok * 12), transcendentals=0),
        name="first_pass",
    )(ublk, xoff, tok, dyt, table, idsb, ids_flip, gate)


def second_kernel(first_blk, n_alias, ublk_ref, xoff_ref, dy_ref, tokt_ref, tab_ref, idsb_ref, ids_ref, slope_ref, *rest):
    c_ref, sel_ref, keep_ref, send_ref = rest[n_alias:]
    select_rows(xoff_ref, tab_ref, idsb_ref, sel_ref)
    back = dot_nt(dy_ref[...], sel_ref[...])
    slope = slope_ref[...]
    c = jnp.where(slope != 0.0, slope * back, 0.0)
    c_ref[...] = c
    one, two, three = split3(c)
    tokt = tokt_ref[...]
    grad_t = dot_nn(tokt, one) + dot_nn(tokt, two) + dot_nn(tokt, three)
    place_rows(pl.program_id(0) + first_blk, grad_t, ids_ref, keep_ref, send_ref)


def second_pass(ublk, xoff, dy, tokt, table, idsb, ids_flip, slope):
    n_tok, width = dy.shape
    n_list = slope.shape[1]
    cols = OWN_STEP * 128
    steps = n_list // cols
    per = steps // B_CALLS
    trows = table.shape[0] // steps
    outs = []
    for call in range(B_CALLS):
        at = call * per
        row_blk = pl.BlockSpec((cols, width), lambda i, u, x, at=at: (i + at, 0))
        mat_blk = pl.BlockSpec((n_tok, cols), lambda i, u, x, at=at: (0, i + at))
        outs = pl.pallas_call(
            functools.partial(second_kernel, at, len(outs)),
            grid_spec=pltpu.PrefetchScalarGridSpec(
                num_scalar_prefetch=2,
                grid=(per,),
                in_specs=[
                    pl.BlockSpec((n_tok, width), lambda i, u, x: (0, 0)),
                    pl.BlockSpec((width, n_tok), lambda i, u, x: (0, 0)),
                    pl.BlockSpec((trows, width), lambda i, u, x, at=at: (u[i + at], 0)),
                    pl.BlockSpec((cols, 128), lambda i, u, x, at=at: (i + at, 0)),
                    pl.BlockSpec(ids_flip.shape, lambda i, u, x: (0, 0)),
                    mat_blk,
                ] + [pl.BlockSpec(memory_space=pl.ANY)] * len(outs),
                out_specs=[mat_blk, row_blk, row_blk, pl.BlockSpec((cols, width), lambda i, u, x, at=at: (swap_fields(i + at), 0))],
            ),
            out_shape=[
                jax.ShapeDtypeStruct((n_tok, n_list), F32),
                jax.ShapeDtypeStruct((n_list, width), BF16),
                jax.ShapeDtypeStruct((n_list, width), BF16),
                jax.ShapeDtypeStruct((n_list, width), BF16),
            ],
            input_output_aliases={8 + k: k for k in range(len(outs))},
            compiler_params=pltpu.CompilerParams(vmem_limit_bytes=VMEM_LIMIT),
            cost_estimate=pl.CostEstimate(flops=11 * n_tok * n_list * width // B_CALLS, bytes_accessed=n_list * (width * 10 + n_tok * 8) // B_CALLS, transcendentals=0),
            name="second_pass",
        )(ublk, xoff, dy, tokt, table, idsb, ids_flip, slope, *outs)
    return outs


def out_kernel(has_in, w_ref, c_ref, v_ref, u_ref, *rest):
    y_in, dx_in = rest[:2] if has_in else (None, None)
    y_ref, dx_ref, y_acc, dx_acc = rest[-4:]
    step = pl.program_id(0)

    @pl.when(step == 0)
    def _():
        y_acc[...] = y_in[...] if has_in else jnp.zeros_like(y_acc)
        dx_acc[...] = dx_in[...] if has_in else jnp.zeros_like(dx_acc)

    for mat_ref, row_ref, acc in ((w_ref, v_ref, y_acc), (c_ref, u_ref, dx_acc)):
        one, two, three = split3(mat_ref[...])
        rows = row_ref[...]
        acc[...] += dot_nn(one, rows) + dot_nn(two, rows) + dot_nn(three, rows)

    @pl.when(step == pl.num_programs(0) - 1)
    def _():
        y_ref[...] = y_acc[...].astype(y_ref.dtype)
        dx_ref[...] = dx_acc[...].astype(dx_ref.dtype)


def out_pass(w, c, v_sel, u_sel):
    n_tok, n_list = w.shape
    width = v_sel.shape[1]
    cols = OWN_STEP * 128
    per = n_list // cols // OUT_CALLS
    accs = []
    whole = pl.BlockSpec((n_tok, width), lambda i: (0, 0))
    for call in range(OUT_CALLS):
        at = call * per
        dtype = BF16 if call == OUT_CALLS - 1 else F32
        accs = pl.pallas_call(
            functools.partial(out_kernel, bool(accs)),
            grid=(per,),
            in_specs=[
                pl.BlockSpec((n_tok, cols), lambda i, at=at: (0, i + at)),
                pl.BlockSpec((n_tok, cols), lambda i, at=at: (0, i + at)),
                pl.BlockSpec((cols, width), lambda i, at=at: (i + at, 0)),
                pl.BlockSpec((cols, width), lambda i, at=at: (i + at, 0)),
            ] + [whole] * len(accs),
            out_specs=[whole, whole],
            out_shape=[jax.ShapeDtypeStruct((n_tok, width), dtype)] * 2,
            scratch_shapes=[pltpu.VMEM((n_tok, width), F32)] * 2,
            compiler_params=pltpu.CompilerParams(vmem_limit_bytes=VMEM_LIMIT),
            cost_estimate=pl.CostEstimate(flops=12 * n_tok * n_list * width // OUT_CALLS, bytes_accessed=n_list * (width * 4 + n_tok * 8) // OUT_CALLS, transcendentals=0),
            name="out_pass",
        )(w, c, v_sel, u_sel, *accs)
    return accs


def neighbour_pairs(field, step, table_n):
    pairs = []
    for core in range(2):
        flip = (1 if (core == 0) == (step == 0) else 3) << (2 * field)
        pairs += [(core * table_n + r, core * table_n + (r ^ flip)) for r in range(table_n)]
    return pairs


def halve_rows(keep, send, table_n):
    width = keep.shape[-1]
    axes = ('data', 'table')
    swap = [(i, (i + table_n) % (2 * table_n)) for i in range(2 * table_n)]
    got0 = lax.ppermute(send, axes, swap)
    cube = (SIDE, SIDE, SIDE, 128, width)
    keep, got0 = keep.reshape(cube), got0.reshape(cube)
    done = []
    for strm in range(3):
        cut = slice(ROW_CUTS[strm], ROW_CUTS[strm + 1])
        val = keep[:, :, :, cut].astype(F32) + got0[:, :, :, cut].astype(F32)
        left = [0, 1, 2]
        for axis in AXIS_ORDERS[strm]:
            dim = left.index(axis)
            left.remove(axis)
            field = 2 - axis
            take = lambda arr, lo, hi: lax.slice_in_dim(arr, lo, hi, axis=dim)
            got = lax.ppermute(take(val, 1, 3).astype(BF16), axes, neighbour_pairs(field, 0, table_n))
            far = take(val, 3, 4) + take(got, 1, 2).astype(F32)
            got2 = lax.ppermute(far.astype(BF16), axes, neighbour_pairs(field, 1, table_n))
            val = take(val, 0, 1) + take(got, 0, 1).astype(F32) + got2.astype(F32)
            val = val.reshape(val.shape[:dim] + val.shape[dim + 1:])
        done.append(val)
    mine = jnp.concatenate(done, axis=0).astype(BF16)
    return lax.all_gather(mine, 'data', axis=0, tiled=True)


def solution(mesh):
    table_n = mesh.shape['table']
    tok_spec = P(('replica', 'data', 'table'))
    row_spec = P(('replica', 'table'))

    def device_step(tok, dy, u_loc, v_loc, wanted, pick, gate):
        n_local, width = u_loc.shape
        half = n_local // 2
        n_tok = tok.shape[0]
        core = lax.axis_index('data')
        me = lax.axis_index('table')
        own_rows = lambda arr: lax.dynamic_slice_in_dim(arr, core * half, half, 0)
        full_u = lax.all_gather(own_rows(u_loc), ('table', 'data'), axis=0, tiled=True)
        full_v = lax.all_gather(own_rows(v_loc), ('table', 'data'), axis=0, tiled=True)

        slots = jnp.arange(table_n, dtype=jnp.int32)
        relabel = lambda val: jnp.where(core == 1, swap_fields(val), val)
        owners = relabel(slots) ^ me
        ublk = relabel(jnp.arange(table_n // OWN_STEP, dtype=jnp.int32)) ^ (me >> 2)
        xoff = relabel(jnp.arange(OWN_STEP, dtype=jnp.int32)) ^ (me & 3)
        ids = jnp.take(wanted.reshape(table_n, -1), owners, axis=0, mode='clip') - owners[:, None] * n_local
        ids_flip = ids ^ (core * half)
        idsb = jnp.broadcast_to(ids.reshape(-1, 1), (ids.size, 128))
        pick = pick.reshape(n_tok, -1)
        pick_rel = (relabel((pick >> 7) ^ me) << 7) | (pick & 127)
        gates = gate_matrix(pick_rel, gate.reshape(n_tok, -1), table_n)

        w, slope, u_sel, keep_v, send_v = first_pass(ublk, xoff, tok, dy.T, full_u, idsb, ids_flip, gates)
        grad_v = halve_rows(keep_v, send_v, table_n)
        c, v_sel, keep_u, send_u = second_pass(ublk, xoff, dy, tok.T, full_v, idsb, ids_flip, slope)
        grad_u = halve_rows(keep_u, send_u, table_n)
        y, dx = out_pass(w, c, v_sel, u_sel)
        return y, dx, grad_u, grad_v

    return jax.shard_map(device_step, mesh=mesh, in_specs=(tok_spec, tok_spec, row_spec, row_spec, tok_spec, tok_spec, tok_spec), out_specs=(tok_spec, tok_spec, row_spec, row_spec), check_vma=False)
```

time: 3980 us -> 646 us (0.16)
  other arithmetic: 1850 us -> 90.9 us
  local copies, waits for them, and re-layouts: 880 us -> 46.5 us
  waiting for transfers between devices: 914 us -> 164 us
  Pallas kernels: 0 us -> 275 us
  matrix products: 214 us -> 0 us
    scatter-add x18 -> x0, other arithmetic: 1620 us -> none  [the longest x8 740 us: body(): acc_u.at[flat_pick]]
    all_to_all x4 -> x0, waiting for transfers between devices: 914 us -> none  [the longest x1 260 us: device_step(): lax.all_to_all(sent_v, 'table', 0, 0, tiled=True)]
    gather x18 -> x1, local copies, waits for them, and re-layouts: 849 us -> 0.6 us  [device_step(): jnp.take(wanted.reshape(table_n, -1), owners, axis=0, mode='clip')]
    pallas_call x0 -> x14, Pallas kernels: none -> 275 us  [the longest x8 104 us: out_pass(): pl.pallas_call(functools.partial(out_kernel, bool(accs)), grid=(per,), in...]
    dot_general x32 -> x0, matrix products: 214 us -> none  [the longest x8 65.7 us: body(): jnp.einsum('bs,bsd->bd', weight, sel_v, preferred_element_type=jnp.float32)]
    mul x25 -> x1, other arithmetic: 179 us -> 0.01 us  [device_step(): owners[:, None] * n_local]
    all_gather x0 -> x2, waiting for transfers between devices: none -> 110 us  [the longest x1 72.9 us: device_step(): lax.all_gather(own_rows(u_loc), ('table', 'data'), axis=0, tiled=True)]
    all_to_all x4 -> x0, starting transfers between devices: 59.2 us -> none  [the longest x1 29 us: device_step(): lax.all_to_all(sent_v, 'table', 0, 0, tiled=True)]
  transfers between devices with their start and end apart: 4 -> 40, of which waited for: 4 -> 16; matrix products, arithmetic and copies ran while one was open for 3% -> 20% of each run, Pallas kernels for 0% -> 43%
where the time goes in v1:
time: 646 us; the launch traced here: 641 us
  Pallas kernels  275 us (43%)
  waiting for transfers between devices  164 us (25%)
  other arithmetic  90.9 us (14%)
  local copies, waits for them, and re-layouts  46.5 us (7%)
  starting transfers between devices  36.1 us (6%)
  between operations  15.3 us (2%)
  blocking collectives  12.9 us (2%)
    pallas_call x8, Pallas kernels, out_pass(): pl.pallas_call(functools.partial(out_kernel, bool(accs)), grid=(per,), in...  104 us
    pallas_call x4, Pallas kernels, second_pass(): pl.pallas_call(functools.partial(second_kernel, at, len(outs)), grid_spec...  74.6 us
    all_gather x1, waiting for transfers between devices, device_step(): lax.all_gather(own_rows(u_loc), ('table', 'data'), axis=0, tiled=True)  72.9 us
    pallas_call x1, Pallas kernels, first_pass(): pl.pallas_call(first_kernel, grid_spec=pltpu.PrefetchScalarGridSpec(num_s...  67.3 us
    add x4, other arithmetic, halve_rows(): val = keep[:, :, :, cut].astype(F32) + got0[:, :, :, cut].astype(F32)  48.3 us
    all_gather x1, waiting for transfers between devices, device_step(): lax.all_gather(own_rows(v_loc), ('table', 'data'), axis=0, tiled=True)  37.4 us
    ppermute x18, waiting for transfers between devices, halve_rows(): lax.ppermute(take(val, 1, 3).astype(BF16), axes, neighbour_pairs(field, 0...  31.5 us
    pallas_call x1, Pallas kernels, gate_matrix(): pl.pallas_call(functools.partial(gate_kernel, n_own), grid=(tok // blk,),...  29.3 us
  transfers between devices with their start and end apart: 40, of which 16 were waited for; matrix products, arithmetic and copies ran while one was open for 20% of the time, Pallas kernels for 43%

profile of v1, /device:TPU:1, one launch (start us, length us, event | category | flops | bytes accessed | tf_op | source)
XLA Modules:
  0.0 640.8 jit_solution(17075575841414870044)
XLA Ops:
  19.7 29.3 %gate_matrix.1.gate_ref = f32[512,8192]{1,0:T(8,128)} custom-call(s32[512,128]{1,0:T(8,128)} %fusion.35.pick_ref, f32[512,128]{1,0:T(8,128)} %copy.37.gate_ref), custom_call_target="tpu_custom_call" | custom-call | flops 12884901888 | bytes 16777216 | tf_op jit(solution)/shard_map/gate_matrix/pallas_call | solution.py:67
  49.0 72.9 %all-gather.3.cloned.1.call-done.tab_ref = bf16[16384,1024]{1,0:T(8,128)(2,1)} async-done(((bf16[128,1024]{1,0:T(8,128)(2,1)}), bf16[16384,1024]{1,0:T(8,128)(2,1)}) %all-gather.3.cloned.1.call-update) | async-done | bytes 33554448 | tf_op jit(solution)/shard_map/all_gather | solution.py:304
  122.0 4.9 broadcast_in_dim.4.idsb_ref
  126.9 67.3 %first_pass.1 = (f32[512,8192]{1,0:T(8,128)}, f32[512,8192]{1,0:T(8,128)}, bf16[8192,1024]{1,0:T(8,128)(2,1)}, bf16[8192,1024]{1,0:T(8,128)(2,1)}, bf16[8192,1024]{1,0:T(8,128)(2,1)}) custom-call(s32[16]{0:T(128)} %fusion.83.ublk_ref, s32[4]{0:T(128)} %fusion.82.xoff_ref, bf16[512,1024]{1,0:T(8,128)(2,1)} %tok_ref.1, bf16[1024,512]{1,0:T(8,128)(2,1)} %bitcast.191, ...), custom_call_target="tpu_custom_call" | custom-call | flops 47244640256 | bytes 134217728 | tf_op jit(solution)/shard_map/first_pass/pallas_call | solution.py:125
  194.7 37.4 %all-gather.5.cloned.1.call-done.tab_ref = bf16[16384,1024]{1,0:T(8,128)(2,1)} async-done(((bf16[128,1024]{1,0:T(8,128)(2,1)}), bf16[16384,1024]{1,0:T(8,128)(2,1)}) %all-gather.5.cloned.1.call-update) | async-done | bytes 33554448 | tf_op jit(solution)/shard_map/all_gather | solution.py:305
  232.1 18.6 %second_pass.4 = (f32[512,8192]{1,0:T(8,128)}, bf16[8192,1024]{1,0:T(8,128)(2,1)}, bf16[8192,1024]{1,0:T(8,128)(2,1)}, bf16[8192,1024]{1,0:T(8,128)(2,1)}) custom-call(s32[16]{0:T(128)} %fusion.83.ublk_ref, s32[4]{0:T(128)} %fusion.82.xoff_ref, bf16[512,1024]{1,0:T(8,128)(2,1)} %dy_ref.7, bf16[1024,512]{1,0:T(8,128)(2,1)} %bitcast.180, ...), custom_call_target="tpu_custom_call" | custom-call | flops 11811160064 | bytes 29360128 | tf_op jit(solution)/shard_map/second_pass/pallas_call | solution.py:178
  250.8 18.7 %second_pass.5 = (f32[512,8192]{1,0:T(8,128)}, bf16[8192,1024]{1,0:T(8,128)(2,1)}, bf16[8192,1024]{1,0:T(8,128)(2,1)}, bf16[8192,1024]{1,0:T(8,128)(2,1)}) custom-call(s32[16]{0:T(128)} %fusion.83.ublk_ref, s32[4]{0:T(128)} %fusion.82.xoff_ref, bf16[512,1024]{1,0:T(8,128)(2,1)} %dy_ref.7, ...), custom_call_target="tpu_custom_call", output_to_operand_aliasing={{0}: (8, {}), {1}: (9, {}), {2}: (10, {}), {3}: (11, {})} | custom-call | flops 11811160064 | bytes 29360128 | tf_op jit(solution)/shard_map/second_pass/pallas_call | solution.py:178
  269.4 18.6 %second_pass.6 = (f32[512,8192]{1,0:T(8,128)}, bf16[8192,1024]{1,0:T(8,128)(2,1)}, bf16[8192,1024]{1,0:T(8,128)(2,1)}, bf16[8192,1024]{1,0:T(8,128)(2,1)}) custom-call(s32[16]{0:T(128)} %fusion.83.ublk_ref, s32[4]{0:T(128)} %fusion.82.xoff_ref, bf16[512,1024]{1,0:T(8,128)(2,1)} %dy_ref.7, ...), custom_call_target="tpu_custom_call", output_to_operand_aliasing={{0}: (8, {}), {1}: (9, {}), {2}: (10, {}), {3}: (11, {})} | custom-call | flops 11811160064 | bytes 29360128 | tf_op jit(solution)/shard_map/second_pass/pallas_call | solution.py:178
  288.1 18.7 %second_pass.7 = (f32[512,8192]{1,0:T(8,128)}, bf16[8192,1024]{1,0:T(8,128)(2,1)}, bf16[8192,1024]{1,0:T(8,128)(2,1)}, bf16[8192,1024]{1,0:T(8,128)(2,1)}) custom-call(s32[16]{0:T(128)} %fusion.83.ublk_ref, s32[4]{0:T(128)} %fusion.82.xoff_ref, bf16[512,1024]{1,0:T(8,128)(2,1)} %dy_ref.7, ...), custom_call_target="tpu_custom_call", output_to_operand_aliasing={{0}: (8, {}), {1}: (9, {}), {2}: (10, {}), {3}: (11, {})} | custom-call | flops 11811160064 | bytes 29360128 | tf_op jit(solution)/shard_map/second_pass/pallas_call | solution.py:178
  307.2 11.7 %out_pass.8 = (f32[512,1024]{1,0:T(8,128)}, f32[512,1024]{1,0:T(8,128)}) custom-call(f32[512,8192]{1,0:T(8,128)} %get-tuple-element.41.w_ref, f32[512,8192]{1,0:T(8,128)} %get-tuple-element.55.c_ref, bf16[8192,1024]{1,0:T(8,128)(2,1)} %get-tuple-element.56.v_ref, bf16[8192,1024]{1,0:T(8,128)(2,1)} %get-tuple-element.57.u_ref), custom_call_target="tpu_custom_call" | custom-call | flops 6442450944 | bytes 8388608 | tf_op jit(solution)/shard_map/out_pass/pallas_call | solution.py:238
  318.9 13.3 %out_pass.9 = (f32[512,1024]{1,0:T(8,128)}, f32[512,1024]{1,0:T(8,128)}) custom-call(f32[512,8192]{1,0:T(8,128)} %get-tuple-element.41.w_ref, f32[512,8192]{1,0:T(8,128)} %get-tuple-element.55.c_ref, bf16[8192,1024]{1,0:T(8,128)(2,1)} %get-tuple-element.56.v_ref, bf16[8192,1024]{1,0:T(8,128)(2,1)} %get-tuple-element.57.u_ref, ...), custom_call_target="tpu_custom_call" | custom-call | flops 6442450944 | bytes 8388608 | tf_op jit(solution)/shard_map/out_pass/pallas_call | solution.py:238
  332.2 13.3 %out_pass.10 = (f32[512,1024]{1,0:T(8,128)}, f32[512,1024]{1,0:T(8,128)}) custom-call(f32[512,8192]{1,0:T(8,128)} %get-tuple-element.41.w_ref, f32[512,8192]{1,0:T(8,128)} %get-tuple-element.55.c_ref, bf16[8192,1024]{1,0:T(8,128)(2,1)} %get-tuple-element.56.v_ref, bf16[8192,1024]{1,0:T(8,128)(2,1)} %get-tuple-element.57.u_ref, ...), custom_call_target="tpu_custom_call" | custom-call | flops 6442450944 | bytes 8388608 | tf_op jit(solution)/shard_map/out_pass/pallas_call | solution.py:238
  345.5 13.3 %out_pass.11 = (f32[512,1024]{1,0:T(8,128)}, f32[512,1024]{1,0:T(8,128)}) custom-call(f32[512,8192]{1,0:T(8,128)} %get-tuple-element.41.w_ref, f32[512,8192]{1,0:T(8,128)} %get-tuple-element.55.c_ref, bf16[8192,1024]{1,0:T(8,128)(2,1)} %get-tuple-element.56.v_ref, bf16[8192,1024]{1,0:T(8,128)(2,1)} %get-tuple-element.57.u_ref, ...), custom_call_target="tpu_custom_call" | custom-call | flops 6442450944 | bytes 8388608 | tf_op jit(solution)/shard_map/out_pass/pallas_call | solution.py:238
  358.7 13.7 %out_pass.12 = (f32[512,1024]{1,0:T(8,128)}, f32[512,1024]{1,0:T(8,128)}) custom-call(f32[512,8192]{1,0:T(8,128)} %get-tuple-element.41.w_ref, f32[512,8192]{1,0:T(8,128)} %get-tuple-element.55.c_ref, bf16[8192,1024]{1,0:T(8,128)(2,1)} %get-tuple-element.56.v_ref, bf16[8192,1024]{1,0:T(8,128)(2,1)} %get-tuple-element.57.u_ref, ...), custom_call_target="tpu_custom_call" | custom-call | flops 6442450944 | bytes 8388608 | tf_op jit(solution)/shard_map/out_pass/pallas_call | solution.py:238
  372.5 13.3 %convert_add_fusion.3 = (f32[4,4,4,40,1024]{4,3,2,1,0:T(8,128)S(1)}, f32[4,4,4,40,1024]{4,3,2,1,0:T(8,128)}) fusion(bf16[4,4,4,128,1024]{4,3,2,1,0:T(8,128)(2,1)} %bitcast.30, bf16[4,4,4,128,1024]{4,3,2,1,0:T(8,128)(2,1)} %bitcast.184), kind=kLoop, calls=%fused_computation.4 | loop fusion | flops 15728640 | bytes 41943040 | tf_op jit(solution)/shard_map/add | solution.py:275
  387.7 8.5 %slice.858 = bf16[2,4,4,40,1024]{4,3,2,1,0:T(8,128)(2,1)} slice(f32[4,4,4,40,1024]{4,3,2,1,0:T(8,128)} %get-tuple-element.79), slice={[1:3], [0:4], [0:4], [0:40], [0:1024]} | slice | bytes 5242880 | tf_op jit(solution)/shard_map/slice | solution.py:281
  399.6 10.2 %convert_add_fusion.5 = (f32[4,4,4,40,1024]{4,3,2,1,0:T(8,128)}, f32[4,4,4,40,1024]{4,3,2,1,0:T(8,128)S(1)}) fusion(bf16[4,4,4,128,1024]{4,3,2,1,0:T(8,128)(2,1)} %bitcast.9, bf16[4,4,4,128,1024]{4,3,2,1,0:T(8,128)(2,1)S(1)} %bitcast.177), kind=kLoop, calls=%fused_computation.6 | loop fusion | flops 15728640 | bytes 41943040 | tf_op jit(solution)/shard_map/add | solution.py:275
  409.8 3.9 copy-done.3
  417.6 12.4 %convert_add_fusion = f32[4,4,4,48,1024]{4,3,2,1,0:T(8,128)} fusion(bf16[4,4,4,128,1024]{4,3,2,1,0:T(8,128)(2,1)} %bitcast.30, bf16[4,4,4,128,1024]{4,3,2,1,0:T(8,128)(2,1)} %bitcast.185), kind=kLoop, calls=%fused_computation.1 | loop fusion | flops 9437184 | bytes 25165824 | tf_op jit(solution)/shard_map/add | solution.py:275
  430.0 12.5 %convert_add_fusion.1 = f32[4,4,4,48,1024]{4,3,2,1,0:T(8,128)} fusion(bf16[4,4,4,128,1024]{4,3,2,1,0:T(8,128)(2,1)} %bitcast.9, bf16[4,4,4,128,1024]{4,3,2,1,0:T(8,128)(2,1)} %bitcast.174), kind=kLoop, calls=%fused_computation.2 | loop fusion | flops 9437184 | bytes 25165824 | tf_op jit(solution)/shard_map/add | solution.py:275
  442.5 4.9 slice.856
  449.8 4.4 slice.861
  454.4 5.0 slice.857
  459.8 13.2 %out_pass.13 = (f32[512,1024]{1,0:T(8,128)}, f32[512,1024]{1,0:T(8,128)}) custom-call(f32[512,8192]{1,0:T(8,128)} %get-tuple-element.41.w_ref, f32[512,8192]{1,0:T(8,128)} %get-tuple-element.55.c_ref, bf16[8192,1024]{1,0:T(8,128)(2,1)} %get-tuple-element.56.v_ref, bf16[8192,1024]{1,0:T(8,128)(2,1)} %get-tuple-element.57.u_ref, ...), custom_call_target="tpu_custom_call" | custom-call | flops 6442450944 | bytes 8388608 | tf_op jit(solution)/shard_map/out_pass/pallas_call | solution.py:238
  473.0 13.3 %out_pass.14 = (f32[512,1024]{1,0:T(8,128)}, f32[512,1024]{1,0:T(8,128)}) custom-call(f32[512,8192]{1,0:T(8,128)} %get-tuple-element.41.w_ref, f32[512,8192]{1,0:T(8,128)} %get-tuple-element.55.c_ref, bf16[8192,1024]{1,0:T(8,128)(2,1)} %get-tuple-element.56.v_ref, bf16[8192,1024]{1,0:T(8,128)(2,1)} %get-tuple-element.57.u_ref, ...), custom_call_target="tpu_custom_call" | custom-call | flops 6442450944 | bytes 8388608 | tf_op jit(solution)/shard_map/out_pass/pallas_call | solution.py:238
  486.3 12.5 %out_pass.15 = (bf16[512,1024]{1,0:T(8,128)(2,1)}, bf16[512,1024]{1,0:T(8,128)(2,1)}) custom-call(f32[512,8192]{1,0:T(8,128)} %get-tuple-element.41.w_ref, f32[512,8192]{1,0:T(8,128)} %get-tuple-element.55.c_ref, bf16[8192,1024]{1,0:T(8,128)(2,1)} %get-tuple-element.56.v_ref, bf16[8192,1024]{1,0:T(8,128)(2,1)} %get-tuple-element.57.u_ref, ...), custom_call_target="tpu_custom_call" | custom-call | flops 6442450944 | bytes 8388608 | tf_op jit(solution)/shard_map/out_pass/pallas_call | solution.py:238
  498.8 2.7 fusion.6
  501.6 2.7 fusion.9
  504.5 2.6 fusion.11
  508.4 2.6 fusion.14
  515.3 3.4 collective-permute-done.1
  522.3 2.8 fusion.8
  525.2 2.5 collective-permute-start.34
  527.7 2.8 fusion.10
  533.5 2.8 fusion.13
  538.5 2.8 fusion.15
  546.1 11.2 %collective-permute-done.15 = bf16[4,2,40,1024]{3,2,1,0:T(8,128)(2,1)S(1)} collective-permute-done((bf16[4,2,40,1024]{3,2,1,0:T(8,128)(2,1)S(1)}, bf16[4,2,40,1024]{3,2,1,0:T(8,128)(2,1)S(1)}, u32[]{:S(2)}, u32[]{:S(2)}) %collective-permute-start.15) | collective-permute-done | bytes 655392 | tf_op jit(solution)/shard_map/ppermute | solution.py:282
  559.2 2.8 fusion.2
  562.1 7.2 %collective-permute-done.2 = bf16[4,4,1,48,1024]{4,3,2,1,0:T(8,128)(2,1)S(1)} collective-permute-done((bf16[4,4,1,48,1024]{4,3,2,1,0:T(8,128)(2,1)S(1)}, bf16[4,4,1,48,1024]{4,3,2,1,0:T(8,128)(2,1)S(1)}, u32[]{:S(2)}, u32[]{:S(2)}) %collective-permute-start.2) | collective-permute-done | bytes 1572896 | tf_op jit(solution)/shard_map/ppermute | solution.py:284
  577.9 2.5 collective-permute-start.30
  584.4 7.1 %collective-permute-done.36 = bf16[2,40,1024]{2,1,0:T(8,128)(2,1)S(1)} collective-permute-done((bf16[2,40,1024]{2,1,0:T(8,128)(2,1)S(1)}, bf16[2,40,1024]{2,1,0:T(8,128)(2,1)S(1)}, u32[]{:S(2)}, u32[]{:S(2)}) %collective-permute-start.36) | collective-permute-done | bytes 163872 | tf_op jit(solution)/shard_map/ppermute | solution.py:282
  594.1 3.1 collective-permute-done.11
  597.7 3.1 collective-permute-done.18
  602.7 4.9 collective-permute-done.23
  608.8 3.3 collective-permute-done.4
  614.0 4.1 collective-permute-done.5
  618.9 8.8 %all_gather.15 = bf16[256,1024]{1,0:T(8,128)(2,1)S(1)} all-gather(bf16[128,1024]{1,0:T(8,128)(2,1)S(1)} %pad_maximum_fusion.1), channel_id=1, replica_groups=mesh['replica'=1,'data'=2,'table'=64] {'data'}, dimensions={0}, use_global_device_ids=true | all-gather | bytes 786432 | tf_op jit(solution)/shard_map/all_gather | solution.py:289
  627.7 4.1 all_gather.14
  (163 shorter events, 69.6 us)
Async XLA Ops:
  7.2 114.8 %all-gather.3.cloned.1.call-start = ((), (), s32[]{:S(2)}) async-start(), calls=%async_computation | async-start | bytes 33816576 | tf_op jit(solution)/shard_map/all_gather | solution.py:304
  9.0 223.1 %all-gather.5.cloned.1.call-start = ((), (), s32[]{:S(2)}) async-start(), calls=%async_computation.1 | async-start | bytes 33816576 | tf_op jit(solution)/shard_map/all_gather | solution.py:305
  194.2 178.2 %collective-permute-start.19 = (bf16[8192,1024]{1,0:T(8,128)(2,1)}, bf16[8192,1024]{1,0:T(8,128)(2,1)}, u32[]{:S(2)}, u32[]{:S(2)}) collective-permute-start(bf16[8192,1024]{1,0:T(8,128)(2,1)} %get-tuple-element.77), channel_id=1, source_target_pairs={{0,64},{1,65},{2,66},{3,67},{4,68},{5,69},{6,70},{7,71},{8,72},{9,... | collective-permute-start | bytes 50331656 | tf_op jit(solution)/shard_map/ppermute | solution.py:269
  306.8 92.8 %collective-permute-start = (bf16[8192,1024]{1,0:T(8,128)(2,1)}, bf16[8192,1024]{1,0:T(8,128)(2,1)}, u32[]{:S(2)}, u32[]{:S(2)}) collective-permute-start(bf16[8192,1024]{1,0:T(8,128)(2,1)} %get-tuple-element.75), channel_id=1, source_target_pairs={{0,64},{1,65},{2,66},{3,67},{4,68},{5,69},{6,70},{7,71},{8,72},{9,... | collective-permute-start | bytes 50331656 | tf_op jit(solution)/shard_map/ppermute | solution.py:269
  372.4 27.1 %slice-start = ((s8[16777216]{0:T(1024)(128)(4,1)}), s8[4194304]{0:T(1024)(128)(4,1)S(1)}, s32[]{:S(2)}) async-start(s8[16777216]{0:T(1024)(128)(4,1)} %bitcast.175), calls=%async_computation.2 | async-start | bytes 8388608
  372.5 27.1 %slice-start.1 = ((s8[16777216]{0:T(1024)(128)(4,1)}), s8[4194304]{0:T(1024)(128)(4,1)S(1)}, s32[]{:S(2)}) async-start(s8[16777216]{0:T(1024)(128)(4,1)} %bitcast.175), calls=%async_computation.3 | async-start | bytes 8388608
  372.5 27.1 %slice-start.2 = ((s8[16777216]{0:T(1024)(128)(4,1)}), s8[4194304]{0:T(1024)(128)(4,1)S(1)}, s32[]{:S(2)}) async-start(s8[16777216]{0:T(1024)(128)(4,1)} %bitcast.175), calls=%async_computation.4 | async-start | bytes 8388608
  372.5 27.1 %slice-start.3 = ((s8[16777216]{0:T(1024)(128)(4,1)}), s8[4194304]{0:T(1024)(128)(4,1)S(1)}, s32[]{:S(2)}) async-start(s8[16777216]{0:T(1024)(128)(4,1)} %bitcast.175), calls=%async_computation.5 | async-start | bytes 8388608
  396.1 63.2 %collective-permute-start.32 = (bf16[2,4,4,40,1024]{4,3,2,1,0:T(8,128)(2,1)}, bf16[2,4,4,40,1024]{4,3,2,1,0:T(8,128)(2,1)}, u32[]{:S(2)}, u32[]{:S(2)}) collective-permute-start(bf16[2,4,4,40,1024]{4,3,2,1,0:T(8,128)(2,1)} %slice.858), channel_id=1, source_target_pairs={{0,16},{1,17},{2,18},{3,19},{4,20},{5,21},{6,22},{7,23},{8,24},{9,... | collective-permute-start | bytes 7864328 | tf_op jit(solution)/shard_map/ppermute | solution.py:282
  397.1 104.5 %collective-permute-start.26 = (bf16[4,2,4,40,1024]{4,3,2,1,0:T(8,128)(2,1)}, bf16[4,2,4,40,1024]{4,3,2,1,0:T(8,128)(2,1)}, u32[]{:S(2)}, u32[]{:S(2)}) collective-permute-start(bf16[4,2,4,40,1024]{4,3,2,1,0:T(8,128)(2,1)} %slice.859), channel_id=1, source_target_pairs={{0,4},{1,5},{2,6},{3,7},{4,0},{5,1},{6,2},{7,3},{8,12},{9,13},{10,... | collective-permute-start | bytes 7864328 | tf_op jit(solution)/shard_map/ppermute | solution.py:282
  415.7 88.7 %collective-permute-start.13 = (bf16[2,4,4,40,1024]{4,3,2,1,0:T(8,128)(2,1)}, bf16[2,4,4,40,1024]{4,3,2,1,0:T(8,128)(2,1)}, u32[]{:S(2)}, u32[]{:S(2)}) collective-permute-start(bf16[2,4,4,40,1024]{4,3,2,1,0:T(8,128)(2,1)} %slice.860), channel_id=1, source_target_pairs={{0,16},{1,17},{2,18},{3,19},{4,20},{5,21},{6,22},{7,23},{8,24},{9,... | collective-permute-start | bytes 7864328 | tf_op jit(solution)/shard_map/ppermute | solution.py:282
  447.4 63.6 %collective-permute-start.20 = (bf16[4,4,2,48,1024]{4,3,2,1,0:T(8,128)(2,1)}, bf16[4,4,2,48,1024]{4,3,2,1,0:T(8,128)(2,1)S(1)}, u32[]{:S(2)}, u32[]{:S(2)}) collective-permute-start(bf16[4,4,2,48,1024]{4,3,2,1,0:T(8,128)(2,1)} %slice.856), channel_id=1, source_target_pairs={{0,1},{1,0},{2,3},{3,2},{4,5},{5,4},{6,7},{7,6},{8,9},{9,8},{10,11... | collective-permute-start | bytes 9437192 | tf_op jit(solution)/shard_map/ppermute | solution.py:282
  454.1 52.9 %collective-permute-start.7 = (bf16[4,2,4,40,1024]{4,3,2,1,0:T(8,128)(2,1)}, bf16[4,2,4,40,1024]{4,3,2,1,0:T(8,128)(2,1)}, u32[]{:S(2)}, u32[]{:S(2)}) collective-permute-start(bf16[4,2,4,40,1024]{4,3,2,1,0:T(8,128)(2,1)} %slice.861), channel_id=1, source_target_pairs={{0,4},{1,5},{2,6},{3,7},{4,0},{5,1},{6,2},{7,3},{8,12},{9,13},{10,... | collective-permute-start | bytes 7864328 | tf_op jit(solution)/shard_map/ppermute | solution.py:282
  459.4 59.3 %collective-permute-start.1 = (bf16[4,4,2,48,1024]{4,3,2,1,0:T(8,128)(2,1)}, bf16[4,4,2,48,1024]{4,3,2,1,0:T(8,128)(2,1)}, u32[]{:S(2)}, u32[]{:S(2)}) collective-permute-start(bf16[4,4,2,48,1024]{4,3,2,1,0:T(8,128)(2,1)} %slice.857), channel_id=1, source_target_pairs={{0,1},{1,0},{2,3},{3,2},{4,5},{5,4},{6,7},{7,6},{8,9},{9,8},{10,11... | collective-permute-start | bytes 9437192 | tf_op jit(solution)/shard_map/ppermute | solution.py:282
  498.8 19.9 %slice-start.4 = ((s8[12582912]{0:T(1024)(128)(4,1)}), s8[4194304]{0:T(1024)(128)(4,1)S(1)}, s32[]{:S(2)}) async-start(s8[12582912]{0:T(1024)(128)(4,1)} %bitcast.178), calls=%async_computation.6 | async-start | bytes 8388608
  501.5 17.2 %slice-start.5 = ((s8[12582912]{0:T(1024)(128)(4,1)}), s8[4194304]{0:T(1024)(128)(4,1)S(1)}, s32[]{:S(2)}) async-start(s8[12582912]{0:T(1024)(128)(4,1)} %bitcast.178), calls=%async_computation.7 | async-start | bytes 8388608
  501.5 19.2 %collective-permute-start.33 = (bf16[1,4,4,40,1024]{4,3,2,1,0:T(8,128)(2,1)S(1)}, bf16[1,4,4,40,1024]{4,3,2,1,0:T(8,128)(2,1)S(1)}, u32[]{:S(2)}, u32[]{:S(2)}) collective-permute-start(bf16[1,4,4,40,1024]{4,3,2,1,0:T(8,128)(2,1)S(1)} %fusion.6), channel_id=1, source_target_pairs={{0,48},{1,49},{2,50},{3,51},{4,52},{5,53},{6,54},{7,55},{8,56},{9,... | collective-permute-start | bytes 3932168 | tf_op jit(solution)/shard_map/ppermute | solution.py:284
  504.4 20.9 %collective-permute-start.27 = (bf16[4,1,4,40,1024]{4,3,2,1,0:T(8,128)(2,1)S(1)}, bf16[4,1,4,40,1024]{4,3,2,1,0:T(8,128)(2,1)S(1)}, u32[]{:S(2)}, u32[]{:S(2)}) collective-permute-start(bf16[4,1,4,40,1024]{4,3,2,1,0:T(8,128)(2,1)S(1)} %fusion.9), channel_id=1, source_target_pairs={{0,12},{1,13},{2,14},{3,15},{4,8},{5,9},{6,10},{7,11},{8,4},{9,5},... | collective-permute-start | bytes 3932168 | tf_op jit(solution)/shard_map/ppermute | solution.py:284
  507.0 11.7 %slice-start.6 = ((s8[12582912]{0:T(1024)(128)(4,1)}), s8[4194304]{0:T(1024)(128)(4,1)S(1)}, s32[]{:S(2)}) async-start(s8[12582912]{0:T(1024)(128)(4,1)} %bitcast.178), calls=%async_computation.8 | async-start | bytes 8388608
  507.1 25.5 %collective-permute-start.14 = (bf16[1,4,4,40,1024]{4,3,2,1,0:T(8,128)(2,1)S(1)}, bf16[1,4,4,40,1024]{4,3,2,1,0:T(8,128)(2,1)S(1)}, u32[]{:S(2)}, u32[]{:S(2)}) collective-permute-start(bf16[1,4,4,40,1024]{4,3,2,1,0:T(8,128)(2,1)S(1)} %fusion.11), channel_id=1, source_target_pairs={{0,48},{1,49},{2,50},{3,51},{4,52},{5,53},{6,54},{7,55},{8,56},{9,... | collective-permute-start | bytes 3932168 | tf_op jit(solution)/shard_map/ppermute | solution.py:284
  511.0 25.4 %collective-permute-start.8 = (bf16[4,1,4,40,1024]{4,3,2,1,0:T(8,128)(2,1)S(1)}, bf16[4,1,4,40,1024]{4,3,2,1,0:T(8,128)(2,1)S(1)}, u32[]{:S(2)}, u32[]{:S(2)}) collective-permute-start(bf16[4,1,4,40,1024]{4,3,2,1,0:T(8,128)(2,1)S(1)} %fusion.14), channel_id=1, source_target_pairs={{0,12},{1,13},{2,14},{3,15},{4,8},{5,9},{6,10},{7,11},{8,4},{9,5},... | collective-permute-start | bytes 3932168 | tf_op jit(solution)/shard_map/ppermute | solution.py:284
  518.7 38.9 %collective-permute-start.21 = (bf16[4,4,1,48,1024]{4,3,2,1,0:T(8,128)(2,1)S(1)}, bf16[4,4,1,48,1024]{4,3,2,1,0:T(8,128)(2,1)S(1)}, u32[]{:S(2)}, u32[]{:S(2)}) collective-permute-start(bf16[4,4,1,48,1024]{4,3,2,1,0:T(8,128)(2,1)S(1)} %fusion), channel_id=1, source_target_pairs={{0,3},{1,2},{2,1},{3,0},{4,7},{5,6},{6,5},{7,4},{8,11},{9,10},{10,... | collective-permute-start | bytes 4718600 | tf_op jit(solution)/shard_map/ppermute | solution.py:284
  520.8 48.5 %collective-permute-start.2 = (bf16[4,4,1,48,1024]{4,3,2,1,0:T(8,128)(2,1)S(1)}, bf16[4,4,1,48,1024]{4,3,2,1,0:T(8,128)(2,1)S(1)}, u32[]{:S(2)}, u32[]{:S(2)}) collective-permute-start(bf16[4,4,1,48,1024]{4,3,2,1,0:T(8,128)(2,1)S(1)} %fusion.3), channel_id=1, source_target_pairs={{0,3},{1,2},{2,1},{3,0},{4,7},{5,6},{6,5},{7,4},{8,11},{9,10},{10,... | collective-permute-start | bytes 4718600 | tf_op jit(solution)/shard_map/ppermute | solution.py:284
  525.2 18.0 %collective-permute-start.34 = (bf16[4,2,40,1024]{3,2,1,0:T(8,128)(2,1)S(1)}, bf16[4,2,40,1024]{3,2,1,0:T(8,128)(2,1)}, u32[]{:S(2)}, u32[]{:S(2)}) collective-permute-start(bf16[4,2,40,1024]{3,2,1,0:T(8,128)(2,1)S(1)} %slice.864), channel_id=1, source_target_pairs={{0,1},{1,0},{2,3},{3,2},{4,5},{5,4},{6,7},{7,6},{8,9},{9,8},{10,11... | collective-permute-start | bytes 1966088 | tf_op jit(solution)/shard_map/ppermute | solution.py:282
  532.5 13.5 %collective-permute-start.28 = (bf16[2,4,40,1024]{3,2,1,0:T(8,128)(2,1)S(1)}, bf16[2,4,40,1024]{3,2,1,0:T(8,128)(2,1)S(1)}, u32[]{:S(2)}, u32[]{:S(2)}) collective-permute-start(bf16[2,4,40,1024]{3,2,1,0:T(8,128)(2,1)S(1)} %fusion.21), channel_id=1, source_target_pairs={{0,16},{1,17},{2,18},{3,19},{4,20},{5,21},{6,22},{7,23},{8,24},{9,... | collective-permute-start | bytes 1966088 | tf_op jit(solution)/shard_map/ppermute | solution.py:282
  536.4 20.9 %collective-permute-start.15 = (bf16[4,2,40,1024]{3,2,1,0:T(8,128)(2,1)S(1)}, bf16[4,2,40,1024]{3,2,1,0:T(8,128)(2,1)S(1)}, u32[]{:S(2)}, u32[]{:S(2)}) collective-permute-start(bf16[4,2,40,1024]{3,2,1,0:T(8,128)(2,1)S(1)} %slice.865), channel_id=1, source_target_pairs={{0,1},{1,0},{2,3},{3,2},{4,5},{5,4},{6,7},{7,6},{8,9},{9,8},{10,11... | collective-permute-start | bytes 1966088 | tf_op jit(solution)/shard_map/ppermute | solution.py:282
  543.3 14.1 %collective-permute-start.9 = (bf16[2,4,40,1024]{3,2,1,0:T(8,128)(2,1)S(1)}, bf16[2,4,40,1024]{3,2,1,0:T(8,128)(2,1)S(1)}, u32[]{:S(2)}, u32[]{:S(2)}) collective-permute-start(bf16[2,4,40,1024]{3,2,1,0:T(8,128)(2,1)S(1)} %fusion.20), channel_id=1, source_target_pairs={{0,16},{1,17},{2,18},{3,19},{4,20},{5,21},{6,22},{7,23},{8,24},{9,... | collective-permute-start | bytes 1966088 | tf_op jit(solution)/shard_map/ppermute | solution.py:282
  546.0 26.8 %collective-permute-start.35 = (bf16[4,1,40,1024]{3,2,1,0:T(8,128)(2,1)}, bf16[4,1,40,1024]{3,2,1,0:T(8,128)(2,1)}, u32[]{:S(2)}, u32[]{:S(2)}) collective-permute-start(bf16[4,1,40,1024]{3,2,1,0:T(8,128)(2,1)} %fusion.22), channel_id=1, source_target_pairs={{0,3},{1,2},{2,1},{3,0},{4,7},{5,6},{6,5},{7,4},{8,11},{9,10},{10,... | collective-permute-start | bytes 983048 | tf_op jit(solution)/shard_map/ppermute | solution.py:284
  557.3 18.4 %collective-permute-start.29 = (bf16[1,4,40,1024]{3,2,1,0:T(8,128)(2,1)S(1)}, bf16[1,4,40,1024]{3,2,1,0:T(8,128)(2,1)}, u32[]{:S(2)}, u32[]{:S(2)}) collective-permute-start(bf16[1,4,40,1024]{3,2,1,0:T(8,128)(2,1)S(1)} %fusion.25), channel_id=1, source_target_pairs={{0,48},{1,49},{2,50},{3,51},{4,52},{5,53},{6,54},{7,55},{8,56},{9,... | collective-permute-start | bytes 983048 | tf_op jit(solution)/shard_map/ppermute | solution.py:284
  557.4 20.5 %collective-permute-start.16 = (bf16[4,1,40,1024]{3,2,1,0:T(8,128)(2,1)S(1)}, bf16[4,1,40,1024]{3,2,1,0:T(8,128)(2,1)}, u32[]{:S(2)}, u32[]{:S(2)}) collective-permute-start(bf16[4,1,40,1024]{3,2,1,0:T(8,128)(2,1)S(1)} %fusion.28), channel_id=1, source_target_pairs={{0,3},{1,2},{2,1},{3,0},{4,7},{5,6},{6,5},{7,4},{8,11},{9,10},{10,... | collective-permute-start | bytes 983048 | tf_op jit(solution)/shard_map/ppermute | solution.py:284
  557.6 23.9 %collective-permute-start.10 = (bf16[1,4,40,1024]{3,2,1,0:T(8,128)(2,1)S(1)}, bf16[1,4,40,1024]{3,2,1,0:T(8,128)(2,1)}, u32[]{:S(2)}, u32[]{:S(2)}) collective-permute-start(bf16[1,4,40,1024]{3,2,1,0:T(8,128)(2,1)S(1)} %fusion.31), channel_id=1, source_target_pairs={{0,48},{1,49},{2,50},{3,51},{4,52},{5,53},{6,54},{7,55},{8,56},{9,... | collective-permute-start | bytes 983048 | tf_op jit(solution)/shard_map/ppermute | solution.py:284
  569.3 31.5 %collective-permute-start.22 = (bf16[4,2,48,1024]{3,2,1,0:T(8,128)(2,1)S(1)}, bf16[4,2,48,1024]{3,2,1,0:T(8,128)(2,1)S(1)}, u32[]{:S(2)}, u32[]{:S(2)}) collective-permute-start(bf16[4,2,48,1024]{3,2,1,0:T(8,128)(2,1)S(1)} %slice.862), channel_id=1, source_target_pairs={{0,4},{1,5},{2,6},{3,7},{4,0},{5,1},{6,2},{7,3},{8,12},{9,13},{10,... | collective-permute-start | bytes 2359304 | tf_op jit(solution)/shard_map/ppermute | solution.py:282
  572.8 28.2 %collective-permute-start.3 = (bf16[4,2,48,1024]{3,2,1,0:T(8,128)(2,1)S(1)}, bf16[4,2,48,1024]{3,2,1,0:T(8,128)(2,1)S(1)}, u32[]{:S(2)}, u32[]{:S(2)}) collective-permute-start(bf16[4,2,48,1024]{3,2,1,0:T(8,128)(2,1)S(1)} %slice.863), channel_id=1, source_target_pairs={{0,4},{1,5},{2,6},{3,7},{4,0},{5,1},{6,2},{7,3},{8,12},{9,13},{10,... | collective-permute-start | bytes 2359304 | tf_op jit(solution)/shard_map/ppermute | solution.py:282
  575.7 15.8 %collective-permute-start.36 = (bf16[2,40,1024]{2,1,0:T(8,128)(2,1)S(1)}, bf16[2,40,1024]{2,1,0:T(8,128)(2,1)S(1)}, u32[]{:S(2)}, u32[]{:S(2)}) collective-permute-start(bf16[2,40,1024]{2,1,0:T(8,128)(2,1)S(1)} %fusion.51), channel_id=1, source_target_pairs={{0,4},{1,5},{2,6},{3,7},{4,0},{5,1},{6,2},{7,3},{8,12},{9,13},{10,... | collective-permute-start | bytes 491528 | tf_op jit(solution)/shard_map/ppermute | solution.py:282
  577.9 15.9 %collective-permute-start.30 = (bf16[2,40,1024]{2,1,0:T(8,128)(2,1)S(1)}, bf16[2,40,1024]{2,1,0:T(8,128)(2,1)S(1)}, u32[]{:S(2)}, u32[]{:S(2)}) collective-permute-start(bf16[2,40,1024]{2,1,0:T(8,128)(2,1)S(1)} %fusion.50), channel_id=1, source_target_pairs={{0,1},{1,0},{2,3},{3,2},{4,5},{5,4},{6,7},{7,6},{8,9},{9,8},{10,11... | collective-permute-start | bytes 491528 | tf_op jit(solution)/shard_map/ppermute | solution.py:282
  581.6 12.4 %collective-permute-start.17 = (bf16[2,40,1024]{2,1,0:T(8,128)(2,1)S(1)}, bf16[2,40,1024]{2,1,0:T(8,128)(2,1)S(1)}, u32[]{:S(2)}, u32[]{:S(2)}) collective-permute-start(bf16[2,40,1024]{2,1,0:T(8,128)(2,1)S(1)} %fusion.49), channel_id=1, source_target_pairs={{0,4},{1,5},{2,6},{3,7},{4,0},{5,1},{6,2},{7,3},{8,12},{9,13},{10,... | collective-permute-start | bytes 491528 | tf_op jit(solution)/shard_map/ppermute | solution.py:282
  591.5 5.7 collective-permute-start.11
  593.9 3.7 collective-permute-start.37
  594.0 3.7 collective-permute-start.31
  597.2 3.6 collective-permute-start.18
  597.5 3.5 collective-permute-start.12
  600.9 6.7 %collective-permute-start.23 = (bf16[4,1,48,1024]{3,2,1,0:T(8,128)(2,1)S(1)}, bf16[4,1,48,1024]{3,2,1,0:T(8,128)(2,1)S(1)}, u32[]{:S(2)}, u32[]{:S(2)}) collective-permute-start(bf16[4,1,48,1024]{3,2,1,0:T(8,128)(2,1)S(1)} %fusion.16), channel_id=1, source_target_pairs={{0,12},{1,13},{2,14},{3,15},{4,8},{5,9},{6,10},{7,11},{8,4},{9,5},... | collective-permute-start | bytes 1179656 | tf_op jit(solution)/shard_map/ppermute | solution.py:284
  601.1 11.0 %collective-permute-start.4 = (bf16[4,1,48,1024]{3,2,1,0:T(8,128)(2,1)S(1)}, bf16[4,1,48,1024]{3,2,1,0:T(8,128)(2,1)S(1)}, u32[]{:S(2)}, u32[]{:S(2)}) collective-permute-start(bf16[4,1,48,1024]{3,2,1,0:T(8,128)(2,1)S(1)} %fusion.18), channel_id=1, source_target_pairs={{0,12},{1,13},{2,14},{3,15},{4,8},{5,9},{6,10},{7,11},{8,4},{9,5},... | collective-permute-start | bytes 1179656 | tf_op jit(solution)/shard_map/ppermute | solution.py:284
  607.8 6.1 collective-permute-start.24
  612.3 5.8 collective-permute-start.5
  613.9 19.6 %copy-start.1 = (bf16[256,1024]{1,0:T(8,128)(2,1)S(1)}, bf16[256,1024]{1,0:T(8,128)(2,1)}, u32[]{:S(2)}) copy-start(bf16[256,1024]{1,0:T(8,128)(2,1)} %param.9) | copy-start | bytes 1572868
  613.9 4.9 collective-permute-start.25
  618.1 9.5 %collective-permute-start.6 = (bf16[1,48,1024]{2,1,0:T(8,128)(2,1)S(1)}, bf16[1,48,1024]{2,1,0:T(8,128)(2,1)S(1)}, u32[]{:S(2)}, u32[]{:S(2)}) collective-permute-start(bf16[1,48,1024]{2,1,0:T(8,128)(2,1)S(1)} %fusion.44), channel_id=1, source_target_pairs={{0,48},{1,49},{2,50},{3,51},{4,52},{5,53},{6,54},{7,55},{8,56},{9,... | collective-permute-start | bytes 294920 | tf_op jit(solution)/shard_map/ppermute | solution.py:284
  (8 other events, 50.5 us)
Sparse Core Ops, SparseCore 0:
  11.6 110.3 all-gather.2
  125.0 107.1 all-gather.4

commit v2 on v1

--- a/solution.py
+++ b/solution.py
@@ -12,7 +12,6 @@
 OWN_STEP = 4
 VMEM_LIMIT = 60 * 1024 * 1024
 B_CALLS = 4
-OUT_CALLS = 8
 ROW_CUTS = (0, 48, 88, 128)
 AXIS_ORDERS = ((2, 1, 0), (1, 0, 2), (0, 2, 1))
 
@@ -151,7 +150,7 @@
 
 
 def second_kernel(first_blk, n_alias, ublk_ref, xoff_ref, dy_ref, tokt_ref, tab_ref, idsb_ref, ids_ref, slope_ref, *rest):
-    c_ref, sel_ref, keep_ref, send_ref = rest[n_alias:]
+    c_ref, sel_ref, keep_ref, send_ref, tok_ref = rest[n_alias:]
     select_rows(xoff_ref, tab_ref, idsb_ref, sel_ref)
     back = dot_nt(dy_ref[...], sel_ref[...])
     slope = slope_ref[...]
@@ -161,97 +160,89 @@
     tokt = tokt_ref[...]
     grad_t = dot_nn(tokt, one) + dot_nn(tokt, two) + dot_nn(tokt, three)
     place_rows(pl.program_id(0) + first_blk, grad_t, ids_ref, keep_ref, send_ref)
-
-
-def second_pass(ublk, xoff, dy, tokt, table, idsb, ids_flip, slope):
+    tok_ref[...] = jnp.zeros_like(tok_ref)
+
+
+def second_part(call, ublk, xoff, dy, tokt, table, idsb, ids_flip, slope, outs):
     n_tok, width = dy.shape
     n_list = slope.shape[1]
     cols = OWN_STEP * 128
     steps = n_list // cols
     per = steps // B_CALLS
     trows = table.shape[0] // steps
-    outs = []
-    for call in range(B_CALLS):
-        at = call * per
-        row_blk = pl.BlockSpec((cols, width), lambda i, u, x, at=at: (i + at, 0))
-        mat_blk = pl.BlockSpec((n_tok, cols), lambda i, u, x, at=at: (0, i + at))
-        outs = pl.pallas_call(
-            functools.partial(second_kernel, at, len(outs)),
-            grid_spec=pltpu.PrefetchScalarGridSpec(
-                num_scalar_prefetch=2,
-                grid=(per,),
-                in_specs=[
-                    pl.BlockSpec((n_tok, width), lambda i, u, x: (0, 0)),
-                    pl.BlockSpec((width, n_tok), lambda i, u, x: (0, 0)),
-                    pl.BlockSpec((trows, width), lambda i, u, x, at=at: (u[i + at], 0)),
-                    pl.BlockSpec((cols, 128), lambda i, u, x, at=at: (i + at, 0)),
-                    pl.BlockSpec(ids_flip.shape, lambda i, u, x: (0, 0)),
-                    mat_blk,
-                ] + [pl.BlockSpec(memory_space=pl.ANY)] * len(outs),
-                out_specs=[mat_blk, row_blk, row_blk, pl.BlockSpec((cols, width), lambda i, u, x, at=at: (swap_fields(i + at), 0))],
-            ),
-            out_shape=[
-                jax.ShapeDtypeStruct((n_tok, n_list), F32),
-                jax.ShapeDtypeStruct((n_list, width), BF16),
-                jax.ShapeDtypeStruct((n_list, width), BF16),
-                jax.ShapeDtypeStruct((n_list, width), BF16),
-            ],
-            input_output_aliases={8 + k: k for k in range(len(outs))},
-            compiler_params=pltpu.CompilerParams(vmem_limit_bytes=VMEM_LIMIT),
-            cost_estimate=pl.CostEstimate(flops=11 * n_tok * n_list * width // B_CALLS, bytes_accessed=n_list * (width * 10 + n_tok * 8) // B_CALLS, transcendentals=0),
-            name="second_pass",
-        )(ublk, xoff, dy, tokt, table, idsb, ids_flip, slope, *outs)
-    return outs
-
-
-def out_kernel(has_in, w_ref, c_ref, v_ref, u_ref, *rest):
-    y_in, dx_in = rest[:2] if has_in else (None, None)
-    y_ref, dx_ref, y_acc, dx_acc = rest[-4:]
+    at = call * per
+    row_blk = pl.BlockSpec((cols, width), lambda i, u, x: (i + at, 0))
+    mat_blk = pl.BlockSpec((n_tok, cols), lambda i, u, x: (0, i + at))
+    return pl.pallas_call(
+        functools.partial(second_kernel, at, len(outs)),
+        grid_spec=pltpu.PrefetchScalarGridSpec(
+            num_scalar_prefetch=2,
+            grid=(per,),
+            in_specs=[
+                pl.BlockSpec((n_tok, width), lambda i, u, x: (0, 0)),
+                pl.BlockSpec((width, n_tok), lambda i, u, x: (0, 0)),
+                pl.BlockSpec((trows, width), lambda i, u, x: (u[i + at], 0)),
+                pl.BlockSpec((cols, 128), lambda i, u, x: (i + at, 0)),
+                pl.BlockSpec(ids_flip.shape, lambda i, u, x: (0, 0)),
+                mat_blk,
+            ] + [pl.BlockSpec(memory_space=pl.ANY)] * len(outs),
+            out_specs=[mat_blk, row_blk, row_blk, pl.BlockSpec((cols, width), lambda i, u, x: (swap_fields(i + at), 0)), pl.BlockSpec((8, 128), lambda i, u, x: (0, 0))],
+        ),
+        out_shape=[
+            jax.ShapeDtypeStruct((n_tok, n_list), F32),
+            jax.ShapeDtypeStruct((n_list, width), BF16),
+            jax.ShapeDtypeStruct((n_list, width), BF16),
+            jax.ShapeDtypeStruct((n_list, width), BF16),
+            jax.ShapeDtypeStruct((8, 128), F32),
+        ],
+        input_output_aliases={8 + k: k for k in range(len(outs))},
+        compiler_params=pltpu.CompilerParams(vmem_limit_bytes=VMEM_LIMIT),
+        cost_estimate=pl.CostEstimate(flops=11 * n_tok * n_list * width // B_CALLS, bytes_accessed=n_list * (width * 10 + n_tok * 8) // B_CALLS, transcendentals=0),
+        name="second_pass",
+    )(ublk, xoff, dy, tokt, table, idsb, ids_flip, slope, *outs)
+
+
+def out_kernel(tie_ref, mat_ref, row_ref, out_ref, tok_ref, acc_ref):
     step = pl.program_id(0)
+    one, two, three = split3(mat_ref[...])
+    rows = row_ref[...]
+    part = dot_nn(one, rows) + dot_nn(two, rows) + dot_nn(three, rows)
 
     @pl.when(step == 0)
     def _():
-        y_acc[...] = y_in[...] if has_in else jnp.zeros_like(y_acc)
-        dx_acc[...] = dx_in[...] if has_in else jnp.zeros_like(dx_acc)
-
-    for mat_ref, row_ref, acc in ((w_ref, v_ref, y_acc), (c_ref, u_ref, dx_acc)):
-        one, two, three = split3(mat_ref[...])
-        rows = row_ref[...]
-        acc[...] += dot_nn(one, rows) + dot_nn(two, rows) + dot_nn(three, rows)
+        acc_ref[...] = part
+        tok_ref[...] = jnp.zeros_like(tok_ref)
+
+    @pl.when(step > 0)
+    def _():
+        acc_ref[...] += part
 
     @pl.when(step == pl.num_programs(0) - 1)
     def _():
-        y_ref[...] = y_acc[...].astype(y_ref.dtype)
-        dx_ref[...] = dx_acc[...].astype(dx_ref.dtype)
-
-
-def out_pass(w, c, v_sel, u_sel):
-    n_tok, n_list = w.shape
-    width = v_sel.shape[1]
-    cols = OWN_STEP * 128
-    per = n_list // cols // OUT_CALLS
-    accs = []
-    whole = pl.BlockSpec((n_tok, width), lambda i: (0, 0))
-    for call in range(OUT_CALLS):
-        at = call * per
-        dtype = BF16 if call == OUT_CALLS - 1 else F32
-        accs = pl.pallas_call(
-            functools.partial(out_kernel, bool(accs)),
-            grid=(per,),
+        out_ref[...] = acc_ref[...].astype(out_ref.dtype)
+
+
+def out_half(tie, mat, rows, half):
+    n_tok, n_list = mat.shape
+    width = rows.shape[1] // 2
+    cols = 1024
+    return pl.pallas_call(
+        out_kernel,
+        grid_spec=pltpu.PrefetchScalarGridSpec(
+            num_scalar_prefetch=1,
+            grid=(n_list // cols,),
             in_specs=[
-                pl.BlockSpec((n_tok, cols), lambda i, at=at: (0, i + at)),
-                pl.BlockSpec((n_tok, cols), lambda i, at=at: (0, i + at)),
-                pl.BlockSpec((cols, width), lambda i, at=at: (i + at, 0)),
-                pl.BlockSpec((cols, width), lambda i, at=at: (i + at, 0)),
-            ] + [whole] * len(accs),
-            out_specs=[whole, whole],
-            out_shape=[jax.ShapeDtypeStruct((n_tok, width), dtype)] * 2,
-            scratch_shapes=[pltpu.VMEM((n_tok, width), F32)] * 2,
-            compiler_params=pltpu.CompilerParams(vmem_limit_bytes=VMEM_LIMIT),
-            cost_estimate=pl.CostEstimate(flops=12 * n_tok * n_list * width // OUT_CALLS, bytes_accessed=n_list * (width * 4 + n_tok * 8) // OUT_CALLS, transcendentals=0),
-            name="out_pass",
-        )(w, c, v_sel, u_sel, *accs)
-    return accs
+                pl.BlockSpec((n_tok, cols), lambda i, t: (0, i)),
+                pl.BlockSpec((cols, width), lambda i, t: (i, half)),
+            ],
+            out_specs=[pl.BlockSpec((n_tok, width), lambda i, t: (0, 0)), pl.BlockSpec((8, 128), lambda i, t: (0, 0))],
+            scratch_shapes=[pltpu.VMEM((n_tok, width), F32)],
+        ),
+        out_shape=[jax.ShapeDtypeStruct((n_tok, width), BF16), jax.ShapeDtypeStruct((8, 128), F32)],
+        compiler_params=pltpu.CompilerParams(vmem_limit_bytes=VMEM_LIMIT),
+        cost_estimate=pl.CostEstimate(flops=6 * n_tok * n_list * width, bytes_accessed=n_list * (width * 2 + n_tok * 4), transcendentals=0),
+        name="out_half",
+    )(tie, mat, rows)
 
 
 def neighbour_pairs(field, step, table_n):
@@ -262,31 +253,67 @@
     return pairs
 
 
-def halve_rows(keep, send, table_n):
-    width = keep.shape[-1]
-    axes = ('data', 'table')
-    swap = [(i, (i + table_n) % (2 * table_n)) for i in range(2 * table_n)]
-    got0 = lax.ppermute(send, axes, swap)
-    cube = (SIDE, SIDE, SIDE, 128, width)
-    keep, got0 = keep.reshape(cube), got0.reshape(cube)
-    done = []
-    for strm in range(3):
-        cut = slice(ROW_CUTS[strm], ROW_CUTS[strm + 1])
-        val = keep[:, :, :, cut].astype(F32) + got0[:, :, :, cut].astype(F32)
-        left = [0, 1, 2]
-        for axis in AXIS_ORDERS[strm]:
-            dim = left.index(axis)
-            left.remove(axis)
-            field = 2 - axis
+class HalveRows:
+    def __init__(self, keep, send, table_n):
+        self.table_n = table_n
+        swap = [(i, (i + table_n) % (2 * table_n)) for i in range(2 * table_n)]
+        self.keep = keep
+        self.gots = [lax.ppermute(send, ('data', 'table'), swap)]
+        self.stage = 0
+
+    def tie(self, token):
+        out = lax.optimization_barrier((token, *self.gots))
+        self.gots = list(out[1:])
+
+    def make_sends(self):
+        if self.stage == 0:
+            cube = (SIDE, SIDE, SIDE, 128, self.keep.shape[-1])
+            pair = [self.keep.reshape(cube), self.gots[0].reshape(cube)]
+            self.terms = [[arr[:, :, :, ROW_CUTS[k]:ROW_CUTS[k + 1]] for arr in pair] for k in range(3)]
+            self.left = [[0, 1, 2] for _ in range(3)]
+        sends = []
+        for k in range(3):
+            axis = AXIS_ORDERS[k][self.stage // 2]
+            dim = self.left[k].index(axis)
             take = lambda arr, lo, hi: lax.slice_in_dim(arr, lo, hi, axis=dim)
-            got = lax.ppermute(take(val, 1, 3).astype(BF16), axes, neighbour_pairs(field, 0, table_n))
-            far = take(val, 3, 4) + take(got, 1, 2).astype(F32)
-            got2 = lax.ppermute(far.astype(BF16), axes, neighbour_pairs(field, 1, table_n))
-            val = take(val, 0, 1) + take(got, 0, 1).astype(F32) + got2.astype(F32)
-            val = val.reshape(val.shape[:dim] + val.shape[dim + 1:])
-        done.append(val)
-    mine = jnp.concatenate(done, axis=0).astype(BF16)
-    return lax.all_gather(mine, 'data', axis=0, tiled=True)
+            add = lambda arrs: functools.reduce(jnp.add, [arr.astype(F32) for arr in arrs]).astype(BF16)
+            if self.stage % 2 == 0:
+                if self.stage > 0:
+                    prev = self.left_dim[k]
+                    self.terms[k] = [t.reshape(t.shape[:prev] + t.shape[prev + 1:]) for t in self.kept[k] + [self.gots[k]]]
+                    self.left[k].remove(AXIS_ORDERS[k][self.stage // 2 - 1])
+                    dim = self.left[k].index(axis)
+                sends.append(add([take(t, 1, 3) for t in self.terms[k]]))
+            else:
+                got = self.gots[k]
+                sends.append(add([take(t, 3, 4) for t in self.terms[k]] + [take(got, 1, 2)]))
+                if k == 0:
+                    self.kept, self.left_dim = [], []
+                self.kept.append([take(t, 0, 1) for t in self.terms[k]] + [take(got, 0, 1)])
+                self.left_dim.append(dim)
+        self.sends = sends
+
+    def send(self):
+        self.gots = [lax.ppermute(self.sends[k], ('data', 'table'), neighbour_pairs(2 - AXIS_ORDERS[k][self.stage // 2], self.stage % 2, self.table_n)) for k in range(3)]
+        self.stage += 1
+
+    def step(self, token=None, hold=None):
+        if token is not None:
+            self.tie(token)
+        self.make_sends()
+        if hold is not None:
+            out = lax.optimization_barrier((hold, *self.sends))
+            hold, self.sends = out[0], list(out[1:])
+        self.send()
+        return hold
+
+    def finish(self):
+        done = []
+        for k in range(3):
+            arrs = [t.reshape(t.shape[-2:]) for t in self.kept[k] + [self.gots[k]]]
+            done.append(functools.reduce(jnp.add, [t.astype(F32) for t in arrs]))
+        mine = jnp.concatenate(done, axis=0).astype(BF16)
+        return lax.all_gather(mine, 'data', axis=0, tiled=True)
 
 
 def solution(mesh):
@@ -317,10 +344,32 @@
         gates = gate_matrix(pick_rel, gate.reshape(n_tok, -1), table_n)
 
         w, slope, u_sel, keep_v, send_v = first_pass(ublk, xoff, tok, dy.T, full_u, idsb, ids_flip, gates)
-        grad_v = halve_rows(keep_v, send_v, table_n)
-        c, v_sel, keep_u, send_u = second_pass(ublk, xoff, dy, tok.T, full_v, idsb, ids_flip, slope)
-        grad_u = halve_rows(keep_u, send_u, table_n)
-        y, dx = out_pass(w, c, v_sel, u_sel)
+        red_v = HalveRows(keep_v, send_v, table_n)
+        tokt = tok.T
+        outs, token = [], None
+        for call in range(B_CALLS):
+            tie = ublk
+            if call != 1:
+                tie = red_v.step(token, ublk)
+            *outs, token = second_part(call, tie, xoff, dy, tokt, full_v, idsb, ids_flip, slope, outs)
+        c, v_sel, keep_u, send_u = outs
+        red_u = HalveRows(keep_u, send_u, table_n)
+        tie = red_v.step(token, xoff)
+        y0, token = out_half(tie, w, v_sel, 0)
+        tie = red_v.step(token, xoff)
+        y1, token = out_half(tie, w, v_sel, 1)
+        tie = red_v.step(token, xoff)
+        tie = red_u.step(token, tie)
+        dx0, token = out_half(tie, c, u_sel, 0)
+        red_v.tie(token)
+        grad_v = red_v.finish()
+        dx1, token = out_half(token[0, :4].astype(jnp.int32), c, u_sel, 1)
+        red_u.step(token)
+        for _ in range(4):
+            red_u.step()
+        grad_u = red_u.finish()
+        y = jnp.concatenate([y0, y1], axis=1)
+        dx = jnp.concatenate([dx0, dx1], axis=1)
         return y, dx, grad_u, grad_v
 
     return jax.shard_map(device_step, mesh=mesh, in_specs=(tok_spec, tok_spec, row_spec, row_spec, tok_spec, tok_spec, tok_spec), out_specs=(tok_spec, tok_spec, row_spec, row_spec), check_vma=False)

time: 646 us -> 609 us (0.943)
  Pallas kernels: 275 us -> 246 us
  waiting for transfers between devices: 164 us -> 144 us
  local copies, waits for them, and re-layouts: 46.5 us -> 33.1 us
  other arithmetic: 90.9 us -> 104 us
  blocking collectives: 12.9 us -> 24 us
    convert_element_type x18 -> x36, other arithmetic: 17.4 us -> 83.8 us  [the longest x34 80.1 us: make_sends(): functools.reduce(jnp.add, [arr.astype(F32) for arr in arrs]).astype(BF16)]
    add x12 -> x2, other arithmetic: 58.8 us -> 5.14 us  [make_sends(): functools.reduce(jnp.add, [arr.astype(F32) for arr in arrs]).astype(BF16)]
    all_gather x1, waiting for transfers between devices: 37.4 us -> 0.02 us  [device_step(): lax.all_gather(own_rows(v_loc), ('table', 'data'), axis=0, tiled=True)]
    pallas_call x12 -> x8, Pallas kernels: 179 us -> 149 us  [the longest x4 74.7 us: out_half(): pl.pallas_call(out_kernel, grid_spec=pltpu.PrefetchScalarGridSpec(num_sca...]
    slice x10 -> x0, local copies, waits for them, and re-layouts: 27 us -> none  [halve_rows(): take = lambda arr, lo, hi: lax.slice_in_dim(arr, lo, hi, axis=dim)]
    reshape x0 -> x9, local copies, waits for them, and re-layouts: none -> 18 us  [make_sends(): t.reshape(t.shape[:prev] + t.shape[prev + 1:])]
    ppermute x38, waiting for transfers between devices: 53.2 us -> 69.4 us  [the longest x2 39.8 us: __init__(): self.gots = [lax.ppermute(send, ('data', 'table'), swap)]]
    all_gather x2, blocking collectives: 12.9 us -> 24 us  [finish(): return lax.all_gather(mine, 'data', axis=0, tiled=True)]
  transfers between devices with their start and end apart: 40 -> 40, of which waited for: 16 -> 13; matrix products, arithmetic and copies ran while one was open for 20% -> 18% of each run, Pallas kernels for 43% -> 38%
where the time goes in v2:
time: 609 us; the launch traced here: 601 us
  Pallas kernels  246 us (40%)
  waiting for transfers between devices  144 us (24%)
  other arithmetic  104 us (17%)
  starting transfers between devices  34.5 us (6%)
  local copies, waits for them, and re-layouts  33.1 us (5%)
  blocking collectives  24 us (4%)
  between operations  15.1 us (2%)
    convert_element_type x34, other arithmetic, make_sends(): functools.reduce(jnp.add, [arr.astype(F32) for arr in arrs]).astype(BF16)  80.1 us
    all_gather x1, waiting for transfers between devices, device_step(): lax.all_gather(own_rows(u_loc), ('table', 'data'), axis=0, tiled=True)  75 us
    pallas_call x4, Pallas kernels, out_half(): pl.pallas_call(out_kernel, grid_spec=pltpu.PrefetchScalarGridSpec(num_sca...  74.7 us
    pallas_call x4, Pallas kernels, second_part(): pl.pallas_call(functools.partial(second_kernel, at, len(outs)), grid_spec...  74.6 us
    pallas_call x1, Pallas kernels, first_pass(): pl.pallas_call(first_kernel, grid_spec=pltpu.PrefetchScalarGridSpec(num_s...  67.3 us
    ppermute x2, waiting for transfers between devices, __init__(): self.gots = [lax.ppermute(send, ('data', 'table'), swap)]  39.8 us
    ppermute x36, starting transfers between devices, send(): lax.ppermute(self.sends[k], ('data', 'table'), neighbour_pairs(2 - AXIS_O...  31 us
    ppermute x36, waiting for transfers between devices, send(): lax.ppermute(self.sends[k], ('data', 'table'), neighbour_pairs(2 - AXIS_O...  29.5 us
  transfers between devices with their start and end apart: 40, of which 13 were waited for; matrix products, arithmetic and copies ran while one was open for 18% of the time, Pallas kernels for 38%

profile of v2, /device:TPU:1, one launch (start us, length us, event | category | flops | bytes accessed | tf_op | source)
XLA Modules:
  0.0 601.1 jit_solution(4807820895506626006)
XLA Ops:
  17.3 29.3 %gate_matrix.1.gate_ref = f32[512,8192]{1,0:T(8,128)} custom-call(s32[512,128]{1,0:T(8,128)} %fusion.9.pick_ref, f32[512,128]{1,0:T(8,128)} %copy.57.gate_ref), custom_call_target="tpu_custom_call" | custom-call | flops 12884901888 | bytes 16777216 | tf_op jit(solution)/shard_map/gate_matrix/pallas_call | solution.py:66
  46.6 75.0 %all-gather.3.cloned.1.call-done.tab_ref = bf16[16384,1024]{1,0:T(8,128)(2,1)} async-done(((bf16[128,1024]{1,0:T(8,128)(2,1)}), bf16[16384,1024]{1,0:T(8,128)(2,1)}) %all-gather.3.cloned.1.call-update) | async-done | bytes 33554448 | tf_op jit(solution)/shard_map/all_gather | solution.py:331
  121.7 5.0 broadcast_in_dim.4.idsb_ref
  126.7 67.3 %first_pass.1 = (f32[512,8192]{1,0:T(8,128)}, f32[512,8192]{1,0:T(8,128)}, bf16[8192,1024]{1,0:T(8,128)(2,1)}, bf16[8192,1024]{1,0:T(8,128)(2,1)}, bf16[8192,1024]{1,0:T(8,128)(2,1)}) custom-call(s32[16]{0:T(128)} %fusion.35.ublk_ref, s32[4]{0:T(128)} %fusion.36.xoff_ref.tie_ref, bf16[512,1024]{1,0:T(8,128)(2,1)} %tok_ref.1, bf16[1024,512]{1,0:T(8,128)(2,1)} %bitcast.296, ...), custom_call_target="tpu_custom_call" | custom-call | flops 47244640256 | bytes 134217728 | tf_op jit(solution)/shard_map/first_pass/pallas_call | solution.py:124
  194.3 39.8 %collective-permute-done = bf16[8192,1024]{1,0:T(8,128)(2,1)S(1)} collective-permute-done((bf16[8192,1024]{1,0:T(8,128)(2,1)}, bf16[8192,1024]{1,0:T(8,128)(2,1)S(1)}, u32[]{:S(2)}, u32[]{:S(2)}) %collective-permute-start) | collective-permute-done | bytes 16777248 | tf_op jit(solution)/shard_map/ppermute | solution.py:261
  234.1 6.6 %add_convert_fusion.4 = bf16[2,4,4,40,1024]{4,3,2,1,0:T(8,128)(2,1)} fusion(bf16[4,4,4,128,1024]{4,3,2,1,0:T(8,128)(2,1)S(1)} %bitcast.272, bf16[4,4,4,128,1024]{4,3,2,1,0:T(8,128)(2,1)} %bitcast.259), kind=kLoop, calls=%fused_computation.5 | loop fusion | flops 5242880 | bytes 7864320 | tf_op jit(solution)/shard_map/convert_element_type | solution.py:279
  240.7 5.2 add_convert_fusion.5
  246.0 4.1 add_convert_fusion.1
  250.0 2.4 collective-permute-start.1
  253.8 2.5 collective-permute-start.2
  257.2 2.6 slice_bitcast_fusion.5
  261.4 18.7 %second_pass.4 = (f32[512,8192]{1,0:T(8,128)}, bf16[8192,1024]{1,0:T(8,128)(2,1)}, bf16[8192,1024]{1,0:T(8,128)(2,1)}, bf16[8192,1024]{1,0:T(8,128)(2,1)}, f32[8,128]{1,0:T(8,128)}) custom-call(s32[16]{0:T(128)} %fusion.35.ublk_ref, s32[4]{0:T(128)} %fusion.36.xoff_ref.tie_ref, bf16[512,1024]{1,0:T(8,128)(2,1)} %dy_ref.7, bf16[1024,512]{1,0:T(8,128)(2,1)} %bitcast.255, ...), custom_call_target="tpu_custom_call" | custom-call | flops 11811160064 | bytes 29360128 | tf_op jit(solution)/shard_map/second_pass/pallas_call | solution.py:176
  280.0 18.7 %second_pass.5 = (f32[512,8192]{1,0:T(8,128)}, bf16[8192,1024]{1,0:T(8,128)(2,1)}, bf16[8192,1024]{1,0:T(8,128)(2,1)}, bf16[8192,1024]{1,0:T(8,128)(2,1)}, f32[8,128]{1,0:T(8,128)}) custom-call(s32[16]{0:T(128)} %fusion.35.ublk_ref, s32[4]{0:T(128)} %fusion.36.xoff_ref.tie_ref, ...), custom_call_target="tpu_custom_call", output_to_operand_aliasing={{0}: (8, {}), {1}: (9, {}), {2}: (10, {}), {3}: (11, {})} | custom-call | flops 11811160064 | bytes 29360128 | tf_op jit(solution)/shard_map/second_pass/pallas_call | solution.py:176
  298.7 4.1 add_convert_fusion.8
  302.8 4.1 add_convert_fusion.9
  306.9 3.6 slice_bitcast_fusion.1
  310.5 3.9 fusion.1
  316.4 3.8 slice_bitcast_fusion.4
  320.2 18.6 %second_pass.6 = (f32[512,8192]{1,0:T(8,128)}, bf16[8192,1024]{1,0:T(8,128)(2,1)}, bf16[8192,1024]{1,0:T(8,128)(2,1)}, bf16[8192,1024]{1,0:T(8,128)(2,1)}, f32[8,128]{1,0:T(8,128)}) custom-call(s32[16]{0:T(128)} %fusion.35.ublk_ref, s32[4]{0:T(128)} %fusion.36.xoff_ref.tie_ref, ...), custom_call_target="tpu_custom_call", output_to_operand_aliasing={{0}: (8, {}), {1}: (9, {}), {2}: (10, {}), {3}: (11, {})} | custom-call | flops 11811160064 | bytes 29360128 | tf_op jit(solution)/shard_map/second_pass/pallas_call | solution.py:176
  338.9 3.2 fusion.2
  342.1 2.7 add_convert_fusion.14
  344.8 2.6 add_convert_fusion.11
  347.4 18.6 %second_pass.7 = (f32[512,8192]{1,0:T(8,128)}, bf16[8192,1024]{1,0:T(8,128)(2,1)}, bf16[8192,1024]{1,0:T(8,128)(2,1)}, bf16[8192,1024]{1,0:T(8,128)(2,1)}, f32[8,128]{1,0:T(8,128)}) custom-call(s32[16]{0:T(128)} %fusion.35.ublk_ref, s32[4]{0:T(128)} %fusion.36.xoff_ref.tie_ref, ...), custom_call_target="tpu_custom_call", output_to_operand_aliasing={{0}: (8, {}), {1}: (9, {}), {2}: (10, {}), {3}: (11, {})} | custom-call | flops 11811160064 | bytes 29360128 | tf_op jit(solution)/shard_map/second_pass/pallas_call | solution.py:176
  366.1 3.1 collective-permute-start.16
  372.4 2.5 slice_bitcast_fusion.3
  376.5 4.2 collective-permute-done.8
  382.1 2.8 add_convert_fusion.19
  384.9 2.3 fusion.5
  389.7 18.7 %out_half.4 = (bf16[512,512]{1,0:T(8,128)(2,1)}, f32[8,128]{1,0:T(8,128)}) custom-call(s32[4]{0:T(128)} %fusion.36.xoff_ref.tie_ref, f32[512,8192]{1,0:T(8,128)} %get-tuple-element.102.mat_ref, bf16[8192,1024]{1,0:T(8,128)(2,1)} %get-tuple-element.119.row_ref), custom_call_target="tpu_custom_call" | custom-call | flops 12884901888 | bytes 25165824 | tf_op jit(solution)/shard_map/out_half/pallas_call | solution.py:229
  418.2 18.7 %out_half.5 = (bf16[512,512]{1,0:T(8,128)(2,1)}, f32[8,128]{1,0:T(8,128)}) custom-call(s32[4]{0:T(128)} %fusion.36.xoff_ref.tie_ref, f32[512,8192]{1,0:T(8,128)} %get-tuple-element.102.mat_ref, bf16[8192,1024]{1,0:T(8,128)(2,1)} %get-tuple-element.119.row_ref), custom_call_target="tpu_custom_call" | custom-call | flops 12884901888 | bytes 25165824 | tf_op jit(solution)/shard_map/out_half/pallas_call | solution.py:229
  445.1 5.5 add_convert_fusion.2
  450.6 4.7 add_convert_fusion
  455.3 5.3 add_convert_fusion.3
  464.9 18.7 %out_half.6 = (bf16[512,512]{1,0:T(8,128)(2,1)}, f32[8,128]{1,0:T(8,128)}) custom-call(s32[4]{0:T(128)} %fusion.36.xoff_ref.tie_ref, f32[512,8192]{1,0:T(8,128)} %get-tuple-element.141.mat_ref, bf16[8192,1024]{1,0:T(8,128)(2,1)} %get-tuple-element.142.row_ref), custom_call_target="tpu_custom_call" | custom-call | flops 12884901888 | bytes 25165824 | tf_op jit(solution)/shard_map/out_half/pallas_call | solution.py:229
  489.2 18.7 %out_half.7 = (bf16[512,512]{1,0:T(8,128)(2,1)}, f32[8,128]{1,0:T(8,128)}) custom-call(s32[4]{0:T(128)} %convert_bitcast_fusion.tie_ref, f32[512,8192]{1,0:T(8,128)} %get-tuple-element.141.mat_ref, bf16[8192,1024]{1,0:T(8,128)(2,1)} %get-tuple-element.142.row_ref), custom_call_target="tpu_custom_call" | custom-call | flops 12884901888 | bytes 25165824 | tf_op jit(solution)/shard_map/out_half/pallas_call | solution.py:229
  507.9 3.0 add_convert_fusion.7
  511.0 3.0 add_convert_fusion.6
  514.0 2.5 slice_convert_fusion
  517.1 2.7 fusion
  524.4 3.3 collective-permute-done.25
  531.0 2.3 collective-permute-done.30
  534.8 11.8 %all_gather.15 = bf16[256,1024]{1,0:T(8,128)(2,1)S(1)} all-gather(bf16[128,1024]{1,0:T(8,128)(2,1)S(1)} %pad_maximum_fusion.3), channel_id=1, replica_groups=mesh['replica'=1,'data'=2,'table'=64] {'data'}, dimensions={0}, use_global_device_ids=true | all-gather | bytes 786432 | tf_op jit(solution)/shard_map/all_gather | solution.py:316
  547.3 2.7 collective-permute-start.21
  553.6 4.2 collective-permute-done.27
  561.7 5.1 collective-permute-done.28
  573.5 2.5 collective-permute-done.23
  576.3 3.6 collective-permute-done.24
  580.1 12.1 %all_gather.14 = bf16[256,1024]{1,0:T(8,128)(2,1)S(1)} all-gather(bf16[128,1024]{1,0:T(8,128)(2,1)S(1)} %pad_maximum_fusion.2), channel_id=1, replica_groups=mesh['replica'=1,'data'=2,'table'=64] {'data'}, dimensions={0}, use_global_device_ids=true | all-gather | bytes 786432 | tf_op jit(solution)/shard_map/all_gather | solution.py:316
  (161 shorter events, 79.5 us)
Async XLA Ops:
  7.2 114.4 %all-gather.3.cloned.1.call-start = ((), (), s32[]{:S(2)}) async-start(), calls=%async_computation | async-start | bytes 33816576 | tf_op jit(solution)/shard_map/all_gather | solution.py:331
  9.0 252.4 %all-gather.5.cloned.1.call-start = ((), (), s32[]{:S(2)}) async-start(), calls=%async_computation.1 | async-start | bytes 33816576 | tf_op jit(solution)/shard_map/all_gather | solution.py:332
  194.0 40.1 %collective-permute-start = (bf16[8192,1024]{1,0:T(8,128)(2,1)}, bf16[8192,1024]{1,0:T(8,128)(2,1)S(1)}, u32[]{:S(2)}, u32[]{:S(2)}) collective-permute-start(bf16[8192,1024]{1,0:T(8,128)(2,1)} %get-tuple-element.82), channel_id=1, source_target_pairs={{0,64},{1,65},{2,66},{3,67},{4,68},{5,69},{6,70},{7,71},{8,72},{9,... | collective-permute-start | bytes 50331656 | tf_op jit(solution)/shard_map/ppermute | solution.py:261
  234.1 11.9 %copy-start.3 = (bf16[8192,1024]{1,0:T(8,128)(2,1)}, bf16[8192,1024]{1,0:T(8,128)(2,1)S(1)}, u32[]{:S(2)}) copy-start(bf16[8192,1024]{1,0:T(8,128)(2,1)S(1)} %collective-permute-done) | copy-start | bytes 50331652
  250.0 48.7 %collective-permute-start.1 = (bf16[4,4,2,48,1024]{4,3,0,1,2:T(8,128)(2,1)}, bf16[4,4,2,48,1024]{4,3,0,1,2:T(8,128)(2,1)}, u32[]{:S(2)}, u32[]{:S(2)}) collective-permute-start(bf16[4,4,2,48,1024]{4,3,0,1,2:T(8,128)(2,1)} %add_convert_fusion.1), channel_id=1, source_target_pairs={{0,1},{1,0},{2,3},{3,2},{4,5},{5,4},{6,7},{7,6},{8,9},{9,8},{10,11... | collective-permute-start | bytes 9437192 | tf_op jit(solution)/shard_map/ppermute | solution.py:297
  253.8 44.9 %collective-permute-start.2 = (bf16[4,2,4,40,1024]{4,3,2,1,0:T(8,128)(2,1)}, bf16[4,2,4,40,1024]{4,3,2,1,0:T(8,128)(2,1)}, u32[]{:S(2)}, u32[]{:S(2)}) collective-permute-start(bf16[4,2,4,40,1024]{4,3,2,1,0:T(8,128)(2,1)} %add_convert_fusion.5), channel_id=1, source_target_pairs={{0,4},{1,5},{2,6},{3,7},{4,0},{5,1},{6,2},{7,3},{8,12},{9,13},{10,... | collective-permute-start | bytes 7864328 | tf_op jit(solution)/shard_map/ppermute | solution.py:297
  256.2 42.5 %collective-permute-start.3 = (bf16[2,4,4,40,1024]{4,3,2,1,0:T(8,128)(2,1)}, bf16[2,4,4,40,1024]{4,3,2,1,0:T(8,128)(2,1)}, u32[]{:S(2)}, u32[]{:S(2)}) collective-permute-start(bf16[2,4,4,40,1024]{4,3,2,1,0:T(8,128)(2,1)} %add_convert_fusion.4), channel_id=1, source_target_pairs={{0,16},{1,17},{2,18},{3,19},{4,20},{5,21},{6,22},{7,23},{8,24},{9,... | collective-permute-start | bytes 7864328 | tf_op jit(solution)/shard_map/ppermute | solution.py:297
  314.4 24.5 %collective-permute-start.4 = (bf16[4,4,1,48,1024]{4,3,2,1,0:T(8,128)(2,1)}, bf16[4,4,1,48,1024]{4,3,2,1,0:T(8,128)(2,1)}, u32[]{:S(2)}, u32[]{:S(2)}) collective-permute-start(bf16[4,4,1,48,1024]{4,3,2,1,0:T(8,128)(2,1)} %fusion.1), channel_id=1, source_target_pairs={{0,3},{1,2},{2,1},{3,0},{4,7},{5,6},{6,5},{7,4},{8,11},{9,10},{10,... | collective-permute-start | bytes 4718600 | tf_op jit(solution)/shard_map/ppermute | solution.py:297
  316.0 28.8 %copy-start.4 = (bf16[4,4,48,1024]{3,2,0,1:T(8,128)(2,1)}, bf16[4,4,48,1024]{3,2,0,1:T(8,128)(2,1)S(1)}, u32[]{:S(2)}) copy-start(bf16[4,4,48,1024]{3,2,0,1:T(8,128)(2,1)S(1)} %copy_bitcast_fusion.2) | copy-start | bytes 4718596
  316.0 22.8 %collective-permute-start.5 = (bf16[4,1,4,40,1024]{4,3,2,1,0:T(8,128)(2,1)}, bf16[4,1,4,40,1024]{4,3,2,1,0:T(8,128)(2,1)}, u32[]{:S(2)}, u32[]{:S(2)}) collective-permute-start(bf16[4,1,4,40,1024]{4,3,2,1,0:T(8,128)(2,1)} %add_convert_fusion.9), channel_id=1, source_target_pairs={{0,12},{1,13},{2,14},{3,15},{4,8},{5,9},{6,10},{7,11},{8,4},{9,5},... | collective-permute-start | bytes 3932168 | tf_op jit(solution)/shard_map/ppermute | solution.py:297
  316.1 22.8 %collective-permute-start.6 = (bf16[1,4,4,40,1024]{4,3,2,1,0:T(8,128)(2,1)}, bf16[1,4,4,40,1024]{4,3,2,1,0:T(8,128)(2,1)}, u32[]{:S(2)}, u32[]{:S(2)}) collective-permute-start(bf16[1,4,4,40,1024]{4,3,2,1,0:T(8,128)(2,1)} %add_convert_fusion.8), channel_id=1, source_target_pairs={{0,48},{1,49},{2,50},{3,51},{4,52},{5,53},{6,54},{7,55},{8,56},{9,... | collective-permute-start | bytes 3932168 | tf_op jit(solution)/shard_map/ppermute | solution.py:297
  366.1 79.0 %collective-permute-start.16 = (bf16[8192,1024]{1,0:T(8,128)(2,1)}, bf16[8192,1024]{1,0:T(8,128)(2,1)}, u32[]{:S(2)}, u32[]{:S(2)}) collective-permute-start(bf16[8192,1024]{1,0:T(8,128)(2,1)} %get-tuple-element.138), channel_id=1, source_target_pairs={{0,64},{1,65},{2,66},{3,67},{4,68},{5,69},{6,70},{7,71},{8,72},{9,... | collective-permute-start | bytes 50331656 | tf_op jit(solution)/shard_map/ppermute | solution.py:261
  369.2 12.9 %collective-permute-start.7 = (bf16[4,2,48,1024]{3,2,0,1:T(8,128)(2,1)}, bf16[4,2,48,1024]{3,2,0,1:T(8,128)(2,1)S(1)}, u32[]{:S(2)}, u32[]{:S(2)}) collective-permute-start(bf16[4,2,48,1024]{3,2,0,1:T(8,128)(2,1)} %add_convert_fusion.11), channel_id=1, source_target_pairs={{0,4},{1,5},{2,6},{3,7},{4,0},{5,1},{6,2},{7,3},{8,12},{9,13},{10,... | collective-permute-start | bytes 2359304 | tf_op jit(solution)/shard_map/ppermute | solution.py:297
  370.1 10.6 %collective-permute-start.8 = (bf16[2,4,40,1024]{3,2,1,0:T(8,128)(2,1)}, bf16[2,4,40,1024]{3,2,1,0:T(8,128)(2,1)S(1)}, u32[]{:S(2)}, u32[]{:S(2)}) collective-permute-start(bf16[2,4,40,1024]{3,2,1,0:T(8,128)(2,1)} %fusion.2), channel_id=1, source_target_pairs={{0,16},{1,17},{2,18},{3,19},{4,20},{5,21},{6,22},{7,23},{8,24},{9,... | collective-permute-start | bytes 1966088 | tf_op jit(solution)/shard_map/ppermute | solution.py:297
  371.5 10.6 %collective-permute-start.9 = (bf16[4,2,40,1024]{3,2,1,0:T(8,128)(2,1)}, bf16[4,2,40,1024]{3,2,1,0:T(8,128)(2,1)S(1)}, u32[]{:S(2)}, u32[]{:S(2)}) collective-permute-start(bf16[4,2,40,1024]{3,2,1,0:T(8,128)(2,1)} %add_convert_fusion.14), channel_id=1, source_target_pairs={{0,1},{1,0},{2,3},{3,2},{4,5},{5,4},{6,7},{7,6},{8,9},{9,8},{10,11... | collective-permute-start | bytes 1966088 | tf_op jit(solution)/shard_map/ppermute | solution.py:297
  380.7 8.0 %copy-start.13 = (bf16[2,4,40,1024]{3,2,1,0:T(8,128)(2,1)}, bf16[2,4,40,1024]{3,2,1,0:T(8,128)(2,1)S(1)}, u32[]{:S(2)}) copy-start(bf16[2,4,40,1024]{3,2,1,0:T(8,128)(2,1)S(1)} %collective-permute-done.8) | copy-start | bytes 1966084
  382.1 6.6 %copy-start.12 = (bf16[4,2,40,1024]{3,2,1,0:T(8,128)(2,1)}, bf16[4,2,40,1024]{3,2,1,0:T(8,128)(2,1)S(1)}, u32[]{:S(2)}) copy-start(bf16[4,2,40,1024]{3,2,1,0:T(8,128)(2,1)S(1)} %collective-permute-done.9) | copy-start | bytes 1966084
  382.1 6.6 %copy-start.11 = (bf16[4,2,48,1024]{3,2,0,1:T(8,128)(2,1)}, bf16[4,2,48,1024]{3,2,0,1:T(8,128)(2,1)S(1)}, u32[]{:S(2)}) copy-start(bf16[4,2,48,1024]{3,2,0,1:T(8,128)(2,1)S(1)} %collective-permute-done.7) | copy-start | bytes 2359300
  388.8 19.6 %collective-permute-start.10 = (bf16[4,1,48,1024]{3,2,0,1:T(8,128)(2,1)S(1)}, bf16[4,1,48,1024]{3,2,0,1:T(8,128)(2,1)S(1)}, u32[]{:S(2)}, u32[]{:S(2)}) collective-permute-start(bf16[4,1,48,1024]{3,2,0,1:T(8,128)(2,1)S(1)} %add_convert_fusion.17), channel_id=1, source_target_pairs={{0,12},{1,13},{2,14},{3,15},{4,8},{5,9},{6,10},{7,11},{8,4},{9,5},... | collective-permute-start | bytes 1179656 | tf_op jit(solution)/shard_map/ppermute | solution.py:297
  388.9 19.5 %collective-permute-start.11 = (bf16[1,4,40,1024]{3,2,1,0:T(8,128)(2,1)}, bf16[1,4,40,1024]{3,2,1,0:T(8,128)(2,1)}, u32[]{:S(2)}, u32[]{:S(2)}) collective-permute-start(bf16[1,4,40,1024]{3,2,1,0:T(8,128)(2,1)} %fusion.5), channel_id=1, source_target_pairs={{0,48},{1,49},{2,50},{3,51},{4,52},{5,53},{6,54},{7,55},{8,56},{9,... | collective-permute-start | bytes 983048 | tf_op jit(solution)/shard_map/ppermute | solution.py:297
  389.5 18.9 %collective-permute-start.12 = (bf16[4,1,40,1024]{3,2,1,0:T(8,128)(2,1)}, bf16[4,1,40,1024]{3,2,1,0:T(8,128)(2,1)}, u32[]{:S(2)}, u32[]{:S(2)}) collective-permute-start(bf16[4,1,40,1024]{3,2,1,0:T(8,128)(2,1)} %add_convert_fusion.19), channel_id=1, source_target_pairs={{0,3},{1,2},{2,1},{3,0},{4,7},{5,6},{6,5},{7,4},{8,11},{9,10},{10,... | collective-permute-start | bytes 983048 | tf_op jit(solution)/shard_map/ppermute | solution.py:297
  414.7 22.2 %copy-start.16 = (bf16[512,512]{1,0:T(8,128)(2,1)S(1)}, bf16[512,512]{1,0:T(8,128)(2,1)}, u32[]{:S(2)}) copy-start(bf16[512,512]{1,0:T(8,128)(2,1)} %get-tuple-element.120) | copy-start | bytes 1572868
  414.7 24.4 %collective-permute-start.13 = (bf16[2,48,1024]{2,1,0:T(8,128)(2,1)}, bf16[2,48,1024]{2,1,0:T(8,128)(2,1)}, u32[]{:S(2)}, u32[]{:S(2)}) collective-permute-start(bf16[2,48,1024]{2,1,0:T(8,128)(2,1)} %fusion.10), channel_id=1, source_target_pairs={{0,16},{1,17},{2,18},{3,19},{4,20},{5,21},{6,22},{7,23},{8,24},{9,... | collective-permute-start | bytes 589832 | tf_op jit(solution)/shard_map/ppermute | solution.py:297
  415.8 23.2 %collective-permute-start.14 = (bf16[2,40,1024]{2,1,0:T(8,128)(2,1)}, bf16[2,40,1024]{2,1,0:T(8,128)(2,1)}, u32[]{:S(2)}, u32[]{:S(2)}) collective-permute-start(bf16[2,40,1024]{2,1,0:T(8,128)(2,1)} %fusion.7), channel_id=1, source_target_pairs={{0,1},{1,0},{2,3},{3,2},{4,5},{5,4},{6,7},{7,6},{8,9},{9,8},{10,11... | collective-permute-start | bytes 491528 | tf_op jit(solution)/shard_map/ppermute | solution.py:297
  416.5 22.6 %collective-permute-start.15 = (bf16[2,40,1024]{2,1,0:T(8,128)(2,1)}, bf16[2,40,1024]{2,1,0:T(8,128)(2,1)}, u32[]{:S(2)}, u32[]{:S(2)}) collective-permute-start(bf16[2,40,1024]{2,1,0:T(8,128)(2,1)} %fusion.19), channel_id=1, source_target_pairs={{0,4},{1,5},{2,6},{3,7},{4,0},{5,1},{6,2},{7,3},{8,12},{9,13},{10,... | collective-permute-start | bytes 491528 | tf_op jit(solution)/shard_map/ppermute | solution.py:297
  442.7 41.0 %collective-permute-start.35 = (bf16[1,48,1024]{2,1,0:T(8,128)(2,1)S(1)}, bf16[1,48,1024]{2,1,0:T(8,128)(2,1)S(1)}, u32[]{:S(2)}, u32[]{:S(2)}) collective-permute-start(bf16[1,48,1024]{2,1,0:T(8,128)(2,1)S(1)} %fusion.18), channel_id=1, source_target_pairs={{0,48},{1,49},{2,50},{3,51},{4,52},{5,53},{6,54},{7,55},{8,56},{9,... | collective-permute-start | bytes 294920 | tf_op jit(solution)/shard_map/ppermute | solution.py:297
  443.5 19.8 %collective-permute-start.36 = (bf16[1,40,1024]{2,1,0:T(8,128)(2,1)S(1)}, bf16[1,40,1024]{2,1,0:T(8,128)(2,1)S(1)}, u32[]{:S(2)}, u32[]{:S(2)}) collective-permute-start(bf16[1,40,1024]{2,1,0:T(8,128)(2,1)S(1)} %fusion.28), channel_id=1, source_target_pairs={{0,3},{1,2},{2,1},{3,0},{4,7},{5,6},{6,5},{7,4},{8,11},{9,10},{10,... | collective-permute-start | bytes 245768 | tf_op jit(solution)/shard_map/ppermute | solution.py:297
  444.3 39.3 %collective-permute-start.37 = (bf16[1,40,1024]{2,1,0:T(8,128)(2,1)S(1)}, bf16[1,40,1024]{2,1,0:T(8,128)(2,1)S(1)}, u32[]{:S(2)}, u32[]{:S(2)}) collective-permute-start(bf16[1,40,1024]{2,1,0:T(8,128)(2,1)S(1)} %fusion.30), channel_id=1, source_target_pairs={{0,12},{1,13},{2,14},{3,15},{4,8},{5,9},{6,10},{7,11},{8,4},{9,5},... | collective-permute-start | bytes 245768 | tf_op jit(solution)/shard_map/ppermute | solution.py:297
  460.6 47.2 %collective-permute-start.17 = (bf16[4,4,2,48,1024]{4,3,0,1,2:T(8,128)(2,1)}, bf16[4,4,2,48,1024]{4,3,0,1,2:T(8,128)(2,1)}, u32[]{:S(2)}, u32[]{:S(2)}) collective-permute-start(bf16[4,4,2,48,1024]{4,3,0,1,2:T(8,128)(2,1)} %add_convert_fusion), channel_id=1, source_target_pairs={{0,1},{1,0},{2,3},{3,2},{4,5},{5,4},{6,7},{7,6},{8,9},{9,8},{10,11... | collective-permute-start | bytes 9437192 | tf_op jit(solution)/shard_map/ppermute | solution.py:297
  462.4 45.4 %collective-permute-start.18 = (bf16[4,2,4,40,1024]{4,3,2,1,0:T(8,128)(2,1)}, bf16[4,2,4,40,1024]{4,3,2,1,0:T(8,128)(2,1)}, u32[]{:S(2)}, u32[]{:S(2)}) collective-permute-start(bf16[4,2,4,40,1024]{4,3,2,1,0:T(8,128)(2,1)} %add_convert_fusion.3), channel_id=1, source_target_pairs={{0,4},{1,5},{2,6},{3,7},{4,0},{5,1},{6,2},{7,3},{8,12},{9,13},{10,... | collective-permute-start | bytes 7864328 | tf_op jit(solution)/shard_map/ppermute | solution.py:297
  463.3 44.5 %collective-permute-start.19 = (bf16[2,4,4,40,1024]{4,3,2,1,0:T(8,128)(2,1)}, bf16[2,4,4,40,1024]{4,3,2,1,0:T(8,128)(2,1)}, u32[]{:S(2)}, u32[]{:S(2)}) collective-permute-start(bf16[2,4,4,40,1024]{4,3,2,1,0:T(8,128)(2,1)} %add_convert_fusion.2), channel_id=1, source_target_pairs={{0,16},{1,17},{2,18},{3,19},{4,20},{5,21},{6,22},{7,23},{8,24},{9,... | collective-permute-start | bytes 7864328 | tf_op jit(solution)/shard_map/ppermute | solution.py:297
  510.9 16.8 %collective-permute-start.25 = (bf16[4,1,4,40,1024]{4,3,2,1,0:T(8,128)(2,1)S(1)}, bf16[4,1,4,40,1024]{4,3,2,1,0:T(8,128)(2,1)S(1)}, u32[]{:S(2)}, u32[]{:S(2)}) collective-permute-start(bf16[4,1,4,40,1024]{4,3,2,1,0:T(8,128)(2,1)S(1)} %add_convert_fusion.7), channel_id=1, source_target_pairs={{0,12},{1,13},{2,14},{3,15},{4,8},{5,9},{6,10},{7,11},{8,4},{9,5},... | collective-permute-start | bytes 3932168 | tf_op jit(solution)/shard_map/ppermute | solution.py:297
  516.5 16.8 %collective-permute-start.30 = (bf16[1,4,4,40,1024]{4,3,2,1,0:T(8,128)(2,1)S(1)}, bf16[1,4,4,40,1024]{4,3,2,1,0:T(8,128)(2,1)S(1)}, u32[]{:S(2)}, u32[]{:S(2)}) collective-permute-start(bf16[1,4,4,40,1024]{4,3,2,1,0:T(8,128)(2,1)S(1)} %add_convert_fusion.6), channel_id=1, source_target_pairs={{0,48},{1,49},{2,50},{3,51},{4,52},{5,53},{6,54},{7,55},{8,56},{9,... | collective-permute-start | bytes 3932168 | tf_op jit(solution)/shard_map/ppermute | solution.py:297
  519.8 26.8 %collective-permute-start.20 = (bf16[4,4,1,48,1024]{4,3,2,1,0:T(8,128)(2,1)S(1)}, bf16[4,4,1,48,1024]{4,3,2,1,0:T(8,128)(2,1)S(1)}, u32[]{:S(2)}, u32[]{:S(2)}) collective-permute-start(bf16[4,4,1,48,1024]{4,3,2,1,0:T(8,128)(2,1)S(1)} %fusion), channel_id=1, source_target_pairs={{0,3},{1,2},{2,1},{3,0},{4,7},{5,6},{6,5},{7,4},{8,11},{9,10},{10,... | collective-permute-start | bytes 4718600 | tf_op jit(solution)/shard_map/ppermute | solution.py:297
  524.4 8.9 %copy-start.8 = (bf16[4,4,40,1024]{3,2,1,0:T(8,128)(2,1)S(1)}, bf16[4,4,40,1024]{3,2,1,0:T(8,128)(2,1)}, u32[]{:S(2)}) copy-start(bf16[4,4,40,1024]{3,2,1,0:T(8,128)(2,1)} %slice_bitcast_fusion.3) | copy-start | bytes 3932164
  529.7 20.4 %collective-permute-start.26 = (bf16[2,4,40,1024]{3,2,1,0:T(8,128)(2,1)S(1)}, bf16[2,4,40,1024]{3,2,1,0:T(8,128)(2,1)S(1)}, u32[]{:S(2)}, u32[]{:S(2)}) collective-permute-start(bf16[2,4,40,1024]{3,2,1,0:T(8,128)(2,1)S(1)} %fusion.3), channel_id=1, source_target_pairs={{0,16},{1,17},{2,18},{3,19},{4,20},{5,21},{6,22},{7,23},{8,24},{9,... | collective-permute-start | bytes 1966088 | tf_op jit(solution)/shard_map/ppermute | solution.py:297
  533.8 18.0 %collective-permute-start.31 = (bf16[4,2,40,1024]{3,2,1,0:T(8,128)(2,1)S(1)}, bf16[4,2,40,1024]{3,2,1,0:T(8,128)(2,1)S(1)}, u32[]{:S(2)}, u32[]{:S(2)}) collective-permute-start(bf16[4,2,40,1024]{3,2,1,0:T(8,128)(2,1)S(1)} %add_convert_fusion.12), channel_id=1, source_target_pairs={{0,1},{1,0},{2,3},{3,2},{4,5},{5,4},{6,7},{7,6},{8,9},{9,8},{10,11... | collective-permute-start | bytes 1966088 | tf_op jit(solution)/shard_map/ppermute | solution.py:297
  547.3 13.2 %collective-permute-start.21 = (bf16[4,2,48,1024]{3,2,0,1:T(8,128)(2,1)S(1)}, bf16[4,2,48,1024]{3,2,0,1:T(8,128)(2,1)S(1)}, u32[]{:S(2)}, u32[]{:S(2)}) collective-permute-start(bf16[4,2,48,1024]{3,2,0,1:T(8,128)(2,1)S(1)} %add_convert_fusion.10), channel_id=1, source_target_pairs={{0,4},{1,5},{2,6},{3,7},{4,0},{5,1},{6,2},{7,3},{8,12},{9,13},{10,... | collective-permute-start | bytes 2359304 | tf_op jit(solution)/shard_map/ppermute | solution.py:297
  551.5 6.3 %collective-permute-start.27 = (bf16[1,4,40,1024]{3,2,1,0:T(8,128)(2,1)S(1)}, bf16[1,4,40,1024]{3,2,1,0:T(8,128)(2,1)S(1)}, u32[]{:S(2)}, u32[]{:S(2)}) collective-permute-start(bf16[1,4,40,1024]{3,2,1,0:T(8,128)(2,1)S(1)} %fusion.4), channel_id=1, source_target_pairs={{0,48},{1,49},{2,50},{3,51},{4,52},{5,53},{6,54},{7,55},{8,56},{9,... | collective-permute-start | bytes 983048 | tf_op jit(solution)/shard_map/ppermute | solution.py:297
  552.1 7.9 %collective-permute-start.32 = (bf16[4,1,40,1024]{3,2,1,0:T(8,128)(2,1)S(1)}, bf16[4,1,40,1024]{3,2,1,0:T(8,128)(2,1)S(1)}, u32[]{:S(2)}, u32[]{:S(2)}) collective-permute-start(bf16[4,1,40,1024]{3,2,1,0:T(8,128)(2,1)S(1)} %add_convert_fusion.18), channel_id=1, source_target_pairs={{0,3},{1,2},{2,1},{3,0},{4,7},{5,6},{6,5},{7,4},{8,11},{9,10},{10,... | collective-permute-start | bytes 983048 | tf_op jit(solution)/shard_map/ppermute | solution.py:297
  559.0 7.8 %collective-permute-start.28 = (bf16[2,40,1024]{2,1,0:T(8,128)(2,1)S(1)}, bf16[2,40,1024]{2,1,0:T(8,128)(2,1)S(1)}, u32[]{:S(2)}, u32[]{:S(2)}) collective-permute-start(bf16[2,40,1024]{2,1,0:T(8,128)(2,1)S(1)} %fusion.6), channel_id=1, source_target_pairs={{0,1},{1,0},{2,3},{3,2},{4,5},{5,4},{6,7},{7,6},{8,9},{9,8},{10,11... | collective-permute-start | bytes 491528 | tf_op jit(solution)/shard_map/ppermute | solution.py:297
  560.2 7.8 %collective-permute-start.33 = (bf16[2,40,1024]{2,1,0:T(8,128)(2,1)S(1)}, bf16[2,40,1024]{2,1,0:T(8,128)(2,1)S(1)}, u32[]{:S(2)}, u32[]{:S(2)}) collective-permute-start(bf16[2,40,1024]{2,1,0:T(8,128)(2,1)S(1)} %fusion.20), channel_id=1, source_target_pairs={{0,4},{1,5},{2,6},{3,7},{4,0},{5,1},{6,2},{7,3},{8,12},{9,13},{10,... | collective-permute-start | bytes 491528 | tf_op jit(solution)/shard_map/ppermute | solution.py:297
  560.8 8.9 %collective-permute-start.22 = (bf16[4,1,48,1024]{3,2,0,1:T(8,128)(2,1)S(1)}, bf16[4,1,48,1024]{3,2,0,1:T(8,128)(2,1)S(1)}, u32[]{:S(2)}, u32[]{:S(2)}) collective-permute-start(bf16[4,1,48,1024]{3,2,0,1:T(8,128)(2,1)S(1)} %add_convert_fusion.16), channel_id=1, source_target_pairs={{0,12},{1,13},{2,14},{3,15},{4,8},{5,9},{6,10},{7,11},{8,4},{9,5},... | collective-permute-start | bytes 1179656 | tf_op jit(solution)/shard_map/ppermute | solution.py:297
  567.9 4.5 collective-permute-start.29
  568.1 8.1 %collective-permute-start.34 = (bf16[1,40,1024]{2,1,0:T(8,128)(2,1)S(1)}, bf16[1,40,1024]{2,1,0:T(8,128)(2,1)S(1)}, u32[]{:S(2)}, u32[]{:S(2)}) collective-permute-start(bf16[1,40,1024]{2,1,0:T(8,128)(2,1)S(1)} %fusion.29), channel_id=1, source_target_pairs={{0,12},{1,13},{2,14},{3,15},{4,8},{5,9},{6,10},{7,11},{8,4},{9,5},... | collective-permute-start | bytes 245768 | tf_op jit(solution)/shard_map/ppermute | solution.py:297
  569.9 6.1 %collective-permute-start.23 = (bf16[2,48,1024]{2,1,0:T(8,128)(2,1)S(1)}, bf16[2,48,1024]{2,1,0:T(8,128)(2,1)S(1)}, u32[]{:S(2)}, u32[]{:S(2)}) collective-permute-start(bf16[2,48,1024]{2,1,0:T(8,128)(2,1)S(1)} %fusion.11), channel_id=1, source_target_pairs={{0,16},{1,17},{2,18},{3,19},{4,20},{5,21},{6,22},{7,23},{8,24},{9,... | collective-permute-start | bytes 589832 | tf_op jit(solution)/shard_map/ppermute | solution.py:297
  576.1 3.8 collective-permute-start.24
  576.2 17.6 %copy-start.1 = (bf16[256,1024]{1,0:T(8,128)(2,1)S(1)}, bf16[256,1024]{1,0:T(8,128)(2,1)}, u32[]{:S(2)}) copy-start(bf16[256,1024]{1,0:T(8,128)(2,1)} %param.9) | copy-start | bytes 1572868
  (11 other events, 41.8 us)
Sparse Core Ops, SparseCore 0:
  11.6 110.0 all-gather.2
  124.6 107.1 all-gather.4

commit v3 on v1

v3 whole, which is shorter than its diff:
```python
import functools
import jax
import jax.numpy as jnp
from jax import lax
from jax.experimental import pallas as pl
from jax.experimental.pallas import tpu as pltpu
from jax.sharding import PartitionSpec as P

F32 = jnp.float32
BF16 = jnp.bfloat16
SIDE = 4
OWN_STEP = 4
VMEM_LIMIT = 60 * 1024 * 1024
ROW_CUTS = (0, 48, 88, 128)
AXIS_ORDERS = ((2, 1, 0), (1, 0, 2), (0, 2, 1))


def split3(val):
    one = val.astype(BF16)
    rest = val - one.astype(F32)
    two = rest.astype(BF16)
    rest = rest - two.astype(F32)
    return one, two, rest.astype(BF16)


def dot_nn(lhs, rhs):
    return lax.dot_general(lhs, rhs, (((1,), (0,)), ((), ())), preferred_element_type=F32)


def dot_nt(lhs, rhs):
    return lax.dot_general(lhs, rhs, (((1,), (1,)), ((), ())), preferred_element_type=F32)


def xor_field(val, other):
    return (val // 2 + other // 2) % 2 * 2 + (val % 2 + other % 2) % 2


def table_block(step):
    me = lax.axis_index('table')
    return xor_field(step // 4, me // 16) * 4 + xor_field(step % 4, (me // 4) % 4)


def gate_kernel(n_own, pick_ref, gate_ref, out_ref, tile_ref):
    sel = pick_ref.shape[1]
    iota_own = lax.broadcasted_iota(jnp.int32, (n_own, sel), 0)
    iota_lo = lax.broadcasted_iota(jnp.int32, (128, sel), 0)

    def body(grp, carry):
        base = pl.multiple_of(grp * 8, 8)
        pick = pick_ref[pl.ds(base, 8), :]
        hi = pick >> 7
        lo = pick & 127
        parts = [piece.astype(F32) for piece in split3(gate_ref[pl.ds(base, 8), :])]
        for j in range(8):
            mask = iota_own == hi[j:j + 1, :]
            left = jnp.concatenate([jnp.where(mask, piece[j:j + 1, :], 0.0).astype(BF16) for piece in parts], axis=0)
            right = jnp.where(iota_lo == lo[j:j + 1, :], 1.0, 0.0).astype(BF16)
            res = dot_nt(left, right)
            tile_ref[j * n_own:(j + 1) * n_own, :] = res[:n_own] + res[n_own:2 * n_own] + res[2 * n_own:]
        for o in range(n_own):
            out_ref[pl.ds(base, 8), o * 128:(o + 1) * 128] = tile_ref[pl.ds(o, 8, stride=n_own), :]
        return carry

    lax.fori_loop(0, pick_ref.shape[0] // 8, body, 0)


def gate_matrix(pick_rel, gate, n_own):
    tok, sel = pick_rel.shape
    blk = max(8, tok // 4)
    return pl.pallas_call(
        functools.partial(gate_kernel, n_own),
        grid=(tok // blk,),
        in_specs=[pl.BlockSpec((blk, sel), lambda i: (i, 0)), pl.BlockSpec((blk, sel), lambda i: (i, 0))],
        out_specs=pl.BlockSpec((blk, n_own * 128), lambda i: (i, 0)),
        out_shape=jax.ShapeDtypeStruct((tok, n_own * 128), F32),
        scratch_shapes=[pltpu.VMEM((8 * n_own, 128), F32)],
        compiler_params=pltpu.CompilerParams(vmem_limit_bytes=VMEM_LIMIT),
        cost_estimate=pl.CostEstimate(flops=2 * tok * 256 * 256 * 192, bytes_accessed=tok * n_own * 512, transcendentals=0),
        name="gate_matrix",
    )(pick_rel, gate)


def select_rows(tab_ref, idsb_ref, sel_ref):
    n_rows = tab_ref.shape[0] // OWN_STEP
    iota = lax.broadcasted_iota(jnp.int32, (128, 128), 1)
    my_x = lax.axis_index('table') % 4
    for j in range(OWN_STEP):
        ids = idsb_ref[j * 128:(j + 1) * 128, :]
        hot = jnp.concatenate([jnp.where(ids == iota + 128 * h, 1.0, 0.0).astype(BF16) for h in range(n_rows // 128)], axis=1)
        start = pl.multiple_of(xor_field(j, my_x) * n_rows, n_rows)
        sel_ref[j * 128:(j + 1) * 128, :] = dot_nn(hot, tab_ref[pl.ds(start, n_rows), :]).astype(BF16)


def place_rows(blk, grad_t, ids_ref, keep_ref, send_ref):
    iota = lax.broadcasted_iota(jnp.int32, (256, 128), 0)
    grad_b = grad_t.astype(BF16)
    for j in range(OWN_STEP):
        hot = jnp.where(iota == ids_ref[pl.ds(blk * OWN_STEP + j, 1), :], 1.0, 0.0).astype(BF16)
        rows = dot_nt(hot, grad_b[:, j * 128:(j + 1) * 128]).astype(BF16)
        keep_ref[j * 128:(j + 1) * 128, :] = rows[:128]
        send_ref[j * 128:(j + 1) * 128, :] = rows[128:]


def first_kernel(tok_ref, dyt_ref, tab_ref, idsb_ref, ids_ref, gate_ref, w_ref, slope_ref, sel_ref, keep_ref, send_ref):
    select_rows(tab_ref, idsb_ref, sel_ref)
    pre = dot_nt(tok_ref[...], sel_ref[...])
    gate = gate_ref[...]
    cdf = 0.5 * (1.0 + lax.erf(pre * 0.7071067811865476))
    pdf = jnp.exp(-0.5 * pre * pre) * 0.3989422804014327
    live = gate != 0.0
    w = jnp.where(live, gate * (pre * cdf), 0.0)
    w_ref[...] = w
    slope_ref[...] = jnp.where(live, gate * (cdf + pre * pdf), 0.0)
    one, two, three = split3(w)
    dyt = dyt_ref[...]
    grad_t = dot_nn(dyt, one) + dot_nn(dyt, two) + dot_nn(dyt, three)
    place_rows(pl.program_id(0), grad_t, ids_ref, keep_ref, send_ref)


def first_pass(tok, dyt, table, idsb, ids_flip, gate):
    n_tok, width = tok.shape
    n_list = gate.shape[1]
    cols = OWN_STEP * 128
    steps = n_list // cols
    trows = table.shape[0] // steps
    row_blk = pl.BlockSpec((cols, width), lambda i: (i, 0))
    mat_blk = pl.BlockSpec((n_tok, cols), lambda i: (0, i))
    return pl.pallas_call(
        first_kernel,
        grid=(steps,),
        in_specs=[
            pl.BlockSpec((n_tok, width), lambda i: (0, 0)),
            pl.BlockSpec((width, n_tok), lambda i: (0, 0)),
            pl.BlockSpec((trows, width), lambda i: (table_block(i), 0)),
            pl.BlockSpec((cols, 128), lambda i: (i, 0)),
            pl.BlockSpec(ids_flip.shape, lambda i: (0, 0)),
            mat_blk,
        ],
        out_specs=[mat_blk, mat_blk, row_blk, row_blk, row_blk],
        out_shape=[
            jax.ShapeDtypeStruct((n_tok, n_list), F32),
            jax.ShapeDtypeStruct((n_tok, n_list), F32),
            jax.ShapeDtypeStruct((n_list, width), BF16),
            jax.ShapeDtypeStruct((n_list, width), BF16),
            jax.ShapeDtypeStruct((n_list, width), BF16),
        ],
        compiler_params=pltpu.CompilerParams(vmem_limit_bytes=VMEM_LIMIT),
        cost_estimate=pl.CostEstimate(flops=11 * n_tok * n_list * width, bytes_accessed=n_list * (width * 10 + n_tok * 12), transcendentals=0),
        name="first_pass",
    )(tok, dyt, table, idsb, ids_flip, gate)


class Reducer:
    N_COPIES = 9

    @staticmethod
    def scratch(width):
        shapes = []
        for k in range(3):
            rows = ROW_CUTS[k + 1] - ROW_CUTS[k]
            lead = [(2, SIDE, SIDE), (2, SIDE, SIDE), (SIDE, SIDE), (2, SIDE), (SIDE,), (2,), (1,)]
            shapes += [pltpu.VMEM(dims + (rows, width), BF16) for dims in lead]
        return shapes + [pltpu.SemaphoreType.DMA((27,)), pltpu.SemaphoreType.DMA((27,)), pltpu.SemaphoreType.DMA((6,))]

    def __init__(self, src, out, scratch):
        self.src, self.out = src, out
        self.bufs = [scratch[7 * k:7 * k + 7] for k in range(3)]
        self.send_sem, self.recv_sem, self.load_sem = scratch[21:]
        core = lax.axis_index('data')
        self.core = core
        self.near, self.far = 1 + 2 * core, 3 - 2 * core

    def partner(self, axis, first):
        me = lax.axis_index('table')
        stride = SIDE ** (2 - axis)
        pos = (me // stride) % SIDE
        even, odd = pos + 1 - 2 * (pos % 2), 3 - pos
        new = even + self.core * (odd - even) if first else odd + self.core * (even - odd)
        return me + (new - pos) * stride

    def remote(self, k, num, src, dst, axis, first):
        at = k * self.N_COPIES + num
        return pltpu.make_async_remote_copy(src_ref=src, dst_ref=dst, send_sem=self.send_sem.at[at], recv_sem=self.recv_sem.at[at], device_id={'table': self.partner(axis, first)}, device_id_type=pl.DeviceIdType.MESH)

    def slab(self, k, slot):
        idx = [slice(None)] * 3
        idx[AXIS_ORDERS[k][0]] = slot
        return self.src.at[idx[0], idx[1], idx[2], pl.ds(ROW_CUTS[k], ROW_CUTS[k + 1] - ROW_CUTS[k])]

    def order(self, k, b, c):
        return (b, c) if AXIS_ORDERS[k][1] < AXIS_ORDERS[k][2] else (c, b)

    def loads(self):
        return [pltpu.make_async_copy(self.slab(k, slot), self.bufs[k][0].at[j], self.load_sem.at[2 * k + j]) for k in range(3) for j, slot in enumerate((0, self.far))]

    def copies(self, stage):
        out = []
        for k in range(3):
            a, b, c = AXIS_ORDERS[k]
            held, got1, got2, got3, got4, got5, got6 = self.bufs[k]
            if stage == 1:
                out += [self.remote(k, j, self.slab(k, slot), got1.at[j], a, True) for j, slot in enumerate((self.near, 2))]
            elif stage == 2:
                out.append(self.remote(k, 2, held.at[1], got2, a, False))
            elif stage == 3:
                out += [self.remote(k, 3 + j, self.row_of(k, held, slot), got3.at[j], b, True) for j, slot in enumerate((self.near, 2))]
            elif stage == 4:
                out.append(self.remote(k, 5, self.row_of(k, held, self.far), got4, b, False))
            elif stage == 5:
                out += [self.remote(k, 6 + j, held.at[(0,) + self.order(k, 0, slot)], got5.at[j], c, True) for j, slot in enumerate((self.near, 2))]
            else:
                out.append(self.remote(k, 8, held.at[(0,) + self.order(k, 0, self.far)], got6.at[0], c, False))
        return out

    def row_of(self, k, held, slot):
        p, q = self.order(k, slot, slice(None))
        return held.at[0, p, q]

    def terms(self, k, b, c, depth):
        held, got1, got2, got3, got4, got5, got6 = self.bufs[k]
        p, q = self.order(k, b, c)
        arrs = [held[0, p, q], got1[0, p, q], got2[p, q]]
        return p, q, arrs

    def total(self, arrs):
        return functools.reduce(jnp.add, [arr.astype(F32) for arr in arrs])

    def add(self, stage):
        for k in range(3):
            held, got1, got2, got3, got4, got5, got6 = self.bufs[k]
            if stage == 2:
                def body(i, carry):
                    p, q = i // SIDE, i % SIDE
                    held[1, p, q] = self.total([held[1, p, q], got1[1, p, q]]).astype(BF16)
                    return carry
                lax.fori_loop(0, SIDE * SIDE, body, 0)
            elif stage == 3:
                def body(i, carry):
                    j = i // SIDE
                    p, q, arrs = self.terms(k, self.near + j * (2 - self.near), i % SIDE, 3)
                    held[0, p, q] = self.total(arrs).astype(BF16)
                    return carry
                lax.fori_loop(0, 2 * SIDE, body, 0)
            elif stage == 4:
                def body(c, carry):
                    p, q, arrs = self.terms(k, self.far, c, 4)
                    held[0, p, q] = self.total(arrs + [got3[1, c]]).astype(BF16)
                    return carry
                lax.fori_loop(0, SIDE, body, 0)
            elif stage == 5:
                for slot in (self.near, 2):
                    p, q, arrs = self.terms(k, 0, slot, 5)
                    held[0, p, q] = self.total(arrs + [got3[0, slot], got4[slot]]).astype(BF16)
            elif stage == 6:
                p, q, arrs = self.terms(k, 0, self.far, 6)
                held[0, p, q] = self.total(arrs + [got3[0, self.far], got4[self.far], got5[1]]).astype(BF16)
            else:
                p, q, arrs = self.terms(k, 0, 0, 7)
                self.out[ROW_CUTS[k]:ROW_CUTS[k + 1], :] = self.total(arrs + [got3[0, 0], got4[0], got5[0], got6[0]]).astype(self.out.dtype)

    def run(self, stage):
        if stage == 1:
            for copy in self.loads():
                copy.start()
        else:
            if stage == 2:
                for copy in self.loads():
                    copy.wait()
            for copy in self.copies(stage - 1):
                copy.wait_recv()
            self.add(stage)
        if stage < 7:
            for copy in self.copies(stage):
                copy.start()
        else:
            for done in range(1, 7):
                for copy in self.copies(done):
                    copy.wait_send()


def run_stages(reducer, step, last, marks):
    for stage, mark in marks:
        if last is None and mark is not None:
            pl.when(step == mark)(functools.partial(reducer.run, stage))
    if last is not None:
        @pl.when(step == last)
        def _():
            for stage, mark in marks:
                if mark is None:
                    reducer.run(stage)


SECOND_MARKS = ((1, 0), (2, 9), (3, 14), (4, None), (5, None), (6, None), (7, None))
OUT_MARKS = ((1, 0), (2, None), (3, None), (4, None), (5, None), (6, None), (7, None))


def second_kernel(dy_ref, tokt_ref, tab_ref, idsb_ref, ids_ref, slope_ref, part_ref, c_ref, sel_ref, keep_ref, send_ref, red_ref, *scratch):
    step = pl.program_id(0)
    reducer = Reducer(part_ref, red_ref, scratch)
    run_stages(reducer, step, None, SECOND_MARKS)
    select_rows(tab_ref, idsb_ref, sel_ref)
    back = dot_nt(dy_ref[...], sel_ref[...])
    slope = slope_ref[...]
    c = jnp.where(slope != 0.0, slope * back, 0.0)
    c_ref[...] = c
    one, two, three = split3(c)
    tokt = tokt_ref[...]
    grad_t = dot_nn(tokt, one) + dot_nn(tokt, two) + dot_nn(tokt, three)
    place_rows(step, grad_t, ids_ref, keep_ref, send_ref)
    run_stages(reducer, step, pl.num_programs(0) - 1, SECOND_MARKS)


def second_pass(dy, tokt, table, idsb, ids_flip, slope, part):
    n_tok, width = dy.shape
    n_list = slope.shape[1]
    cols = OWN_STEP * 128
    steps = n_list // cols
    trows = table.shape[0] // steps
    row_blk = pl.BlockSpec((cols, width), lambda i: (i, 0))
    mat_blk = pl.BlockSpec((n_tok, cols), lambda i: (0, i))
    return pl.pallas_call(
        second_kernel,
        grid=(steps,),
        in_specs=[
            pl.BlockSpec((n_tok, width), lambda i: (0, 0)),
            pl.BlockSpec((width, n_tok), lambda i: (0, 0)),
            pl.BlockSpec((trows, width), lambda i: (table_block(i), 0)),
            pl.BlockSpec((cols, 128), lambda i: (i, 0)),
            pl.BlockSpec(ids_flip.shape, lambda i: (0, 0)),
            mat_blk,
            pl.BlockSpec(memory_space=pl.ANY),
        ],
        out_specs=[mat_blk, row_blk, row_blk, row_blk, pl.BlockSpec((128, width), lambda i: (0, 0))],
        out_shape=[
            jax.ShapeDtypeStruct((n_tok, n_list), F32),
            jax.ShapeDtypeStruct((n_list, width), BF16),
            jax.ShapeDtypeStruct((n_list, width), BF16),
            jax.ShapeDtypeStruct((n_list, width), BF16),
            jax.ShapeDtypeStruct((128, width), BF16),
        ],
        scratch_shapes=Reducer.scratch(width),
        compiler_params=pltpu.CompilerParams(vmem_limit_bytes=VMEM_LIMIT, has_side_effects=True),
        cost_estimate=pl.CostEstimate(flops=11 * n_tok * n_list * width, bytes_accessed=n_list * (width * 10 + n_tok * 8), transcendentals=0),
        name="second_pass",
    )(dy, tokt, table, idsb, ids_flip, slope, part)


def out_step(mat_ref, row_ref, out_ref, acc_ref):
    step = pl.program_id(0)
    one, two, three = split3(mat_ref[...])
    rows = row_ref[...]
    part = dot_nn(one, rows) + dot_nn(two, rows) + dot_nn(three, rows)

    @pl.when(step == 0)
    def _():
        acc_ref[...] = part

    @pl.when(step > 0)
    def _():
        acc_ref[...] += part

    @pl.when(step == pl.num_programs(0) - 1)
    def _():
        out_ref[...] = acc_ref[...].astype(out_ref.dtype)


def out_reduce_step(mat_ref, row_ref, part_ref, out_ref, red_ref, acc_ref, *scratch):
    step = pl.program_id(0)
    reducer = Reducer(part_ref, red_ref, scratch)
    run_stages(reducer, step, None, OUT_MARKS)
    out_step(mat_ref, row_ref, out_ref, acc_ref)
    run_stages(reducer, step, pl.num_programs(0) - 1, OUT_MARKS)


def out_pass(mat, rows, part=None):
    n_tok, n_list = mat.shape
    width = rows.shape[1]
    cols = 1024
    extra = part is not None
    return pl.pallas_call(
        out_reduce_step if extra else out_step,
        grid=(n_list // cols,),
        in_specs=[pl.BlockSpec((n_tok, cols), lambda i: (0, i)), pl.BlockSpec((cols, width), lambda i: (i, 0))] + [pl.BlockSpec(memory_space=pl.ANY)] * extra,
        out_specs=[pl.BlockSpec((n_tok, width), lambda i: (0, 0))] + [pl.BlockSpec((128, width), lambda i: (0, 0))] * extra,
        out_shape=[jax.ShapeDtypeStruct((n_tok, width), BF16)] + [jax.ShapeDtypeStruct((128, width), BF16)] * extra,
        scratch_shapes=[pltpu.VMEM((n_tok, width), F32)] + (Reducer.scratch(width) if extra else []),
        compiler_params=pltpu.CompilerParams(vmem_limit_bytes=VMEM_LIMIT, has_side_effects=extra),
        cost_estimate=pl.CostEstimate(flops=6 * n_tok * n_list * width, bytes_accessed=n_list * (width * 2 + n_tok * 4), transcendentals=0),
        name="out_reduce" if extra else "out_pass",
    )(mat, rows, *([part] if extra else []))


def solution(mesh):
    table_n = mesh.shape['table']
    tok_spec = P(('replica', 'data', 'table'))
    row_spec = P(('replica', 'table'))

    def device_step(tok, dy, u_loc, v_loc, wanted, pick, gate):
        n_local, width = u_loc.shape
        half = n_local // 2
        n_tok = tok.shape[0]
        core = lax.axis_index('data')
        me = lax.axis_index('table')
        own_rows = lambda arr: lax.dynamic_slice_in_dim(arr, core * half, half, 0)
        full_u = lax.all_gather(own_rows(u_loc), ('table', 'data'), axis=0, tiled=True)
        full_v = lax.all_gather(own_rows(v_loc), ('table', 'data'), axis=0, tiled=True)

        owners = jnp.arange(table_n, dtype=jnp.int32) ^ me
        ids = jnp.take(wanted.reshape(table_n, -1), owners, axis=0, mode='clip') - owners[:, None] * n_local
        ids_flip = ids ^ (core * half)
        idsb = jnp.broadcast_to(ids.reshape(-1, 1), (ids.size, 128))
        pick_rel = pick.reshape(n_tok, -1) ^ (me << 7)
        gates = gate_matrix(pick_rel, gate.reshape(n_tok, -1), table_n)

        swap = [(i, (i + table_n) % (2 * table_n)) for i in range(2 * table_n)]
        cube = (SIDE, SIDE, SIDE, half, width)

        def pair_sum(keep, send):
            got = lax.ppermute(send, ('data', 'table'), swap)
            return (keep.astype(F32) + got.astype(F32)).astype(BF16).reshape(cube)

        both_cores = lambda rows: lax.all_gather(rows, 'data', axis=0, tiled=True)
        w, slope, u_sel, keep_v, send_v = first_pass(tok, dy.T, full_u, idsb, ids_flip, gates)
        c, v_sel, keep_u, send_u, red_v = second_pass(dy, tok.T, full_v, idsb, ids_flip, slope, pair_sum(keep_v, send_v))
        grad_v = both_cores(red_v)
        part_u = pair_sum(keep_u, send_u)
        y, = out_pass(w, v_sel)
        part_u, y = lax.optimization_barrier((part_u, y))
        dx, red_u = out_pass(c, u_sel, part_u)
        grad_u = both_cores(red_u)
        return y, dx, grad_u, grad_v

    return jax.shard_map(device_step, mesh=mesh, in_specs=(tok_spec, tok_spec, row_spec, row_spec, tok_spec, tok_spec, tok_spec), out_specs=(tok_spec, tok_spec, row_spec, row_spec), check_vma=False)
```

time: 646 us -> 552 us (0.85)
  waiting for transfers between devices: 164 us -> 112 us
  other arithmetic: 90.9 us -> 42 us
  Pallas kernels: 275 us -> 323 us
  starting transfers between devices: 36.1 us -> 7.14 us
  local copies, waits for them, and re-layouts: 46.5 us -> 19.8 us
  blocking collectives: 12.9 us -> 34.1 us
    add x12 -> x0, other arithmetic: 58.8 us -> none  [the longest x4 48.3 us: halve_rows(): val = keep[:, :, :, cut].astype(F32) + got0[:, :, :, cut].astype(F32)]
    pallas_call x13 -> x4, Pallas kernels: 246 us -> 294 us  [the longest x2 127 us: out_pass(): pl.pallas_call(out_reduce_step if extra else out_step, grid=(n_list // co...]
    all_gather x1, waiting for transfers between devices: 37.4 us -> 0.01 us  [device_step(): lax.all_gather(own_rows(v_loc), ('table', 'data'), axis=0, tiled=True)]
    ppermute x38 -> x2, starting transfers between devices: 36 us -> 7.06 us  [pair_sum(): got = lax.ppermute(send, ('data', 'table'), swap)]
    slice x10 -> x0, local copies, waits for them, and re-layouts: 27 us -> none  [halve_rows(): take = lambda arr, lo, hi: lax.slice_in_dim(arr, lo, hi, axis=dim)]
    convert_element_type x18 -> x2, other arithmetic: 17.4 us -> 40.4 us  [pair_sum(): return (keep.astype(F32) + got.astype(F32)).astype(BF16).reshape(cube)]
    all_gather x2, blocking collectives: 12.9 us -> 34.1 us  [device_step(): both_cores = lambda rows: lax.all_gather(rows, 'data', axis=0, tiled=True)]
    ppermute x38 -> x2, waiting for transfers between devices: 53.2 us -> 37.7 us  [pair_sum(): got = lax.ppermute(send, ('data', 'table'), swap)]
  transfers between devices with their start and end apart: 40 -> 4, of which waited for: 16 -> 2; matrix products, arithmetic and copies ran while one was open for 20% -> 7% of each run, Pallas kernels for 43% -> 24%
where the time goes in v3:
time: 552 us
  Pallas kernels  323 us (59%)
  waiting for transfers between devices  112 us (20%)
  other arithmetic  42 us (8%)
  blocking collectives  34.1 us (6%)
  local copies, waits for them, and re-layouts  19.8 us (4%)
  between operations  14.1 us (3%)
  starting transfers between devices  7.14 us (1%)
    pallas_call x2, Pallas kernels, out_pass(): pl.pallas_call(out_reduce_step if extra else out_step, grid=(n_list // co...  127 us
    pallas_call x1, Pallas kernels, second_pass(): pl.pallas_call(second_kernel, grid=(steps,), in_specs=[pl.BlockSpec((n_to...  98.2 us
    all_gather x1, waiting for transfers between devices, device_step(): lax.all_gather(own_rows(u_loc), ('table', 'data'), axis=0, tiled=True)  73.9 us
    pallas_call x1, Pallas kernels, first_pass(): pl.pallas_call(first_kernel, grid=(steps,), in_specs=[pl.BlockSpec((n_tok...  68.3 us
    convert_element_type x2, other arithmetic, pair_sum(): return (keep.astype(F32) + got.astype(F32)).astype(BF16).reshape(cube)  40.4 us
    ppermute x2, waiting for transfers between devices, pair_sum(): got = lax.ppermute(send, ('data', 'table'), swap)  37.7 us
    all_gather x2, blocking collectives, device_step(): both_cores = lambda rows: lax.all_gather(rows, 'data', axis=0, tiled=True)  34.1 us
    pallas_call x1, Pallas kernels, gate_matrix(): pl.pallas_call(functools.partial(gate_kernel, n_own), grid=(tok // blk,),...  29.3 us
  transfers between devices with their start and end apart: 4, of which 2 were waited for; matrix products, arithmetic and copies ran while one was open for 7% of the time, Pallas kernels for 24%

profile of v3, /device:TPU:1, one launch (start us, length us, event | category | flops | bytes accessed | tf_op | source)
XLA Modules:
  0.0 551.7 jit_solution(13651011375473852684)
XLA Ops:
  7.2 0.0 copy-start
  7.2 0.0 all-gather.5.cloned.1.call-start
  7.2 1.0 copy-done
  8.2 0.7 constant_dynamic-slice_fusion
  8.9 0.0 all-gather.5.cloned.1.call-update
  9.0 0.0 all-gather.3.cloned.1.call-start
  9.0 1.7 constant_dynamic-slice_fusion.1
  10.7 0.0 all-gather.3.cloned.1.call-update
  10.7 1.0 broadcast_xor_fusion
  11.7 0.8 copy.17.pick_ref
  12.5 1.8 copy.18.gate_ref
  14.3 2.3 copy.16
  16.6 1.4 gather_fusion
  18.0 0.7 subtract_xor_fusion
  18.6 29.3 %gate_matrix.1.gate_ref = f32[512,8192]{1,0:T(8,128)} custom-call(s32[512,128]{1,0:T(8,128)} %copy.17.pick_ref, f32[512,128]{1,0:T(8,128)} %copy.18.gate_ref), custom_call_target="tpu_custom_call" | custom-call | flops 12884901888 | bytes 16777216 | tf_op jit(solution)/shard_map/gate_matrix/pallas_call | solution.py:70
  47.9 73.9 %all-gather.5.cloned.1.call-done.tab_ref = bf16[16384,1024]{1,0:T(8,128)(2,1)} async-done(((bf16[128,1024]{1,0:T(8,128)(2,1)}), bf16[16384,1024]{1,0:T(8,128)(2,1)}) %all-gather.5.cloned.1.call-update) | async-done | bytes 33554448 | tf_op jit(solution)/shard_map/all_gather | solution.py:405
  121.8 5.0 broadcast_in_dim.4.idsb_ref
  126.8 0.0 copy-start.2
  126.8 68.3 %first_pass.1 = (f32[512,8192]{1,0:T(8,128)}, f32[512,8192]{1,0:T(8,128)}, bf16[8192,1024]{1,0:T(8,128)(2,1)}, bf16[8192,1024]{1,0:T(8,128)(2,1)}, bf16[8192,1024]{1,0:T(8,128)(2,1)}) custom-call(bf16[512,1024]{1,0:T(8,128)(2,1)} %tok_ref.1, bf16[1024,512]{1,0:T(8,128)(2,1)} %bitcast.15, bf16[16384,1024]{1,0:T(8,128)(2,1)} %all-gather.5.cloned.1.call-done.tab_ref, ...), custom_call_target="tpu_custom_call" | custom-call | flops 47244640256 | bytes 134217728 | tf_op jit(solution)/shard_map/first_pass/pallas_call | solution.py:128
  195.1 0.3 collective-permute-start
  195.3 0.0 copy-done.2
  195.3 1.3 copy.15
  196.6 37.7 %collective-permute-done = bf16[8192,1024]{1,0:T(8,128)(2,1)} collective-permute-done((bf16[8192,1024]{1,0:T(8,128)(2,1)}, bf16[8192,1024]{1,0:T(8,128)(2,1)}, u32[]{:S(2)}, u32[]{:S(2)}) %collective-permute-start) | collective-permute-done | bytes 16777248 | tf_op jit(solution)/shard_map/ppermute | solution.py:419
  234.4 20.2 %add_convert_fusion.1 = bf16[8192,1024]{1,0:T(8,128)(2,1)} fusion(bf16[8192,1024]{1,0:T(8,128)(2,1)} %collective-permute-done, bf16[8192,1024]{1,0:T(8,128)(2,1)} %get-tuple-element.19), kind=kLoop, calls=%fused_computation.2 | loop fusion | flops 33554432 | bytes 50331648 | tf_op jit(solution)/shard_map/convert_element_type | solution.py:420
  254.6 0.0 all-gather.3.cloned.1.call-done.tab_ref
  254.6 98.2 %second_pass.1 = (f32[512,8192]{1,0:T(8,128)}, bf16[8192,1024]{1,0:T(8,128)(2,1)}, bf16[8192,1024]{1,0:T(8,128)(2,1)}, bf16[8192,1024]{1,0:T(8,128)(2,1)}, bf16[128,1024]{1,0:T(8,128)(2,1)}) custom-call(bf16[512,1024]{1,0:T(8,128)(2,1)} %dy_ref.1, bf16[1024,512]{1,0:T(8,128)(2,1)} %bitcast.16, bf16[16384,1024]{1,0:T(8,128)(2,1)} %all-gather.3.cloned.1.call-done.tab_ref, ...), custom_call_target="tpu_custom_call" | custom-call | flops 47244640256 | bytes 117440512 | tf_op jit(solution)/shard_map/second_pass/pallas_call | solution.py:321
  352.8 6.8 %collective-permute-start.1 = (bf16[8192,1024]{1,0:T(8,128)(2,1)}, bf16[8192,1024]{1,0:T(8,128)(2,1)}, u32[]{:S(2)}, u32[]{:S(2)}) collective-permute-start(bf16[8192,1024]{1,0:T(8,128)(2,1)} %get-tuple-element.22), channel_id=1, source_target_pairs={{0,64},{1,65},{2,66},{3,67},{4,68},{5,69},{6,70},{7,71},{8,72},{9,... | collective-permute-start | bytes 50331656 | tf_op jit(solution)/shard_map/ppermute | solution.py:419
  359.6 25.2 %all_gather.15 = bf16[256,1024]{1,0:T(8,128)(2,1)S(1)} all-gather(bf16[128,1024]{1,0:T(8,128)(2,1)} %get-tuple-element.31), channel_id=1, replica_groups=mesh['replica'=1,'data'=2,'table'=64] {'data'}, dimensions={0}, use_global_device_ids=true | all-gather | bytes 786432 | tf_op jit(solution)/shard_map/all_gather | solution.py:422
  384.8 32.3 %out_pass.1 = bf16[512,1024]{1,0:T(8,128)(2,1)} custom-call(f32[512,8192]{1,0:T(8,128)} %get-tuple-element.23.mat_ref, bf16[8192,1024]{1,0:T(8,128)(2,1)} %get-tuple-element.24.row_ref), custom_call_target="tpu_custom_call" | custom-call | flops 25769803776 | bytes 33554432 | tf_op jit(solution)/shard_map/out_pass/pallas_call | solution.py:380
  417.1 0.0 collective-permute-done.1
  417.1 20.2 %add_convert_fusion = bf16[8192,1024]{1,0:T(8,128)(2,1)} fusion(bf16[8192,1024]{1,0:T(8,128)(2,1)} %collective-permute-done.1, bf16[8192,1024]{1,0:T(8,128)(2,1)} %get-tuple-element.21), kind=kLoop, calls=%fused_computation.1 | loop fusion | flops 33554432 | bytes 50331648 | tf_op jit(solution)/shard_map/convert_element_type | solution.py:420
  437.2 0.0 copy-start.1
  437.2 94.9 %out_reduce.1 = (bf16[512,1024]{1,0:T(8,128)(2,1)}, bf16[128,1024]{1,0:T(8,128)(2,1)}) custom-call(f32[512,8192]{1,0:T(8,128)} %get-tuple-element.26.mat_ref, bf16[8192,1024]{1,0:T(8,128)(2,1)} %get-tuple-element.27.row_ref, bf16[4,4,4,128,1024]{4,3,2,1,0:T(8,128)(2,1)} %bitcast.12), custom_call_target="tpu_custom_call" | custom-call | flops 25769803776 | bytes 33554432 | tf_op jit(solution)/shard_map/out_reduce/pallas_call | solution.py:380
  532.1 9.0 %all_gather.14 = bf16[256,1024]{1,0:T(8,128)(2,1)S(1)} all-gather(bf16[128,1024]{1,0:T(8,128)(2,1)} %get-tuple-element.30), channel_id=1, replica_groups=mesh['replica'=1,'data'=2,'table'=64] {'data'}, dimensions={0}, use_global_device_ids=true | all-gather | bytes 786432 | tf_op jit(solution)/shard_map/all_gather | solution.py:422
  541.1 2.3 copy.22
  543.3 0.8 copy.23
  544.1 0.8 copy.24
  544.9 0.0 copy-done.1
  (3 shorter events, 0.0 us)
Async XLA Ops:
  7.2 1.1 copy-start
  7.2 114.6 %all-gather.5.cloned.1.call-start = ((), (), s32[]{:S(2)}) async-start(), calls=%async_computation.1 | async-start | bytes 33816576 | tf_op jit(solution)/shard_map/all_gather | solution.py:405
  9.0 245.6 %all-gather.3.cloned.1.call-start = ((), (), s32[]{:S(2)}) async-start(), calls=%async_computation | async-start | bytes 33816576 | tf_op jit(solution)/shard_map/all_gather | solution.py:406
  126.8 68.5 %copy-start.2 = (bf16[512,1024]{1,0:T(8,128)(2,1)S(1)}, bf16[512,1024]{1,0:T(8,128)(2,1)}, u32[]{:S(2)}) copy-start(bf16[512,1024]{1,0:T(8,128)(2,1)} %tok_ref.1) | copy-start | bytes 3145732
  195.1 39.3 %collective-permute-start = (bf16[8192,1024]{1,0:T(8,128)(2,1)}, bf16[8192,1024]{1,0:T(8,128)(2,1)}, u32[]{:S(2)}, u32[]{:S(2)}) collective-permute-start(bf16[8192,1024]{1,0:T(8,128)(2,1)} %get-tuple-element.20), channel_id=1, source_target_pairs={{0,64},{1,65},{2,66},{3,67},{4,68},{5,69},{6,70},{7,71},{8,72},{9,... | collective-permute-start | bytes 50331656 | tf_op jit(solution)/shard_map/ppermute | solution.py:419
  352.8 64.3 %collective-permute-start.1 = (bf16[8192,1024]{1,0:T(8,128)(2,1)}, bf16[8192,1024]{1,0:T(8,128)(2,1)}, u32[]{:S(2)}, u32[]{:S(2)}) collective-permute-start(bf16[8192,1024]{1,0:T(8,128)(2,1)} %get-tuple-element.22), channel_id=1, source_target_pairs={{0,64},{1,65},{2,66},{3,67},{4,68},{5,69},{6,70},{7,71},{8,72},{9,... | collective-permute-start | bytes 50331656 | tf_op jit(solution)/shard_map/ppermute | solution.py:419
  437.2 107.7 %copy-start.1 = (bf16[256,1024]{1,0:T(8,128)(2,1)S(1)}, bf16[256,1024]{1,0:T(8,128)(2,1)}, u32[]{:S(2)}) copy-start(bf16[256,1024]{1,0:T(8,128)(2,1)} %param.9) | copy-start | bytes 1572868
Sparse Core Ops, SparseCore 0:
  11.6 110.2 all-gather.4
  124.8 107.1 all-gather.2

commit v4 on v3

--- a/solution.py
+++ b/solution.py
@@ -11,7 +11,7 @@
 SIDE = 4
 OWN_STEP = 4
 VMEM_LIMIT = 60 * 1024 * 1024
-ROW_CUTS = (0, 48, 88, 128)
+ROW_CUTS = (0, 48, 96, 128)
 AXIS_ORDERS = ((2, 1, 0), (1, 0, 2), (0, 2, 1))
 
 
@@ -91,30 +91,150 @@
         sel_ref[j * 128:(j + 1) * 128, :] = dot_nn(hot, tab_ref[pl.ds(start, n_rows), :]).astype(BF16)
 
 
-def place_rows(blk, grad_t, ids_ref, keep_ref, send_ref):
+def place_rows(blk, grad_t, ids_ref, slot, keep_ref, send_ref):
     iota = lax.broadcasted_iota(jnp.int32, (256, 128), 0)
     grad_b = grad_t.astype(BF16)
     for j in range(OWN_STEP):
         hot = jnp.where(iota == ids_ref[pl.ds(blk * OWN_STEP + j, 1), :], 1.0, 0.0).astype(BF16)
         rows = dot_nt(hot, grad_b[:, j * 128:(j + 1) * 128]).astype(BF16)
-        keep_ref[j * 128:(j + 1) * 128, :] = rows[:128]
-        send_ref[j * 128:(j + 1) * 128, :] = rows[128:]
-
-
-def first_kernel(tok_ref, dyt_ref, tab_ref, idsb_ref, ids_ref, gate_ref, w_ref, slope_ref, sel_ref, keep_ref, send_ref):
-    select_rows(tab_ref, idsb_ref, sel_ref)
-    pre = dot_nt(tok_ref[...], sel_ref[...])
-    gate = gate_ref[...]
-    cdf = 0.5 * (1.0 + lax.erf(pre * 0.7071067811865476))
-    pdf = jnp.exp(-0.5 * pre * pre) * 0.3989422804014327
-    live = gate != 0.0
-    w = jnp.where(live, gate * (pre * cdf), 0.0)
-    w_ref[...] = w
-    slope_ref[...] = jnp.where(live, gate * (cdf + pre * pdf), 0.0)
-    one, two, three = split3(w)
-    dyt = dyt_ref[...]
-    grad_t = dot_nn(dyt, one) + dot_nn(dyt, two) + dot_nn(dyt, three)
-    place_rows(pl.program_id(0), grad_t, ids_ref, keep_ref, send_ref)
+        keep_ref[slot, j] = rows[:128]
+        send_ref[slot, j] = rows[128:]
+
+
+LAG = 3
+
+
+class Exchanger:
+    @staticmethod
+    def scratch(width):
+        blk = (2, OWN_STEP, 128, width)
+        dma = pltpu.SemaphoreType.DMA
+        return [pltpu.VMEM(blk, BF16)] * 4 + [dma((2,)), dma((2,)), dma((8,)), dma((6,))]
+
+    @staticmethod
+    def out_shapes(width):
+        rows = [ROW_CUTS[k + 1] - ROW_CUTS[k] for k in range(3)]
+        cube = jax.ShapeDtypeStruct((SIDE, SIDE, SIDE, 128, width), BF16)
+        return [cube] + [jax.ShapeDtypeStruct((2, SIDE, SIDE, n, width), BF16) for n in rows]
+
+    @staticmethod
+    def out_specs(width, blocks):
+        def place(i):
+            blk = jnp.clip(i - 2, 0, blocks - 1)
+            return blk // SIDE, blk % SIDE, 0, 0, 0
+        return [pl.BlockSpec((1, 1, SIDE, 128, width), place)] + [pl.BlockSpec(memory_space=pl.ANY)] * 3
+
+    def __init__(self, step, blocks, outs, scratch):
+        self.step, self.blocks = step, blocks
+        self.part_ref, self.first = outs[0], outs[1:]
+        self.keep, self.send, self.got, self.sum = scratch[:4]
+        self.pair_send, self.pair_recv, self.out_send, self.out_recv = scratch[4:]
+        self.ring = Ring()
+
+    def pair_copy(self, slot):
+        other = 1 - lax.axis_index('data')
+        return pltpu.make_async_remote_copy(src_ref=self.send.at[slot], dst_ref=self.got.at[slot], send_sem=self.pair_send.at[slot], recv_sem=self.pair_recv.at[slot], device_id={'data': other}, device_id_type=pl.DeviceIdType.MESH)
+
+    def first_copies(self, blk):
+        slot = blk % 2
+        spots = (blk // SIDE, blk % SIDE)
+        out = []
+        near = self.ring.near
+
+        def copy(k, num, src, dst, way):
+            return pltpu.make_async_remote_copy(src_ref=src, dst_ref=dst, send_sem=self.out_send.at[4 * slot + num], recv_sem=self.out_recv.at[2 * k + way], device_id={'table': self.ring.partner(AXIS_ORDERS[k][0], True)}, device_id_type=pl.DeviceIdType.MESH)
+
+        for k in range(3):
+            axis = AXIS_ORDERS[k][0]
+            rows = pl.ds(ROW_CUTS[k], ROW_CUTS[k + 1] - ROW_CUTS[k])
+            if axis == 2:
+                for way, x in enumerate((near, 2)):
+                    out.append((None, copy(k, way, self.sum.at[slot, x, rows], self.first[k].at[way, spots[0], spots[1]], way)))
+            else:
+                for way, mark in enumerate((near, 2)):
+                    out.append((spots[axis] == mark, copy(k, 3 - axis, self.sum.at[slot, :, rows], self.first[k].at[way, spots[1 - axis]], way)))
+        return out
+
+    def on_first(self, blk, act):
+        for cond, copy in self.first_copies(blk):
+            if cond is None:
+                act(copy)
+            else:
+                pl.when(cond)(functools.partial(act, copy))
+
+    def before(self):
+        step, blocks = self.step, self.blocks
+
+        @pl.when((step >= 4) & (step - 4 < blocks))
+        def _():
+            self.on_first(step - 4, lambda copy: copy.wait_send())
+
+        @pl.when((step >= 3) & (step - 3 < blocks))
+        def _():
+            self.on_first(step - 3, lambda copy: copy.start())
+
+        @pl.when((step >= 2) & (step - 2 < blocks))
+        def _():
+            slot = step % 2
+            copy = self.pair_copy(slot)
+            copy.wait_recv()
+            for j in range(OWN_STEP):
+                rows = (self.keep[slot, j].astype(F32) + self.got[slot, j].astype(F32)).astype(BF16)
+                self.sum[slot, j] = rows
+                self.part_ref[0, 0, j] = rows
+            copy.wait_send()
+
+        @pl.when((step >= 1) & (step - 1 < blocks))
+        def _():
+            self.pair_copy((step - 1) % 2).start()
+
+    def after(self):
+        @pl.when(self.step == self.blocks + LAG - 1)
+        def _():
+            self.on_first(self.blocks - 1, lambda copy: copy.wait_send())
+            for k in range(3):
+                for way in range(2):
+                    dst = self.first[k].at[way]
+                    pltpu.make_async_copy(dst, dst, self.out_recv.at[2 * k + way]).wait()
+
+
+class Ring:
+    def __init__(self):
+        self.core = lax.axis_index('data')
+        self.near, self.far = 1 + 2 * self.core, 3 - 2 * self.core
+
+    def partner(self, axis, first):
+        me = lax.axis_index('table')
+        stride = SIDE ** (2 - axis)
+        pos = (me // stride) % SIDE
+        even, odd = pos + 1 - 2 * (pos % 2), 3 - pos
+        new = even + self.core * (odd - even) if first else odd + self.core * (even - odd)
+        return me + (new - pos) * stride
+
+
+def first_kernel(tok_ref, dyt_ref, tab_ref, idsb_ref, ids_ref, gate_ref, w_ref, slope_ref, sel_ref, *rest):
+    step = pl.program_id(0)
+    blocks = pl.num_programs(0) - LAG
+    swap = Exchanger(step, blocks, rest[:4], rest[4:])
+    swap.before()
+
+    @pl.when(step < blocks)
+    def _():
+        select_rows(tab_ref, idsb_ref, sel_ref)
+        pre = dot_nt(tok_ref[...], sel_ref[...])
+        gate = gate_ref[...]
+        cdf = 0.5 * (1.0 + lax.erf(pre * 0.7071067811865476))
+        pdf = jnp.exp(-0.5 * pre * pre) * 0.3989422804014327
+        live = gate != 0.0
+        w = jnp.where(live, gate * (pre * cdf), 0.0)
+        w_ref[...] = w
+        slope_ref[...] = jnp.where(live, gate * (cdf + pre * pdf), 0.0)
+        one, two, three = split3(w)
+        dyt = dyt_ref[...]
+        grad_t = dot_nn(dyt, one) + dot_nn(dyt, two) + dot_nn(dyt, three)
+        place_rows(step, grad_t, ids_ref, step % 2, swap.keep, swap.send)
+
+    swap.after()
 
 
 def first_pass(tok, dyt, table, idsb, ids_flip, gate):
@@ -123,34 +243,34 @@
     cols = OWN_STEP * 128
     steps = n_list // cols
     trows = table.shape[0] // steps
-    row_blk = pl.BlockSpec((cols, width), lambda i: (i, 0))
-    mat_blk = pl.BlockSpec((n_tok, cols), lambda i: (0, i))
+    at = lambda i: jnp.minimum(i, steps - 1)
+    row_blk = pl.BlockSpec((cols, width), lambda i: (at(i), 0))
+    mat_blk = pl.BlockSpec((n_tok, cols), lambda i: (0, at(i)))
     return pl.pallas_call(
         first_kernel,
-        grid=(steps,),
+        grid=(steps + LAG,),
         in_specs=[
             pl.BlockSpec((n_tok, width), lambda i: (0, 0)),
             pl.BlockSpec((width, n_tok), lambda i: (0, 0)),
-            pl.BlockSpec((trows, width), lambda i: (table_block(i), 0)),
-            pl.BlockSpec((cols, 128), lambda i: (i, 0)),
+            pl.BlockSpec((trows, width), lambda i: (table_block(at(i)), 0)),
+            pl.BlockSpec((cols, 128), lambda i: (at(i), 0)),
             pl.BlockSpec(ids_flip.shape, lambda i: (0, 0)),
             mat_blk,
         ],
-        out_specs=[mat_blk, mat_blk, row_blk, row_blk, row_blk],
+        out_specs=[mat_blk, mat_blk, row_blk] + Exchanger.out_specs(width, steps),
         out_shape=[
             jax.ShapeDtypeStruct((n_tok, n_list), F32),
             jax.ShapeDtypeStruct((n_tok, n_list), F32),
             jax.ShapeDtypeStruct((n_list, width), BF16),
-            jax.ShapeDtypeStruct((n_list, width), BF16),
-            jax.ShapeDtypeStruct((n_list, width), BF16),
-        ],
-        compiler_params=pltpu.CompilerParams(vmem_limit_bytes=VMEM_LIMIT),
+        ] + Exchanger.out_shapes(width),
+        scratch_shapes=Exchanger.scratch(width),
+        compiler_params=pltpu.CompilerParams(vmem_limit_bytes=VMEM_LIMIT, has_side_effects=True),
         cost_estimate=pl.CostEstimate(flops=11 * n_tok * n_list * width, bytes_accessed=n_list * (width * 10 + n_tok * 12), transcendentals=0),
         name="first_pass",
     )(tok, dyt, table, idsb, ids_flip, gate)
 
 
-class Reducer:
+class Reducer(Ring):
     N_COPIES = 9
 
     @staticmethod
@@ -160,23 +280,13 @@
             rows = ROW_CUTS[k + 1] - ROW_CUTS[k]
             lead = [(2, SIDE, SIDE), (2, SIDE, SIDE), (SIDE, SIDE), (2, SIDE), (SIDE,), (2,), (1,)]
             shapes += [pltpu.VMEM(dims + (rows, width), BF16) for dims in lead]
-        return shapes + [pltpu.SemaphoreType.DMA((27,)), pltpu.SemaphoreType.DMA((27,)), pltpu.SemaphoreType.DMA((6,))]
-
-    def __init__(self, src, out, scratch):
-        self.src, self.out = src, out
+        return shapes + [pltpu.SemaphoreType.DMA((27,)), pltpu.SemaphoreType.DMA((27,)), pltpu.SemaphoreType.DMA((12,))]
+
+    def __init__(self, src, first, out, scratch):
+        super().__init__()
+        self.src, self.first, self.out = src, first, out
         self.bufs = [scratch[7 * k:7 * k + 7] for k in range(3)]
         self.send_sem, self.recv_sem, self.load_sem = scratch[21:]
-        core = lax.axis_index('data')
-        self.core = core
-        self.near, self.far = 1 + 2 * core, 3 - 2 * core
-
-    def partner(self, axis, first):
-        me = lax.axis_index('table')
-        stride = SIDE ** (2 - axis)
-        pos = (me // stride) % SIDE
-        even, odd = pos + 1 - 2 * (pos % 2), 3 - pos
-        new = even + self.core * (odd - even) if first else odd + self.core * (even - odd)
-        return me + (new - pos) * stride
 
     def remote(self, k, num, src, dst, axis, first):
         at = k * self.N_COPIES + num
@@ -191,16 +301,16 @@
         return (b, c) if AXIS_ORDERS[k][1] < AXIS_ORDERS[k][2] else (c, b)
 
     def loads(self):
-        return [pltpu.make_async_copy(self.slab(k, slot), self.bufs[k][0].at[j], self.load_sem.at[2 * k + j]) for k in range(3) for j, slot in enumerate((0, self.far))]
+        own = [pltpu.make_async_copy(self.slab(k, slot), self.bufs[k][0].at[j], self.load_sem.at[2 * k + j]) for j, slot in ((1, self.far), (0, 0)) for k in range(3)]
+        come = [pltpu.make_async_copy(self.first[k].at[j], self.bufs[k][1].at[j], self.load_sem.at[6 + 2 * k + j]) for j in (1, 0) for k in range(3)]
+        return [copy for j in range(2) for copy in own[3 * j:3 * j + 3] + come[3 * j:3 * j + 3]]
 
     def copies(self, stage):
         out = []
         for k in range(3):
             a, b, c = AXIS_ORDERS[k]
             held, got1, got2, got3, got4, got5, got6 = self.bufs[k]
-            if stage == 1:
-                out += [self.remote(k, j, self.slab(k, slot), got1.at[j], a, True) for j, slot in enumerate((self.near, 2))]
-            elif stage == 2:
+            if stage == 2:
                 out.append(self.remote(k, 2, held.at[1], got2, a, False))
             elif stage == 3:
                 out += [self.remote(k, 3 + j, self.row_of(k, held, slot), got3.at[j], b, True) for j, slot in enumerate((self.near, 2))]
@@ -262,18 +372,19 @@
         if stage == 1:
             for copy in self.loads():
                 copy.start()
+            return
+        if stage == 2:
+            for copy in self.loads():
+                copy.wait()
         else:
-            if stage == 2:
-                for copy in self.loads():
-                    copy.wait()
             for copy in self.copies(stage - 1):
                 copy.wait_recv()
-            self.add(stage)
+        self.add(stage)
         if stage < 7:
             for copy in self.copies(stage):
                 copy.start()
         else:
-            for done in range(1, 7):
+            for done in range(2, 7):
                 for copy in self.copies(done):
                     copy.wait_send()
 
@@ -290,104 +401,108 @@
                     reducer.run(stage)
 
 
-SECOND_MARKS = ((1, 0), (2, 9), (3, 14), (4, None), (5, None), (6, None), (7, None))
-OUT_MARKS = ((1, 0), (2, None), (3, None), (4, None), (5, None), (6, None), (7, None))
-
-
-def second_kernel(dy_ref, tokt_ref, tab_ref, idsb_ref, ids_ref, slope_ref, part_ref, c_ref, sel_ref, keep_ref, send_ref, red_ref, *scratch):
+SECOND_MARKS = ((1, 0), (2, 2), (3, 8), (4, 12), (5, 14), (6, 16), (7, None))
+OUT_MARKS = ((1, 0), (2, 2), (3, 8), (4, 11), (5, 13), (6, 15), (7, None))
+
+
+def second_kernel(dy_ref, tokt_ref, tab_ref, idsb_ref, ids_ref, slope_ref, part_ref, f0_ref, f1_ref, f2_ref, c_ref, sel_ref, *rest):
     step = pl.program_id(0)
-    reducer = Reducer(part_ref, red_ref, scratch)
+    blocks = pl.num_programs(0) - LAG
+    red_ref = rest[4]
+    swap = Exchanger(step, blocks, rest[:4], rest[5:13])
+    reducer = Reducer(part_ref, (f0_ref, f1_ref, f2_ref), red_ref, rest[13:])
+    swap.before()
     run_stages(reducer, step, None, SECOND_MARKS)
-    select_rows(tab_ref, idsb_ref, sel_ref)
-    back = dot_nt(dy_ref[...], sel_ref[...])
-    slope = slope_ref[...]
-    c = jnp.where(slope != 0.0, slope * back, 0.0)
-    c_ref[...] = c
-    one, two, three = split3(c)
-    tokt = tokt_ref[...]
-    grad_t = dot_nn(tokt, one) + dot_nn(tokt, two) + dot_nn(tokt, three)
-    place_rows(step, grad_t, ids_ref, keep_ref, send_ref)
+
+    @pl.when(step < blocks)
+    def _():
+        select_rows(tab_ref, idsb_ref, sel_ref)
+        back = dot_nt(dy_ref[...], sel_ref[...])
+        slope = slope_ref[...]
+        c = jnp.where(slope != 0.0, slope * back, 0.0)
+        c_ref[...] = c
+        one, two, three = split3(c)
+        tokt = tokt_ref[...]
+        grad_t = dot_nn(tokt, one) + dot_nn(tokt, two) + dot_nn(tokt, three)
+        place_rows(step, grad_t, ids_ref, step % 2, swap.keep, swap.send)
+
+    swap.after()
     run_stages(reducer, step, pl.num_programs(0) - 1, SECOND_MARKS)
 
 
-def second_pass(dy, tokt, table, idsb, ids_flip, slope, part):
+def second_pass(dy, tokt, table, idsb, ids_flip, slope, part, first):
     n_tok, width = dy.shape
     n_list = slope.shape[1]
     cols = OWN_STEP * 128
     steps = n_list // cols
     trows = table.shape[0] // steps
-    row_blk = pl.BlockSpec((cols, width), lambda i: (i, 0))
-    mat_blk = pl.BlockSpec((n_tok, cols), lambda i: (0, i))
+    at = lambda i: jnp.minimum(i, steps - 1)
+    row_blk = pl.BlockSpec((cols, width), lambda i: (at(i), 0))
+    mat_blk = pl.BlockSpec((n_tok, cols), lambda i: (0, at(i)))
     return pl.pallas_call(
         second_kernel,
-        grid=(steps,),
+        grid=(steps + LAG,),
         in_specs=[
             pl.BlockSpec((n_tok, width), lambda i: (0, 0)),
             pl.BlockSpec((width, n_tok), lambda i: (0, 0)),
-            pl.BlockSpec((trows, width), lambda i: (table_block(i), 0)),
-            pl.BlockSpec((cols, 128), lambda i: (i, 0)),
+            pl.BlockSpec((trows, width), lambda i: (table_block(at(i)), 0)),
+            pl.BlockSpec((cols, 128), lambda i: (at(i), 0)),
             pl.BlockSpec(ids_flip.shape, lambda i: (0, 0)),
             mat_blk,
-            pl.BlockSpec(memory_space=pl.ANY),
-        ],
-        out_specs=[mat_blk, row_blk, row_blk, row_blk, pl.BlockSpec((128, width), lambda i: (0, 0))],
+        ] + [pl.BlockSpec(memory_space=pl.ANY)] * 4,
+        out_specs=[mat_blk, row_blk] + Exchanger.out_specs(width, steps) + [pl.BlockSpec((128, width), lambda i: (0, 0))],
         out_shape=[
             jax.ShapeDtypeStruct((n_tok, n_list), F32),
             jax.ShapeDtypeStruct((n_list, width), BF16),
-            jax.ShapeDtypeStruct((n_list, width), BF16),
-            jax.ShapeDtypeStruct((n_list, width), BF16),
-            jax.ShapeDtypeStruct((128, width), BF16),
-        ],
-        scratch_shapes=Reducer.scratch(width),
+        ] + Exchanger.out_shapes(width) + [jax.ShapeDtypeStruct((128, width), BF16)],
+        scratch_shapes=Exchanger.scratch(width) + Reducer.scratch(width),
         compiler_params=pltpu.CompilerParams(vmem_limit_bytes=VMEM_LIMIT, has_side_effects=True),
         cost_estimate=pl.CostEstimate(flops=11 * n_tok * n_list * width, bytes_accessed=n_list * (width * 10 + n_tok * 8), transcendentals=0),
         name="second_pass",
-    )(dy, tokt, table, idsb, ids_flip, slope, part)
-
-
-def out_step(mat_ref, row_ref, out_ref, acc_ref):
+    )(dy, tokt, table, idsb, ids_flip, slope, part, *first)
+
+
+def out_kernel(w_ref, v_ref, c_ref, u_ref, part_ref, f0_ref, f1_ref, f2_ref, y_ref, dx_ref, red_ref, y_acc, dx_acc, *scratch):
     step = pl.program_id(0)
-    one, two, three = split3(mat_ref[...])
-    rows = row_ref[...]
-    part = dot_nn(one, rows) + dot_nn(two, rows) + dot_nn(three, rows)
+    reducer = Reducer(part_ref, (f0_ref, f1_ref, f2_ref), red_ref, scratch)
+    run_stages(reducer, step, None, OUT_MARKS)
 
     @pl.when(step == 0)
     def _():
-        acc_ref[...] = part
-
-    @pl.when(step > 0)
-    def _():
-        acc_ref[...] += part
+        y_acc[...] = jnp.zeros_like(y_acc)
+        dx_acc[...] = jnp.zeros_like(dx_acc)
+
+    for mat_ref, row_ref, acc in ((w_ref, v_ref, y_acc), (c_ref, u_ref, dx_acc)):
+        one, two, three = split3(mat_ref[...])
+        rows = row_ref[...]
+        acc[...] += dot_nn(one, rows) + dot_nn(two, rows) + dot_nn(three, rows)
 
     @pl.when(step == pl.num_programs(0) - 1)
     def _():
-        out_ref[...] = acc_ref[...].astype(out_ref.dtype)
-
-
-def out_reduce_step(mat_ref, row_ref, part_ref, out_ref, red_ref, acc_ref, *scratch):
-    step = pl.program_id(0)
-    reducer = Reducer(part_ref, red_ref, scratch)
-    run_stages(reducer, step, None, OUT_MARKS)
-    out_step(mat_ref, row_ref, out_ref, acc_ref)
+        y_ref[...] = y_acc[...].astype(y_ref.dtype)
+        dx_ref[...] = dx_acc[...].astype(dx_ref.dtype)
+
     run_stages(reducer, step, pl.num_programs(0) - 1, OUT_MARKS)
 
 
-def out_pass(mat, rows, part=None):
-    n_tok, n_list = mat.shape
-    width = rows.shape[1]
-    cols = 1024
-    extra = part is not None
+def out_pass(w, v_sel, c, u_sel, part, first):
+    n_tok, n_list = w.shape
+    width = v_sel.shape[1]
+    cols = 512
+    mat_blk = pl.BlockSpec((n_tok, cols), lambda i: (0, i))
+    row_blk = pl.BlockSpec((cols, width), lambda i: (i, 0))
+    whole = pl.BlockSpec((n_tok, width), lambda i: (0, 0))
     return pl.pallas_call(
-        out_reduce_step if extra else out_step,
+        out_kernel,
         grid=(n_list // cols,),
-        in_specs=[pl.BlockSpec((n_tok, cols), lambda i: (0, i)), pl.BlockSpec((cols, width), lambda i: (i, 0))] + [pl.BlockSpec(memory_space=pl.ANY)] * extra,
-        out_specs=[pl.BlockSpec((n_tok, width), lambda i: (0, 0))] + [pl.BlockSpec((128, width), lambda i: (0, 0))] * extra,
-        out_shape=[jax.ShapeDtypeStruct((n_tok, width), BF16)] + [jax.ShapeDtypeStruct((128, width), BF16)] * extra,
-        scratch_shapes=[pltpu.VMEM((n_tok, width), F32)] + (Reducer.scratch(width) if extra else []),
-        compiler_params=pltpu.CompilerParams(vmem_limit_bytes=VMEM_LIMIT, has_side_effects=extra),
-        cost_estimate=pl.CostEstimate(flops=6 * n_tok * n_list * width, bytes_accessed=n_list * (width * 2 + n_tok * 4), transcendentals=0),
-        name="out_reduce" if extra else "out_pass",
-    )(mat, rows, *([part] if extra else []))
+        in_specs=[mat_blk, row_blk, mat_blk, row_blk] + [pl.BlockSpec(memory_space=pl.ANY)] * 4,
+        out_specs=[whole, whole, pl.BlockSpec((128, width), lambda i: (0, 0))],
+        out_shape=[jax.ShapeDtypeStruct((n_tok, width), BF16)] * 2 + [jax.ShapeDtypeStruct((128, width), BF16)],
+        scratch_shapes=[pltpu.VMEM((n_tok, width), F32)] * 2 + Reducer.scratch(width),
+        compiler_params=pltpu.CompilerParams(vmem_limit_bytes=VMEM_LIMIT, has_side_effects=True),
+        cost_estimate=pl.CostEstimate(flops=12 * n_tok * n_list * width, bytes_accessed=n_list * (width * 4 + n_tok * 8), transcendentals=0),
+        name="out_pass",
+    )(w, v_sel, c, u_sel, part, *first)
 
 
 def solution(mesh):
@@ -412,21 +527,11 @@
         pick_rel = pick.reshape(n_tok, -1) ^ (me << 7)
         gates = gate_matrix(pick_rel, gate.reshape(n_tok, -1), table_n)
 
-        swap = [(i, (i + table_n) % (2 * table_n)) for i in range(2 * table_n)]
-        cube = (SIDE, SIDE, SIDE, half, width)
-
-        def pair_sum(keep, send):
-            got = lax.ppermute(send, ('data', 'table'), swap)
-            return (keep.astype(F32) + got.astype(F32)).astype(BF16).reshape(cube)
-
         both_cores = lambda rows: lax.all_gather(rows, 'data', axis=0, tiled=True)
-        w, slope, u_sel, keep_v, send_v = first_pass(tok, dy.T, full_u, idsb, ids_flip, gates)
-        c, v_sel, keep_u, send_u, red_v = second_pass(dy, tok.T, full_v, idsb, ids_flip, slope, pair_sum(keep_v, send_v))
+        w, slope, u_sel, part_v, *first_v = first_pass(tok, dy.T, full_u, idsb, ids_flip, gates)
+        c, v_sel, part_u, *first_u, red_v = second_pass(dy, tok.T, full_v, idsb, ids_flip, slope, part_v, first_v)
+        y, dx, red_u = out_pass(w, v_sel, c, u_sel, part_u, first_u)
         grad_v = both_cores(red_v)
-        part_u = pair_sum(keep_u, send_u)
-        y, = out_pass(w, v_sel)
-        part_u, y = lax.optimization_barrier((part_u, y))
-        dx, red_u = out_pass(c, u_sel, part_u)
         grad_u = both_cores(red_u)
         return y, dx, grad_u, grad_v
 

time: 552 us -> 490 us (0.89)
  Pallas kernels: 323 us -> 372 us
  waiting for transfers between devices: 112 us -> 71.5 us
  other arithmetic: 42 us -> 1.67 us
  blocking collectives: 34.1 us -> 7.06 us
  starting transfers between devices: 7.14 us -> 0.08 us
    pallas_call x4 -> x3, Pallas kernels: 294 us -> 343 us  [the longest x1 144 us: first_pass(): pl.pallas_call(first_kernel, grid=(steps + LAG,), in_specs=[pl.BlockSpec(...]
    convert_element_type x2 -> x0, other arithmetic: 40.4 us -> none  [pair_sum(): return (keep.astype(F32) + got.astype(F32)).astype(BF16).reshape(cube)]
    ppermute x2 -> x0, waiting for transfers between devices: 37.7 us -> none  [pair_sum(): got = lax.ppermute(send, ('data', 'table'), swap)]
    all_gather x2, blocking collectives: 34.1 us -> 7.06 us  [device_step(): both_cores = lambda rows: lax.all_gather(rows, 'data', axis=0, tiled=True)]
    ppermute x2 -> x0, starting transfers between devices: 7.06 us -> none  [pair_sum(): got = lax.ppermute(send, ('data', 'table'), swap)]
    unnamed x11 -> x12, local copies, waits for them, and re-layouts: 8.43 us -> 11.7 us
  transfers between devices with their start and end apart: 4 -> 2, of which waited for: 2 -> 1; matrix products, arithmetic and copies ran while one was open for 7% -> 3% of each run, Pallas kernels for 24% -> 35%
where the time goes in v4:
time: 490 us
  Pallas kernels  372 us (76%)
  waiting for transfers between devices  71.5 us (15%)
  local copies, waits for them, and re-layouts  23 us (5%)
  between operations  14.1 us (3%)
  blocking collectives  7.06 us (1%)
    pallas_call x1, Pallas kernels, first_pass(): pl.pallas_call(first_kernel, grid=(steps + LAG,), in_specs=[pl.BlockSpec(...  144 us
    pallas_call x1, Pallas kernels, second_pass(): pl.pallas_call(second_kernel, grid=(steps + LAG,), in_specs=[pl.BlockSpec...  121 us
    pallas_call x1, Pallas kernels, out_pass(): pl.pallas_call(out_kernel, grid=(n_list // cols,), in_specs=[mat_blk, row...  77.5 us
    all_gather x1, waiting for transfers between devices, device_step(): lax.all_gather(own_rows(u_loc), ('table', 'data'), axis=0, tiled=True)  71.5 us
    pallas_call x1, Pallas kernels, gate_matrix(): pl.pallas_call(functools.partial(gate_kernel, n_own), grid=(tok // blk,),...  29.3 us
    unnamed x12, local copies, waits for them, and re-layouts  11.7 us
  transfers between devices with their start and end apart: 2, of which 1 were waited for; matrix products, arithmetic and copies ran while one was open for 3% of the time, Pallas kernels for 35%

profile of v4, /device:TPU:1, one launch (start us, length us, event | category | flops | bytes accessed | tf_op | source)
XLA Modules:
  0.0 489.6 jit_solution(662999204181525101)
XLA Ops:
  7.2 0.0 copy-start
  7.2 0.0 all-gather.3.cloned.1.call-start
  7.2 1.0 copy-done
  8.2 0.7 constant_dynamic-slice_fusion.1
  8.9 0.0 all-gather.3.cloned.1.call-update
  9.0 0.0 all-gather.5.cloned.1.call-start
  9.0 1.7 constant_dynamic-slice_fusion
  10.7 0.0 all-gather.5.cloned.1.call-update
  10.7 1.0 broadcast_xor_fusion
  11.7 0.8 copy.16.pick_ref
  12.6 1.8 copy.17.gate_ref
  14.3 2.3 copy.18
  16.6 2.3 copy.15
  18.9 1.4 gather_fusion
  20.3 0.7 subtract_xor_fusion
  20.9 29.3 %gate_matrix.1.gate_ref = f32[512,8192]{1,0:T(8,128)} custom-call(s32[512,128]{1,0:T(8,128)} %copy.16.pick_ref, f32[512,128]{1,0:T(8,128)} %copy.17.gate_ref), custom_call_target="tpu_custom_call" | custom-call | flops 12884901888 | bytes 16777216 | tf_op jit(solution)/shard_map/gate_matrix/pallas_call | solution.py:70
  50.2 71.5 %all-gather.3.cloned.1.call-done.tab_ref = bf16[16384,1024]{1,0:T(8,128)(2,1)} async-done(((bf16[128,1024]{1,0:T(8,128)(2,1)}), bf16[16384,1024]{1,0:T(8,128)(2,1)}) %all-gather.3.cloned.1.call-update) | async-done | bytes 33554448 | tf_op jit(solution)/shard_map/all_gather | solution.py:520
  121.7 4.9 %broadcast_in_dim.4.idsb_ref = s32[8192,128]{1,0:T(8,128)} broadcast(s32[8192]{0:T(1024)S(1)} %get-tuple-element.39), dimensions={0} | broadcast | bytes 4227072 | tf_op jit(solution)/shard_map/broadcast_in_dim | solution.py:526
  126.6 144.4 %first_pass.1 = (f32[512,8192]{1,0:T(8,128)}, f32[512,8192]{1,0:T(8,128)}, bf16[8192,1024]{1,0:T(8,128)(2,1)}, bf16[4,4,4,128,1024]{4,3,2,1,0:T(8,128)(2,1)}, bf...) custom-call(bf16[512,1024]{1,0:T(8,128)(2,1)} %tok_ref.1, ...), custom_call_target="tpu_custom_call" | custom-call | flops 47244640256 | bytes 134217728 | tf_op jit(solution)/shard_map/first_pass/pallas_call | solution.py:249
  271.0 0.0 all-gather.5.cloned.1.call-done.tab_ref
  271.1 121.0 %second_pass.1 = (f32[512,8192]{1,0:T(8,128)}, bf16[8192,1024]{1,0:T(8,128)(2,1)}, bf16[4,4,4,128,1024]{4,3,2,1,0:T(8,128)(2,1)}, bf16[2,4,4,48,1024]{4,3,2,1,0:...) custom-call(bf16[512,1024]{1,0:T(8,128)(2,1)} %dy_ref.1, ...), custom_call_target="tpu_custom_call" | custom-call | flops 47244640256 | bytes 117440512 | tf_op jit(solution)/shard_map/second_pass/pallas_call | solution.py:442
  392.1 0.0 copy-start.2
  392.1 0.0 copy-start.1
  392.1 77.5 %out_pass.1 = (bf16[512,1024]{1,0:T(8,128)(2,1)}, bf16[512,1024]{1,0:T(8,128)(2,1)}, bf16[128,1024]{1,0:T(8,128)(2,1)}) custom-call(f32[512,8192]{1,0:T(8,128)} %get-tuple-element.21.w_ref, bf16[8192,1024]{1,0:T(8,128)(2,1)} %get-tuple-element.27.v_ref, f32[512,8192]{1,0:T(8,128)} %get-tuple-element.28.c_ref, bf16[8192,1024]{1,0:T(8,128)(2,1)} %get-tuple-element.29.u_ref, ...), custom_call_target="tpu_custom_call" | custom-call | flops 51539607552 | bytes 67108864 | tf_op jit(solution)/shard_map/out_pass/pallas_call | solution.py:495
  469.6 4.9 all_gather.14
  474.5 0.0 copy-done.2
  474.5 2.2 all_gather.15
  476.6 2.3 copy.23
  478.9 2.3 copy.24
  481.2 0.8 copy.25
  482.0 0.8 copy.26
  482.7 0.0 copy-done.1
  (3 shorter events, 0.0 us)
Async XLA Ops:
  7.2 1.1 copy-start
  7.2 114.5 %all-gather.3.cloned.1.call-start = ((), (), s32[]{:S(2)}) async-start(), calls=%async_computation | async-start | bytes 33816576 | tf_op jit(solution)/shard_map/all_gather | solution.py:520
  9.0 262.1 %all-gather.5.cloned.1.call-start = ((), (), s32[]{:S(2)}) async-start(), calls=%async_computation.1 | async-start | bytes 33816576 | tf_op jit(solution)/shard_map/all_gather | solution.py:521
  392.1 82.4 %copy-start.2 = (bf16[128,1024]{1,0:T(8,128)(2,1)S(1)}, bf16[128,1024]{1,0:T(8,128)(2,1)}, u32[]{:S(2)}) copy-start(bf16[128,1024]{1,0:T(8,128)(2,1)} %get-tuple-element.37) | copy-start | bytes 786436
  392.1 90.7 %copy-start.1 = (bf16[256,1024]{1,0:T(8,128)(2,1)S(1)}, bf16[256,1024]{1,0:T(8,128)(2,1)}, u32[]{:S(2)}) copy-start(bf16[256,1024]{1,0:T(8,128)(2,1)} %param.9) | copy-start | bytes 1572868
Sparse Core Ops, SparseCore 0:
  11.6 110.0 all-gather.2
  124.7 123.6 all-gather.4

commit v5 on v4

--- a/solution.py
+++ b/solution.py
@@ -31,16 +31,225 @@
     return lax.dot_general(lhs, rhs, (((1,), (1,)), ((), ())), preferred_element_type=F32)
 
 
-def xor_field(val, other):
-    return (val // 2 + other // 2) % 2 * 2 + (val % 2 + other % 2) % 2
-
-
-def table_block(step):
-    me = lax.axis_index('table')
-    return xor_field(step // 4, me // 16) * 4 + xor_field(step % 4, (me // 4) % 4)
-
-
-def gate_kernel(n_own, pick_ref, gate_ref, out_ref, tile_ref):
+def select_rows(tab_ref, idsb_ref, sel_ref):
+    n_rows = tab_ref.shape[0] // OWN_STEP
+    iota = lax.broadcasted_iota(jnp.int32, (128, 128), 1)
+    for j in range(OWN_STEP):
+        ids = idsb_ref[j * 128:(j + 1) * 128, :]
+        hot = jnp.concatenate([jnp.where(ids == iota + 128 * h, 1.0, 0.0).astype(BF16) for h in range(n_rows // 128)], axis=1)
+        sel_ref[j * 128:(j + 1) * 128, :] = dot_nn(hot, tab_ref[j * n_rows:(j + 1) * n_rows, :]).astype(BF16)
+
+
+def place_rows(blk, grad_t, ids_ref, slot, keep_ref, send_ref):
+    iota = lax.broadcasted_iota(jnp.int32, (256, 128), 0)
+    grad_b = grad_t.astype(BF16)
+    for j in range(OWN_STEP):
+        hot = jnp.where(iota == ids_ref[pl.ds(blk * OWN_STEP + j, 1), :], 1.0, 0.0).astype(BF16)
+        rows = dot_nt(hot, grad_b[:, j * 128:(j + 1) * 128]).astype(BF16)
+        keep_ref[slot, j] = rows[:128]
+        send_ref[slot, j] = rows[128:]
+
+
+LAG = 3
+
+
+class Exchanger:
+    @staticmethod
+    def scratch(width):
+        blk = (2, OWN_STEP, 128, width)
+        dma = pltpu.SemaphoreType.DMA
+        return [pltpu.VMEM(blk, BF16)] * 4 + [dma((2,)), dma((2,)), dma((2,)), dma((6,)), dma((6,))]
+
+    @staticmethod
+    def out_shapes(width):
+        rows = [ROW_CUTS[k + 1] - ROW_CUTS[k] for k in range(3)]
+        cube = jax.ShapeDtypeStruct((SIDE, SIDE, SIDE, 128, width), BF16)
+        return [cube] + [jax.ShapeDtypeStruct((2, SIDE, SIDE, n, width), BF16) for n in rows]
+
+    @staticmethod
+    def out_specs():
+        return [pl.BlockSpec(memory_space=pl.ANY)] * 4
+
+    def __init__(self, step, blocks, outs, scratch):
+        self.step, self.blocks = step, blocks
+        self.part_ref, self.first = outs[0], outs[1:]
+        self.keep, self.send, self.got, self.sum = scratch[:4]
+        self.pair_send, self.pair_recv, self.store_sem, self.out_send, self.out_recv = scratch[4:]
+        self.ring = Ring()
+
+    def pair_copy(self, slot):
+        other = 1 - lax.axis_index('data')
+        return pltpu.make_async_remote_copy(src_ref=self.send.at[slot], dst_ref=self.got.at[slot], send_sem=self.pair_send.at[slot], recv_sem=self.pair_recv.at[slot], device_id={'data': other}, device_id_type=pl.DeviceIdType.MESH)
+
+    def store_copy(self, blk):
+        slot = blk % 2
+        return pltpu.make_async_copy(self.sum.at[slot], self.part_ref.at[blk // SIDE, blk % SIDE], self.store_sem.at[slot])
+
+    def start_first(self, blk):
+        spots = (blk // SIDE, blk % SIDE)
+        near = self.ring.near
+        for k in range(3):
+            axis = AXIS_ORDERS[k][0]
+            rows = pl.ds(ROW_CUTS[k], ROW_CUTS[k + 1] - ROW_CUTS[k])
+            for way, mark in enumerate((near, 2)):
+                def start(k=k, axis=axis, rows=rows, way=way, mark=mark):
+                    if axis == 2:
+                        src, dst = self.part_ref.at[spots[0], spots[1], mark, rows], self.first[k].at[way, spots[0], spots[1]]
+                    else:
+                        src, dst = self.part_ref.at[spots[0], spots[1], :, rows], self.first[k].at[way, spots[1 - axis]]
+                    pltpu.make_async_remote_copy(src_ref=src, dst_ref=dst, send_sem=self.out_send.at[2 * k + way], recv_sem=self.out_recv.at[2 * k + way], device_id={'table': self.ring.partner(axis, True)}, device_id_type=pl.DeviceIdType.MESH).start()
+                if axis == 2:
+                    start()
+                else:
+                    pl.when(spots[axis] == mark)(start)
+
+    def before(self):
+        step, blocks = self.step, self.blocks
+
+        @pl.when((step >= 3) & (step - 3 < blocks))
+        def _():
+            self.store_copy(step - 3).wait()
+            self.start_first(step - 3)
+
+        @pl.when((step >= 2) & (step - 2 < blocks))
+        def _():
+            slot = step % 2
+            copy = self.pair_copy(slot)
+            copy.wait_recv()
+            for j in range(OWN_STEP):
+                self.sum[slot, j] = (self.keep[slot, j].astype(F32) + self.got[slot, j].astype(F32)).astype(BF16)
+            self.store_copy(step - 2).start()
+            copy.wait_send()
+
+        @pl.when((step >= 1) & (step - 1 < blocks))
+        def _():
+            self.pair_copy((step - 1) % 2).start()
+
+    def after(self):
+        @pl.when(self.step == self.blocks + LAG - 1)
+        def _():
+            for k in range(3):
+                for way in range(2):
+                    dst = self.first[k].at[way]
+                    pltpu.make_async_copy(dst, dst, self.out_send.at[2 * k + way]).wait()
+                    pltpu.make_async_copy(dst, dst, self.out_recv.at[2 * k + way]).wait()
+
+
+class Ring:
+    def __init__(self):
+        self.core = lax.axis_index('data')
+        self.near, self.far = 1 + 2 * self.core, 3 - 2 * self.core
+
+    def partner(self, axis, first):
+        me = lax.axis_index('table')
+        stride = SIDE ** (2 - axis)
+        pos = (me // stride) % SIDE
+        even, odd = pos + 1 - 2 * (pos % 2), 3 - pos
+        new = even + self.core * (odd - even) if first else odd + self.core * (even - odd)
+        return me + (new - pos) * stride
+
+
+class Gatherer(Ring):
+    STEPS = {1: (0,), 2: (1, 2), 3: (3,), 4: (4, 5), 5: (6,), 6: (7, 8)}
+
+    @staticmethod
+    def scratch():
+        return [pltpu.SemaphoreType.DMA((27,))] * 4 + [pltpu.SemaphoreType.DMA((1,))]
+
+    def __init__(self, own, full, scratch):
+        super().__init__()
+        self.own, self.full = own, full
+        self.send_sem, self.recv_sem, self.pass_send, self.pass_recv, self.own_sem = scratch
+
+    def spot(self, k, ia, ib, ic):
+        idx = [None] * 3
+        for axis, val in zip(AXIS_ORDERS[k], (ia, ib, ic)):
+            idx[axis] = val
+        start = pl.multiple_of(self.core * 128 + ROW_CUTS[k], 16)
+        return self.full.at[idx[0], idx[1], idx[2], pl.ds(start, ROW_CUTS[k + 1] - ROW_CUTS[k])]
+
+    def ends(self, num):
+        near, far, every = self.near, self.far, slice(None)
+        return (
+            ((0, 0, 0), (near, 0, 0)),
+            ((0, 0, 0), (far, 0, 0)),
+            ((near, 0, 0), (2, 0, 0)),
+            ((every, 0, 0), (every, near, 0)),
+            ((every, 0, 0), (every, far, 0)),
+            ((every, near, 0), (every, 2, 0)),
+            ((every, every, 0), (every, every, near)),
+            ((every, every, 0), (every, every, far)),
+            ((every, every, near), (every, every, 2)),
+        )[num]
+
+    def copy(self, k, num):
+        src, dst = self.ends(num)
+        step = [key for key, nums in self.STEPS.items() if num in nums][0]
+        at = 9 * k + num
+        there = self.partner(AXIS_ORDERS[k][(step - 1) // 2], step % 2 == 1)
+        return pltpu.make_async_remote_copy(src_ref=self.spot(k, *src), dst_ref=self.spot(k, *dst), send_sem=self.send_sem.at[at], recv_sem=self.recv_sem.at[at], device_id={'table': there}, device_id_type=pl.DeviceIdType.MESH)
+
+    def forward(self, k, num):
+        here = self.spot(k, *self.ends(num)[1])
+        at = 9 * k + num
+        return pltpu.make_async_remote_copy(src_ref=here, dst_ref=here, send_sem=self.pass_send.at[at], recv_sem=self.pass_recv.at[at], device_id={'data': 1 - self.core}, device_id_type=pl.DeviceIdType.MESH)
+
+    def begin(self):
+        own = pltpu.make_async_copy(self.own, self.full.at[0, 0, 0], self.own_sem.at[0])
+        own.start()
+        own.wait()
+
+    def send(self, step):
+        for k in range(3):
+            for num in self.STEPS[step]:
+                self.copy(k, num).start()
+
+    def arrive(self, *nums):
+        for k in range(3):
+            for num in nums:
+                self.copy(k, num).wait_recv()
+
+    def spread(self, *nums):
+        for k in range(3):
+            for num in nums:
+                self.forward(k, num).start()
+
+    def finish(self, *nums):
+        for k in range(3):
+            for num in nums:
+                self.copy(k, num).wait_send()
+                self.forward(k, num).wait_send()
+                self.forward(k, num).wait_recv()
+
+
+GATE_STEPS = 16
+
+
+def gate_kernel(n_own, pick_ref, gate_ref, u_ref, v_ref, out_ref, full_u_ref, full_v_ref, tile_ref, *scratch):
+    step = pl.program_id(0)
+    get_u = Gatherer(u_ref, full_u_ref, scratch[:5])
+    get_v = Gatherer(v_ref, full_v_ref, scratch[5:])
+
+    @pl.when(step == 0)
+    def _():
+        for get in (get_u, get_v):
+            get.begin()
+            get.send(1)
+
+    for mark, got, then in ((3, (0,), 2), (6, (1, 2), 3), (10, (3,), 4)):
+        @pl.when(step == mark)
+        def _(got=got, then=then):
+            for get in (get_u, get_v):
+                get.arrive(*got)
+                get.send(then)
+                get.spread(*got)
+
+    @pl.when(step == GATE_STEPS - 1)
+    def _():
+        get_u.arrive(4, 5)
+        get_u.send(5)
+        get_u.spread(4, 5)
+
     sel = pick_ref.shape[1]
     iota_own = lax.broadcasted_iota(jnp.int32, (n_own, sel), 0)
     iota_lo = lax.broadcasted_iota(jnp.int32, (128, sel), 0)
@@ -63,159 +272,60 @@
 
     lax.fori_loop(0, pick_ref.shape[0] // 8, body, 0)
 
-
-def gate_matrix(pick_rel, gate, n_own):
+    @pl.when(step == GATE_STEPS - 1)
+    def _():
+        get_v.arrive(4, 5)
+        get_v.spread(4, 5)
+        get_u.arrive(6)
+        get_u.send(6)
+        get_u.spread(6)
+        get_v.finish(0, 1, 2, 3, 4, 5)
+        get_u.arrive(7)
+        get_u.spread(7)
+        get_u.arrive(8)
+        get_u.spread(8)
+        get_u.finish(0, 1, 2, 3, 4, 5, 6, 7, 8)
+
+
+def gate_matrix(pick_rel, gate, u_loc, v_loc, n_own):
     tok, sel = pick_rel.shape
-    blk = max(8, tok // 4)
+    blk = tok // GATE_STEPS
+    own = pl.BlockSpec(u_loc.shape, lambda i: (0, 0))
+    full = jax.ShapeDtypeStruct((SIDE, SIDE, SIDE) + u_loc.shape, BF16)
     return pl.pallas_call(
         functools.partial(gate_kernel, n_own),
-        grid=(tok // blk,),
-        in_specs=[pl.BlockSpec((blk, sel), lambda i: (i, 0)), pl.BlockSpec((blk, sel), lambda i: (i, 0))],
-        out_specs=pl.BlockSpec((blk, n_own * 128), lambda i: (i, 0)),
-        out_shape=jax.ShapeDtypeStruct((tok, n_own * 128), F32),
-        scratch_shapes=[pltpu.VMEM((8 * n_own, 128), F32)],
-        compiler_params=pltpu.CompilerParams(vmem_limit_bytes=VMEM_LIMIT),
+        grid=(GATE_STEPS,),
+        in_specs=[pl.BlockSpec((blk, sel), lambda i: (i, 0)), pl.BlockSpec((blk, sel), lambda i: (i, 0)), own, own],
+        out_specs=[pl.BlockSpec((blk, n_own * 128), lambda i: (i, 0))] + [pl.BlockSpec(memory_space=pl.ANY)] * 2,
+        out_shape=[jax.ShapeDtypeStruct((tok, n_own * 128), F32), full, full],
+        scratch_shapes=[pltpu.VMEM((8 * n_own, 128), F32)] + Gatherer.scratch() + Gatherer.scratch(),
+        compiler_params=pltpu.CompilerParams(vmem_limit_bytes=VMEM_LIMIT, has_side_effects=True),
         cost_estimate=pl.CostEstimate(flops=2 * tok * 256 * 256 * 192, bytes_accessed=tok * n_own * 512, transcendentals=0),
         name="gate_matrix",
-    )(pick_rel, gate)
-
-
-def select_rows(tab_ref, idsb_ref, sel_ref):
-    n_rows = tab_ref.shape[0] // OWN_STEP
-    iota = lax.broadcasted_iota(jnp.int32, (128, 128), 1)
-    my_x = lax.axis_index('table') % 4
-    for j in range(OWN_STEP):
-        ids = idsb_ref[j * 128:(j + 1) * 128, :]
-        hot = jnp.concatenate([jnp.where(ids == iota + 128 * h, 1.0, 0.0).astype(BF16) for h in range(n_rows // 128)], axis=1)
-        start = pl.multiple_of(xor_field(j, my_x) * n_rows, n_rows)
-        sel_ref[j * 128:(j + 1) * 128, :] = dot_nn(hot, tab_ref[pl.ds(start, n_rows), :]).astype(BF16)
-
-
-def place_rows(blk, grad_t, ids_ref, slot, keep_ref, send_ref):
-    iota = lax.broadcasted_iota(jnp.int32, (256, 128), 0)
-    grad_b = grad_t.astype(BF16)
-    for j in range(OWN_STEP):
-        hot = jnp.where(iota == ids_ref[pl.ds(blk * OWN_STEP + j, 1), :], 1.0, 0.0).astype(BF16)
-        rows = dot_nt(hot, grad_b[:, j * 128:(j + 1) * 128]).astype(BF16)
-        keep_ref[slot, j] = rows[:128]
-        send_ref[slot, j] = rows[128:]
-
-
-LAG = 3
-
-
-class Exchanger:
-    @staticmethod
-    def scratch(width):
-        blk = (2, OWN_STEP, 128, width)
-        dma = pltpu.SemaphoreType.DMA
-        return [pltpu.VMEM(blk, BF16)] * 4 + [dma((2,)), dma((2,)), dma((8,)), dma((6,))]
-
-    @staticmethod
-    def out_shapes(width):
-        rows = [ROW_CUTS[k + 1] - ROW_CUTS[k] for k in range(3)]
-        cube = jax.ShapeDtypeStruct((SIDE, SIDE, SIDE, 128, width), BF16)
-        return [cube] + [jax.ShapeDtypeStruct((2, SIDE, SIDE, n, width), BF16) for n in rows]
-
-    @staticmethod
-    def out_specs(width, blocks):
-        def place(i):
-            blk = jnp.clip(i - 2, 0, blocks - 1)
-            return blk // SIDE, blk % SIDE, 0, 0, 0
-        return [pl.BlockSpec((1, 1, SIDE, 128, width), place)] + [pl.BlockSpec(memory_space=pl.ANY)] * 3
-
-    def __init__(self, step, blocks, outs, scratch):
-        self.step, self.blocks = step, blocks
-        self.part_ref, self.first = outs[0], outs[1:]
-        self.keep, self.send, self.got, self.sum = scratch[:4]
-        self.pair_send, self.pair_recv, self.out_send, self.out_recv = scratch[4:]
-        self.ring = Ring()
-
-    def pair_copy(self, slot):
-        other = 1 - lax.axis_index('data')
-        return pltpu.make_async_remote_copy(src_ref=self.send.at[slot], dst_ref=self.got.at[slot], send_sem=self.pair_send.at[slot], recv_sem=self.pair_recv.at[slot], device_id={'data': other}, device_id_type=pl.DeviceIdType.MESH)
-
-    def first_copies(self, blk):
-        slot = blk % 2
-        spots = (blk // SIDE, blk % SIDE)
-        out = []
-        near = self.ring.near
-
-        def copy(k, num, src, dst, way):
-            return pltpu.make_async_remote_copy(src_ref=src, dst_ref=dst, send_sem=self.out_send.at[4 * slot + num], recv_sem=self.out_recv.at[2 * k + way], device_id={'table': self.ring.partner(AXIS_ORDERS[k][0], True)}, device_id_type=pl.DeviceIdType.MESH)
-
-        for k in range(3):
-            axis = AXIS_ORDERS[k][0]
-            rows = pl.ds(ROW_CUTS[k], ROW_CUTS[k + 1] - ROW_CUTS[k])
-            if axis == 2:
-                for way, x in enumerate((near, 2)):
-                    out.append((None, copy(k, way, self.sum.at[slot, x, rows], self.first[k].at[way, spots[0], spots[1]], way)))
-            else:
-                for way, mark in enumerate((near, 2)):
-                    out.append((spots[axis] == mark, copy(k, 3 - axis, self.sum.at[slot, :, rows], self.first[k].at[way, spots[1 - axis]], way)))
-        return out
-
-    def on_first(self, blk, act):
-        for cond, copy in self.first_copies(blk):
-            if cond is None:
-                act(copy)
-            else:
-                pl.when(cond)(functools.partial(act, copy))
-
-    def before(self):
-        step, blocks = self.step, self.blocks
-
-        @pl.when((step >= 4) & (step - 4 < blocks))
-        def _():
-            self.on_first(step - 4, lambda copy: copy.wait_send())
-
-        @pl.when((step >= 3) & (step - 3 < blocks))
-        def _():
-            self.on_first(step - 3, lambda copy: copy.start())
-
-        @pl.when((step >= 2) & (step - 2 < blocks))
-        def _():
-            slot = step % 2
-            copy = self.pair_copy(slot)
-            copy.wait_recv()
-            for j in range(OWN_STEP):
-                rows = (self.keep[slot, j].astype(F32) + self.got[slot, j].astype(F32)).astype(BF16)
-                self.sum[slot, j] = rows
-                self.part_ref[0, 0, j] = rows
-            copy.wait_send()
-
-        @pl.when((step >= 1) & (step - 1 < blocks))
-        def _():
-            self.pair_copy((step - 1) % 2).start()
-
-    def after(self):
-        @pl.when(self.step == self.blocks + LAG - 1)
-        def _():
-            self.on_first(self.blocks - 1, lambda copy: copy.wait_send())
-            for k in range(3):
-                for way in range(2):
-                    dst = self.first[k].at[way]
-                    pltpu.make_async_copy(dst, dst, self.out_recv.at[2 * k + way]).wait()
-
-
-class Ring:
-    def __init__(self):
-        self.core = lax.axis_index('data')
-        self.near, self.far = 1 + 2 * self.core, 3 - 2 * self.core
-
-    def partner(self, axis, first):
-        me = lax.axis_index('table')
-        stride = SIDE ** (2 - axis)
-        pos = (me // stride) % SIDE
-        even, odd = pos + 1 - 2 * (pos % 2), 3 - pos
-        new = even + self.core * (odd - even) if first else odd + self.core * (even - odd)
-        return me + (new - pos) * stride
-
-
-def first_kernel(tok_ref, dyt_ref, tab_ref, idsb_ref, ids_ref, gate_ref, w_ref, slope_ref, sel_ref, *rest):
+    )(pick_rel, gate, u_loc, v_loc)
+
+
+def first_kernel(tok_ref, dyt_ref, tab_ref, idsb_ref, ids_ref, gate_ref, held_ref, w_ref, slope_ref, sel_ref, full_ref, *rest):
     step = pl.program_id(0)
     blocks = pl.num_programs(0) - LAG
-    swap = Exchanger(step, blocks, rest[:4], rest[4:])
+    swap = Exchanger(step, blocks, rest[:4], rest[4:13])
+    get_v = Gatherer(None, full_ref, rest[13:])
+
+    @pl.when(step == 0)
+    def _():
+        get_v.send(5)
+
+    @pl.when(step == 5)
+    def _():
+        get_v.arrive(6)
+        get_v.send(6)
+        get_v.spread(6)
+
+    @pl.when(step == 12)
+    def _():
+        get_v.arrive(7)
+        get_v.spread(7)
+
     swap.before()
 
     @pl.when(step < blocks)
@@ -234,10 +344,19 @@
         grad_t = dot_nn(dyt, one) + dot_nn(dyt, two) + dot_nn(dyt, three)
         place_rows(step, grad_t, ids_ref, step % 2, swap.keep, swap.send)
 
+    @pl.when(step == blocks + LAG - 1)
+    def _():
+        get_v.arrive(8)
+        get_v.spread(8)
+
     swap.after()
 
-
-def first_pass(tok, dyt, table, idsb, ids_flip, gate):
+    @pl.when(step == blocks + LAG - 1)
+    def _():
+        get_v.finish(6, 7, 8)
+
+
+def first_pass(tok, dyt, table, idsb, ids_flip, gate, held):
     n_tok, width = tok.shape
     n_list = gate.shape[1]
     cols = OWN_STEP * 128
@@ -252,22 +371,25 @@
         in_specs=[
             pl.BlockSpec((n_tok, width), lambda i: (0, 0)),
             pl.BlockSpec((width, n_tok), lambda i: (0, 0)),
-            pl.BlockSpec((trows, width), lambda i: (table_block(at(i)), 0)),
+            pl.BlockSpec((trows, width), lambda i: (at(i), 0)),
             pl.BlockSpec((cols, 128), lambda i: (at(i), 0)),
             pl.BlockSpec(ids_flip.shape, lambda i: (0, 0)),
             mat_blk,
+            pl.BlockSpec(memory_space=pl.ANY),
         ],
-        out_specs=[mat_blk, mat_blk, row_blk] + Exchanger.out_specs(width, steps),
+        out_specs=[mat_blk, mat_blk, row_blk, pl.BlockSpec(memory_space=pl.ANY)] + Exchanger.out_specs(),
         out_shape=[
             jax.ShapeDtypeStruct((n_tok, n_list), F32),
             jax.ShapeDtypeStruct((n_tok, n_list), F32),
             jax.ShapeDtypeStruct((n_list, width), BF16),
+            jax.ShapeDtypeStruct(held.shape, BF16),
         ] + Exchanger.out_shapes(width),
-        scratch_shapes=Exchanger.scratch(width),
+        scratch_shapes=Exchanger.scratch(width) + Gatherer.scratch(),
+        input_output_aliases={6: 3},
         compiler_params=pltpu.CompilerParams(vmem_limit_bytes=VMEM_LIMIT, has_side_effects=True),
         cost_estimate=pl.CostEstimate(flops=11 * n_tok * n_list * width, bytes_accessed=n_list * (width * 10 + n_tok * 12), transcendentals=0),
         name="first_pass",
-    )(tok, dyt, table, idsb, ids_flip, gate)
+    )(tok, dyt, table, idsb, ids_flip, gate, held)
 
 
 class Reducer(Ring):
@@ -409,8 +531,8 @@
     step = pl.program_id(0)
     blocks = pl.num_programs(0) - LAG
     red_ref = rest[4]
-    swap = Exchanger(step, blocks, rest[:4], rest[5:13])
-    reducer = Reducer(part_ref, (f0_ref, f1_ref, f2_ref), red_ref, rest[13:])
+    swap = Exchanger(step, blocks, rest[:4], rest[5:14])
+    reducer = Reducer(part_ref, (f0_ref, f1_ref, f2_ref), red_ref, rest[14:])
     swap.before()
     run_stages(reducer, step, None, SECOND_MARKS)
 
@@ -445,12 +567,12 @@
         in_specs=[
             pl.BlockSpec((n_tok, width), lambda i: (0, 0)),
             pl.BlockSpec((width, n_tok), lambda i: (0, 0)),
-            pl.BlockSpec((trows, width), lambda i: (table_block(at(i)), 0)),
+            pl.BlockSpec((trows, width), lambda i: (at(i), 0)),
             pl.BlockSpec((cols, 128), lambda i: (at(i), 0)),
             pl.BlockSpec(ids_flip.shape, lambda i: (0, 0)),
             mat_blk,
         ] + [pl.BlockSpec(memory_space=pl.ANY)] * 4,
-        out_specs=[mat_blk, row_blk] + Exchanger.out_specs(width, steps) + [pl.BlockSpec((128, width), lambda i: (0, 0))],
+        out_specs=[mat_blk, row_blk] + Exchanger.out_specs() + [pl.BlockSpec((128, width), lambda i: (0, 0))],
         out_shape=[
             jax.ShapeDtypeStruct((n_tok, n_list), F32),
             jax.ShapeDtypeStruct((n_list, width), BF16),
@@ -516,20 +638,17 @@
         n_tok = tok.shape[0]
         core = lax.axis_index('data')
         me = lax.axis_index('table')
-        own_rows = lambda arr: lax.dynamic_slice_in_dim(arr, core * half, half, 0)
-        full_u = lax.all_gather(own_rows(u_loc), ('table', 'data'), axis=0, tiled=True)
-        full_v = lax.all_gather(own_rows(v_loc), ('table', 'data'), axis=0, tiled=True)
-
         owners = jnp.arange(table_n, dtype=jnp.int32) ^ me
         ids = jnp.take(wanted.reshape(table_n, -1), owners, axis=0, mode='clip') - owners[:, None] * n_local
         ids_flip = ids ^ (core * half)
         idsb = jnp.broadcast_to(ids.reshape(-1, 1), (ids.size, 128))
         pick_rel = pick.reshape(n_tok, -1) ^ (me << 7)
-        gates = gate_matrix(pick_rel, gate.reshape(n_tok, -1), table_n)
+        gates, full_u, full_v = gate_matrix(pick_rel, gate.reshape(n_tok, -1), u_loc, v_loc, table_n)
+        flat = lambda full: full.reshape(table_n * n_local, width)
 
         both_cores = lambda rows: lax.all_gather(rows, 'data', axis=0, tiled=True)
-        w, slope, u_sel, part_v, *first_v = first_pass(tok, dy.T, full_u, idsb, ids_flip, gates)
-        c, v_sel, part_u, *first_u, red_v = second_pass(dy, tok.T, full_v, idsb, ids_flip, slope, part_v, first_v)
+        w, slope, u_sel, full_v, part_v, *first_v = first_pass(tok, dy.T, flat(full_u), idsb, ids_flip, gates, full_v)
+        c, v_sel, part_u, *first_u, red_v = second_pass(dy, tok.T, flat(full_v), idsb, ids_flip, slope, part_v, first_v)
         y, dx, red_u = out_pass(w, v_sel, c, u_sel, part_u, first_u)
         grad_v = both_cores(red_v)
         grad_u = both_cores(red_u)

time: 490 us -> 425 us (0.87)
  waiting for transfers between devices: 71.5 us -> 0 us
  Pallas kernels: 372 us -> 398 us
  between operations: 14.1 us -> 0.74 us
  local copies, waits for them, and re-layouts: 23 us -> 17.7 us
    pallas_call x1, Pallas kernels: 29.3 us -> 119 us  [gate_matrix(): pl.pallas_call(functools.partial(gate_kernel, n_own), grid=(GATE_STEPS,),...]
    all_gather x2 -> x0, waiting for transfers between devices: 71.5 us -> none  [the longest x1 71.5 us: device_step(): lax.all_gather(own_rows(u_loc), ('table', 'data'), axis=0, tiled=True)]
    pallas_call x1, Pallas kernels: 144 us -> 101 us  [first_pass(): pl.pallas_call(first_kernel, grid=(steps + LAG,), in_specs=[pl.BlockSpec(...]
    pallas_call x1, Pallas kernels: 121 us -> 106 us  [second_pass(): pl.pallas_call(second_kernel, grid=(steps + LAG,), in_specs=[pl.BlockSpec...]
    pallas_call x1, Pallas kernels: 77.5 us -> 71.4 us  [out_pass(): pl.pallas_call(out_kernel, grid=(n_list // cols,), in_specs=[mat_blk, row...]
    unnamed x12 -> x16, local copies, waits for them, and re-layouts: 11.7 us -> 9.5 us
  transfers between devices with their start and end apart: 2 -> 0, of which waited for: 1 -> 0; matrix products, arithmetic and copies ran while one was open for 3% -> 0% of each run, Pallas kernels for 35% -> 0%
where the time goes in v5:
time: 425 us
  Pallas kernels  398 us (94%)
  local copies, waits for them, and re-layouts  17.7 us (4%)
  blocking collectives  7.06 us (2%)
    pallas_call x1, Pallas kernels, gate_matrix(): pl.pallas_call(functools.partial(gate_kernel, n_own), grid=(GATE_STEPS,),...  119 us
    pallas_call x1, Pallas kernels, second_pass(): pl.pallas_call(second_kernel, grid=(steps + LAG,), in_specs=[pl.BlockSpec...  106 us
    pallas_call x1, Pallas kernels, first_pass(): pl.pallas_call(first_kernel, grid=(steps + LAG,), in_specs=[pl.BlockSpec(...  101 us
    pallas_call x1, Pallas kernels, out_pass(): pl.pallas_call(out_kernel, grid=(n_list // cols,), in_specs=[mat_blk, row...  71.4 us
    unnamed x16, local copies, waits for them, and re-layouts  9.5 us

profile of v5, /device:TPU:1, one launch (start us, length us, event | category | flops | bytes accessed | tf_op | source)
XLA Modules:
  0.0 424.8 jit_solution(4676671518429192960)
XLA Ops:
  0.6 0.0 copy-start
  0.7 0.7 copy-done
  1.4 0.6 gather_fusion
  2.0 0.7 subtract_xor_fusion
  2.7 5.0 %broadcast_in_dim.4.idsb_ref = s32[8192,128]{1,0:T(8,128)} broadcast(s32[8192]{0:T(1024)S(1)} %get-tuple-element.47), dimensions={0} | broadcast | bytes 4227072 | tf_op jit(solution)/shard_map/broadcast_in_dim | solution.py:644
  7.7 1.0 broadcast_xor_fusion
  8.6 0.8 copy.17.pick_ref
  9.5 1.8 copy.18.gate_ref
  11.3 0.0 copy-start.3
  11.3 118.6 %gate_matrix.1 = (f32[512,8192]{1,0:T(8,128)}, bf16[4,4,4,256,1024]{4,3,2,1,0:T(8,128)(2,1)}, bf16[4,4,4,256,1024]{4,3,2,1,0:T(8,128)(2,1)}) custom-call(s32[512,128]{1,0:T(8,128)} %copy.17.pick_ref, f32[512,128]{1,0:T(8,128)} %copy.18.gate_ref, bf16[256,1024]{1,0:T(8,128)(2,1)} %u_ref.1, bf16[256,1024]{1,0:T(8,128)(2,1)} %v_ref.1), custom_call_target="tpu_custom_call" | custom-call | flops 12884901888 | bytes 16777216 | tf_op jit(solution)/shard_map/gate_matrix/pallas_call | solution.py:295
  129.9 0.0 copy-done.3
  129.9 1.3 copy.16
  131.2 0.0 copy-start.2
  131.2 101.5 %first_pass.1 = (f32[512,8192]{1,0:T(8,128)}, f32[512,8192]{1,0:T(8,128)}, bf16[8192,1024]{1,0:T(8,128)(2,1)}, bf16[4,4,4,256,1024]{4,3,2,1,0:T(8,128)(2,1)}, bf...) custom-call(bf16[512,1024]{1,0:T(8,128)(2,1)} %tok_ref.1, ...), custom_call_target="tpu_custom_call", output_to_operand_aliasing={{3}: (6, {})} | custom-call | flops 47244640256 | bytes 134217728 | tf_op jit(solution)/shard_map/first_pass/pallas_call | solution.py:368
  232.7 0.0 copy-done.2
  232.7 1.3 copy.19
  234.0 106.1 %second_pass.1 = (f32[512,8192]{1,0:T(8,128)}, bf16[8192,1024]{1,0:T(8,128)(2,1)}, bf16[4,4,4,128,1024]{4,3,2,1,0:T(8,128)(2,1)}, bf16[2,4,4,48,1024]{4,3,2,1,0:...) custom-call(bf16[512,1024]{1,0:T(8,128)(2,1)} %dy_ref.1, ...), custom_call_target="tpu_custom_call" | custom-call | flops 47244640256 | bytes 117440512 | tf_op jit(solution)/shard_map/second_pass/pallas_call | solution.py:564
  340.2 0.0 copy-start.4
  340.2 0.0 copy-start.1
  340.2 71.4 %out_pass.1 = (bf16[512,1024]{1,0:T(8,128)(2,1)}, bf16[512,1024]{1,0:T(8,128)(2,1)}, bf16[128,1024]{1,0:T(8,128)(2,1)}) custom-call(f32[512,8192]{1,0:T(8,128)} %get-tuple-element.28.w_ref, bf16[8192,1024]{1,0:T(8,128)(2,1)} %get-tuple-element.35.v_ref, f32[512,8192]{1,0:T(8,128)} %get-tuple-element.36.c_ref, bf16[8192,1024]{1,0:T(8,128)(2,1)} %get-tuple-element.37.u_ref, ...), custom_call_target="tpu_custom_call" | custom-call | flops 51539607552 | bytes 67108864 | tf_op jit(solution)/shard_map/out_pass/pallas_call | solution.py:617
  411.6 4.9 %all_gather.6 = bf16[256,1024]{1,0:T(8,128)(2,1)S(1)} all-gather(bf16[128,1024]{1,0:T(8,128)(2,1)} %get-tuple-element.44), channel_id=1, replica_groups=mesh['replica'=1,'data'=2,'table'=64] {'data'}, dimensions={0}, use_global_device_ids=true | all-gather | bytes 786432 | tf_op jit(solution)/shard_map/all_gather | solution.py:649
  416.5 0.0 copy-done.4
  416.5 2.2 all_gather.7
  418.7 2.3 copy.25
  420.9 2.3 copy.26
  423.2 0.8 copy.27
  424.0 0.8 copy.28
  424.8 0.0 copy-done.1
  (3 shorter events, 0.0 us)
Async XLA Ops:
  0.6 0.8 copy-start
  11.3 118.6 %copy-start.3 = (bf16[512,1024]{1,0:T(8,128)(2,1)S(1)}, bf16[512,1024]{1,0:T(8,128)(2,1)}, u32[]{:S(2)}) copy-start(bf16[512,1024]{1,0:T(8,128)(2,1)} %dy_ref.1) | copy-start | bytes 3145732
  131.2 101.5 %copy-start.2 = (bf16[512,1024]{1,0:T(8,128)(2,1)S(1)}, bf16[512,1024]{1,0:T(8,128)(2,1)}, u32[]{:S(2)}) copy-start(bf16[512,1024]{1,0:T(8,128)(2,1)} %tok_ref.1) | copy-start | bytes 3145732
  340.2 76.3 %copy-start.4 = (bf16[128,1024]{1,0:T(8,128)(2,1)S(1)}, bf16[128,1024]{1,0:T(8,128)(2,1)}, u32[]{:S(2)}) copy-start(bf16[128,1024]{1,0:T(8,128)(2,1)} %get-tuple-element.45) | copy-start | bytes 786436
  340.2 84.6 %copy-start.1 = (s32[1,8192]{1,0:T(1,128)S(1)}, s32[1,8192]{1,0:T(1,128)}, u32[]{:S(2)}) copy-start(s32[1,8192]{1,0:T(1,128)} %param.11) | copy-start | bytes 98308

commit v6 on v5

--- a/solution.py
+++ b/solution.py
@@ -11,7 +11,7 @@
 SIDE = 4
 OWN_STEP = 4
 VMEM_LIMIT = 60 * 1024 * 1024
-ROW_CUTS = (0, 48, 96, 128)
+ROW_CUTS = (0, 48, 88, 128)
 AXIS_ORDERS = ((2, 1, 0), (1, 0, 2), (0, 2, 1))
 
 
@@ -117,7 +117,7 @@
             copy = self.pair_copy(slot)
             copy.wait_recv()
             for j in range(OWN_STEP):
-                self.sum[slot, j] = (self.keep[slot, j].astype(F32) + self.got[slot, j].astype(F32)).astype(BF16)
+                self.sum[slot, j] = self.keep[slot, j] + self.got[slot, j]
             self.store_copy(step - 2).start()
             copy.wait_send()
 
@@ -165,7 +165,7 @@
         idx = [None] * 3
         for axis, val in zip(AXIS_ORDERS[k], (ia, ib, ic)):
             idx[axis] = val
-        start = pl.multiple_of(self.core * 128 + ROW_CUTS[k], 16)
+        start = pl.multiple_of(self.core * 128 + ROW_CUTS[k], 8)
         return self.full.at[idx[0], idx[1], idx[2], pl.ds(start, ROW_CUTS[k + 1] - ROW_CUTS[k])]
 
     def ends(self, num):
@@ -225,7 +225,7 @@
 GATE_STEPS = 16
 
 
-def gate_kernel(n_own, pick_ref, gate_ref, u_ref, v_ref, out_ref, full_u_ref, full_v_ref, tile_ref, *scratch):
+def gate_kernel(n_own, pick_ref, gate_ref, ids_ref, u_ref, v_ref, out_ref, idsb_ref, full_u_ref, full_v_ref, tile_ref, *scratch):
     step = pl.program_id(0)
     get_u = Gatherer(u_ref, full_u_ref, scratch[:5])
     get_v = Gatherer(v_ref, full_v_ref, scratch[5:])
@@ -235,20 +235,29 @@
         for get in (get_u, get_v):
             get.begin()
             get.send(1)
-
-    for mark, got, then in ((3, (0,), 2), (6, (1, 2), 3), (10, (3,), 4)):
-        @pl.when(step == mark)
-        def _(got=got, then=then):
+        for got, then in (((0,), 2), ((1, 2), 3), ((3,), 4)):
             for get in (get_u, get_v):
                 get.arrive(*got)
                 get.send(then)
                 get.spread(*got)
-
-    @pl.when(step == GATE_STEPS - 1)
-    def _():
         get_u.arrive(4, 5)
         get_u.send(5)
         get_u.spread(4, 5)
+
+    @pl.when(step == 2)
+    def _():
+        get_v.arrive(4, 5)
+        get_v.spread(4, 5)
+
+    @pl.when(step == 9)
+    def _():
+        get_u.arrive(6)
+        get_u.send(6)
+        get_u.spread(6)
+
+    for j in range(OWN_STEP):
+        row = ids_ref[pl.ds(step * OWN_STEP + j, 1), :].astype(F32)
+        idsb_ref[j * 128:(j + 1) * 128, :] = jnp.transpose(jnp.broadcast_to(row, (128, 128))).astype(jnp.int32)
 
     sel = pick_ref.shape[1]
     iota_own = lax.broadcasted_iota(jnp.int32, (n_own, sel), 0)
@@ -274,11 +283,6 @@
 
     @pl.when(step == GATE_STEPS - 1)
     def _():
-        get_v.arrive(4, 5)
-        get_v.spread(4, 5)
-        get_u.arrive(6)
-        get_u.send(6)
-        get_u.spread(6)
         get_v.finish(0, 1, 2, 3, 4, 5)
         get_u.arrive(7)
         get_u.spread(7)
@@ -287,7 +291,7 @@
         get_u.finish(0, 1, 2, 3, 4, 5, 6, 7, 8)
 
 
-def gate_matrix(pick_rel, gate, u_loc, v_loc, n_own):
+def gate_matrix(pick_rel, gate, ids, u_loc, v_loc, n_own):
     tok, sel = pick_rel.shape
     blk = tok // GATE_STEPS
     own = pl.BlockSpec(u_loc.shape, lambda i: (0, 0))
@@ -295,14 +299,14 @@
     return pl.pallas_call(
         functools.partial(gate_kernel, n_own),
         grid=(GATE_STEPS,),
-        in_specs=[pl.BlockSpec((blk, sel), lambda i: (i, 0)), pl.BlockSpec((blk, sel), lambda i: (i, 0)), own, own],
-        out_specs=[pl.BlockSpec((blk, n_own * 128), lambda i: (i, 0))] + [pl.BlockSpec(memory_space=pl.ANY)] * 2,
-        out_shape=[jax.ShapeDtypeStruct((tok, n_own * 128), F32), full, full],
+        in_specs=[pl.BlockSpec((blk, sel), lambda i: (i, 0)), pl.BlockSpec((blk, sel), lambda i: (i, 0)), pl.BlockSpec(ids.shape, lambda i: (0, 0)), own, own],
+        out_specs=[pl.BlockSpec((blk, n_own * 128), lambda i: (i, 0)), pl.BlockSpec((OWN_STEP * 128, 128), lambda i: (i, 0))] + [pl.BlockSpec(memory_space=pl.ANY)] * 2,
+        out_shape=[jax.ShapeDtypeStruct((tok, n_own * 128), F32), jax.ShapeDtypeStruct((n_own * 128, 128), jnp.int32), full, full],
         scratch_shapes=[pltpu.VMEM((8 * n_own, 128), F32)] + Gatherer.scratch() + Gatherer.scratch(),
         compiler_params=pltpu.CompilerParams(vmem_limit_bytes=VMEM_LIMIT, has_side_effects=True),
         cost_estimate=pl.CostEstimate(flops=2 * tok * 256 * 256 * 192, bytes_accessed=tok * n_own * 512, transcendentals=0),
         name="gate_matrix",
-    )(pick_rel, gate, u_loc, v_loc)
+    )(pick_rel, gate, ids, u_loc, v_loc)
 
 
 def first_kernel(tok_ref, dyt_ref, tab_ref, idsb_ref, ids_ref, gate_ref, held_ref, w_ref, slope_ref, sel_ref, full_ref, *rest):
@@ -315,13 +319,13 @@
     def _():
         get_v.send(5)
 
-    @pl.when(step == 5)
+    @pl.when(step == 6)
     def _():
         get_v.arrive(6)
         get_v.send(6)
         get_v.spread(6)
 
-    @pl.when(step == 12)
+    @pl.when(step == 13)
     def _():
         get_v.arrive(7)
         get_v.spread(7)
@@ -523,7 +527,7 @@
                     reducer.run(stage)
 
 
-SECOND_MARKS = ((1, 0), (2, 2), (3, 8), (4, 12), (5, 14), (6, 16), (7, None))
+SECOND_MARKS = ((1, 0), (2, 2), (3, 9), (4, 13), (5, 15), (6, 17), (7, None))
 OUT_MARKS = ((1, 0), (2, 2), (3, 8), (4, 11), (5, 13), (6, 15), (7, None))
 
 
@@ -641,9 +645,8 @@
         owners = jnp.arange(table_n, dtype=jnp.int32) ^ me
         ids = jnp.take(wanted.reshape(table_n, -1), owners, axis=0, mode='clip') - owners[:, None] * n_local
         ids_flip = ids ^ (core * half)
-        idsb = jnp.broadcast_to(ids.reshape(-1, 1), (ids.size, 128))
         pick_rel = pick.reshape(n_tok, -1) ^ (me << 7)
-        gates, full_u, full_v = gate_matrix(pick_rel, gate.reshape(n_tok, -1), u_loc, v_loc, table_n)
+        gates, idsb, full_u, full_v = gate_matrix(pick_rel, gate.reshape(n_tok, -1), ids, u_loc, v_loc, table_n)
         flat = lambda full: full.reshape(table_n * n_local, width)
 
         both_cores = lambda rows: lax.all_gather(rows, 'data', axis=0, tiled=True)

time: 425 us -> 423 us (level)
  local copies, waits for them, and re-layouts: 17.7 us -> 12.7 us
    pallas_call x1, Pallas kernels: 101 us -> 108 us  [first_pass(): pl.pallas_call(first_kernel, grid=(steps + LAG,), in_specs=[pl.BlockSpec(...]
    broadcast_in_dim x1 -> x0, local copies, waits for them, and re-layouts: 4.96 us -> none  [device_step(): idsb = jnp.broadcast_to(ids.reshape(-1, 1), (ids.size, 128))]
where the time goes in v6:
time: 423 us
  Pallas kernels  400 us (95%)
  local copies, waits for them, and re-layouts  12.7 us (3%)
  blocking collectives  7.08 us (2%)
    pallas_call x1, Pallas kernels, gate_matrix(): pl.pallas_call(functools.partial(gate_kernel, n_own), grid=(GATE_STEPS,),...  117 us
    pallas_call x1, Pallas kernels, first_pass(): pl.pallas_call(first_kernel, grid=(steps + LAG,), in_specs=[pl.BlockSpec(...  108 us
    pallas_call x1, Pallas kernels, second_pass(): pl.pallas_call(second_kernel, grid=(steps + LAG,), in_specs=[pl.BlockSpec...  105 us
    pallas_call x1, Pallas kernels, out_pass(): pl.pallas_call(out_kernel, grid=(n_list // cols,), in_specs=[mat_blk, row...  70.7 us
    unnamed x16, local copies, waits for them, and re-layouts  9.5 us

profile of v6, /device:TPU:1, one launch (start us, length us, event | category | flops | bytes accessed | tf_op | source)
XLA Modules:
  0.0 422.5 jit_solution(5626743137892979012)
XLA Ops:
  0.6 0.0 copy-start
  0.7 0.7 copy-done
  1.4 0.6 gather_fusion
  2.0 0.7 broadcast_xor_fusion.1
  2.7 1.0 broadcast_xor_fusion
  3.7 0.8 copy.17.pick_ref
  4.5 1.8 copy.18.gate_ref
  6.3 0.0 copy-start.3
  6.3 117.1 %gate_matrix.1 = (f32[512,8192]{1,0:T(8,128)}, s32[8192,128]{1,0:T(8,128)}, bf16[4,4,4,256,1024]{4,3,2,1,0:T(8,128)(2,1)}, bf16[4,4,4,256,1024]{4,3,2,1,0:T(8,128)(2,1)}) custom-call(s32[512,128]{1,0:T(8,128)} %copy.17.pick_ref, f32[512,128]{1,0:T(8,128)} %copy.18.gate_ref, s32[64,128]{1,0:T(8,128)} %get-tuple-element.49.ids_ref, bf16[256,1024]{1,0:T(8,128)(2,1)} %u_ref.1, ...), custom_call_target="tpu_custom_call" | custom-call | flops 12884901888 | bytes 16777216 | tf_op jit(solution)/shard_map/gate_matrix/pallas_call | solution.py:299
  123.4 0.0 copy-done.3
  123.4 1.3 copy.16
  124.8 0.0 copy-start.2
  124.8 107.7 %first_pass.1 = (f32[512,8192]{1,0:T(8,128)}, f32[512,8192]{1,0:T(8,128)}, bf16[8192,1024]{1,0:T(8,128)(2,1)}, bf16[4,4,4,256,1024]{4,3,2,1,0:T(8,128)(2,1)}, bf...) custom-call(bf16[512,1024]{1,0:T(8,128)(2,1)} %tok_ref.1, ...), custom_call_target="tpu_custom_call", output_to_operand_aliasing={{3}: (6, {})} | custom-call | flops 47244640256 | bytes 134217728 | tf_op jit(solution)/shard_map/first_pass/pallas_call | solution.py:372
  232.4 0.0 copy-done.2
  232.4 1.3 copy.19
  233.8 104.9 %second_pass.1 = (f32[512,8192]{1,0:T(8,128)}, bf16[8192,1024]{1,0:T(8,128)(2,1)}, bf16[4,4,4,128,1024]{4,3,2,1,0:T(8,128)(2,1)}, bf16[2,4,4,48,1024]{4,3,2,1,0:...) custom-call(bf16[512,1024]{1,0:T(8,128)(2,1)} %dy_ref.1, ...), custom_call_target="tpu_custom_call" | custom-call | flops 47244640256 | bytes 117440512 | tf_op jit(solution)/shard_map/second_pass/pallas_call | solution.py:568
  338.7 0.0 copy-start.4
  338.7 0.0 copy-start.1
  338.7 70.7 %out_pass.1 = (bf16[512,1024]{1,0:T(8,128)(2,1)}, bf16[512,1024]{1,0:T(8,128)(2,1)}, bf16[128,1024]{1,0:T(8,128)(2,1)}) custom-call(f32[512,8192]{1,0:T(8,128)} %get-tuple-element.30.w_ref, bf16[8192,1024]{1,0:T(8,128)(2,1)} %get-tuple-element.37.v_ref, f32[512,8192]{1,0:T(8,128)} %get-tuple-element.38.c_ref, bf16[8192,1024]{1,0:T(8,128)(2,1)} %get-tuple-element.39.u_ref, ...), custom_call_target="tpu_custom_call" | custom-call | flops 51539607552 | bytes 67108864 | tf_op jit(solution)/shard_map/out_pass/pallas_call | solution.py:621
  409.3 4.9 %all_gather.6 = bf16[256,1024]{1,0:T(8,128)(2,1)S(1)} all-gather(bf16[128,1024]{1,0:T(8,128)(2,1)} %get-tuple-element.46), channel_id=1, replica_groups=mesh['replica'=1,'data'=2,'table'=64] {'data'}, dimensions={0}, use_global_device_ids=true | all-gather | bytes 786432 | tf_op jit(solution)/shard_map/all_gather | solution.py:652
  414.2 0.0 copy-done.4
  414.2 2.2 all_gather.7
  416.4 2.3 copy.25
  418.7 2.3 copy.26
  420.9 0.8 copy.27
  421.7 0.8 copy.28
  422.5 0.0 copy-done.1
  (3 shorter events, 0.0 us)
Async XLA Ops:
  0.6 0.8 copy-start
  6.3 117.1 %copy-start.3 = (bf16[512,1024]{1,0:T(8,128)(2,1)S(1)}, bf16[512,1024]{1,0:T(8,128)(2,1)}, u32[]{:S(2)}) copy-start(bf16[512,1024]{1,0:T(8,128)(2,1)} %dy_ref.1) | copy-start | bytes 3145732
  124.8 107.7 %copy-start.2 = (bf16[512,1024]{1,0:T(8,128)(2,1)S(1)}, bf16[512,1024]{1,0:T(8,128)(2,1)}, u32[]{:S(2)}) copy-start(bf16[512,1024]{1,0:T(8,128)(2,1)} %tok_ref.1) | copy-start | bytes 3145732
  338.7 75.6 %copy-start.4 = (bf16[128,1024]{1,0:T(8,128)(2,1)S(1)}, bf16[128,1024]{1,0:T(8,128)(2,1)}, u32[]{:S(2)}) copy-start(bf16[128,1024]{1,0:T(8,128)(2,1)} %get-tuple-element.47) | copy-start | bytes 786436
  338.7 83.9 %copy-start.1 = (s32[1,8192]{1,0:T(1,128)S(1)}, s32[1,8192]{1,0:T(1,128)}, u32[]{:S(2)}) copy-start(s32[1,8192]{1,0:T(1,128)} %param.11) | copy-start | bytes 98308

commit v7 on v6

--- a/solution.py
+++ b/solution.py
@@ -194,10 +194,8 @@
         at = 9 * k + num
         return pltpu.make_async_remote_copy(src_ref=here, dst_ref=here, send_sem=self.pass_send.at[at], recv_sem=self.pass_recv.at[at], device_id={'data': 1 - self.core}, device_id_type=pl.DeviceIdType.MESH)
 
-    def begin(self):
-        own = pltpu.make_async_copy(self.own, self.full.at[0, 0, 0], self.own_sem.at[0])
-        own.start()
-        own.wait()
+    def own_copy(self):
+        return pltpu.make_async_copy(self.own, self.full.at[0, 0, 0], self.own_sem.at[0])
 
     def send(self, step):
         for k in range(3):
@@ -233,7 +231,9 @@
     @pl.when(step == 0)
     def _():
         for get in (get_u, get_v):
-            get.begin()
+            get.own_copy().start()
+        for get in (get_u, get_v):
+            get.own_copy().wait()
             get.send(1)
         for got, then in (((0,), 2), ((1, 2), 3), ((3,), 4)):
             for get in (get_u, get_v):
@@ -319,13 +319,13 @@
     def _():
         get_v.send(5)
 
-    @pl.when(step == 6)
+    @pl.when(step == 4)
     def _():
         get_v.arrive(6)
         get_v.send(6)
         get_v.spread(6)
 
-    @pl.when(step == 13)
+    @pl.when(step == 11)
     def _():
         get_v.arrive(7)
         get_v.spread(7)
@@ -528,7 +528,7 @@
 
 
 SECOND_MARKS = ((1, 0), (2, 2), (3, 9), (4, 13), (5, 15), (6, 17), (7, None))
-OUT_MARKS = ((1, 0), (2, 2), (3, 8), (4, 11), (5, 13), (6, 15), (7, None))
+OUT_MARKS = ((1, 0), (2, 1), (3, 4), (4, 6), (5, 7), (6, None), (7, None))
 
 
 def second_kernel(dy_ref, tokt_ref, tab_ref, idsb_ref, ids_ref, slope_ref, part_ref, f0_ref, f1_ref, f2_ref, c_ref, sel_ref, *rest):
@@ -614,7 +614,7 @@
 def out_pass(w, v_sel, c, u_sel, part, first):
     n_tok, n_list = w.shape
     width = v_sel.shape[1]
-    cols = 512
+    cols = 1024
     mat_blk = pl.BlockSpec((n_tok, cols), lambda i: (0, i))
     row_blk = pl.BlockSpec((cols, width), lambda i: (i, 0))
     whole = pl.BlockSpec((n_tok, width), lambda i: (0, 0))

time: 423 us -> 422 us (level)
  no operation moved by 1% of the time
where the time goes in v7:
time: 422 us; the launch traced here: 421 us
  Pallas kernels  397 us (94%)
  local copies, waits for them, and re-layouts  12.7 us (3%)
  blocking collectives  9.55 us (2%)
    pallas_call x1, Pallas kernels, gate_matrix(): pl.pallas_call(functools.partial(gate_kernel, n_own), grid=(GATE_STEPS,),...  117 us
    pallas_call x1, Pallas kernels, first_pass(): pl.pallas_call(first_kernel, grid=(steps + LAG,), in_specs=[pl.BlockSpec(...  104 us
    pallas_call x1, Pallas kernels, second_pass(): pl.pallas_call(second_kernel, grid=(steps + LAG,), in_specs=[pl.BlockSpec...  103 us
    pallas_call x1, Pallas kernels, out_pass(): pl.pallas_call(out_kernel, grid=(n_list // cols,), in_specs=[mat_blk, row...  71.8 us
    all_gather x2, blocking collectives, device_step(): both_cores = lambda rows: lax.all_gather(rows, 'data', axis=0, tiled=True)  9.55 us
    unnamed x16, local copies, waits for them, and re-layouts  9.5 us

profile of v7, /device:TPU:1, one launch (start us, length us, event | category | flops | bytes accessed | tf_op | source)
XLA Modules:
  0.0 421.2 jit_solution(6117529711294911768)
XLA Ops:
  0.6 0.0 copy-start
  0.7 0.7 copy-done
  1.4 0.6 gather_fusion
  2.0 0.7 broadcast_xor_fusion.1
  2.7 1.0 broadcast_xor_fusion
  3.7 0.8 copy.17.pick_ref
  4.5 1.8 copy.18.gate_ref
  6.3 0.0 copy-start.3
  6.3 117.1 %gate_matrix.1 = (f32[512,8192]{1,0:T(8,128)}, s32[8192,128]{1,0:T(8,128)}, bf16[4,4,4,256,1024]{4,3,2,1,0:T(8,128)(2,1)}, bf16[4,4,4,256,1024]{4,3,2,1,0:T(8,128)(2,1)}) custom-call(s32[512,128]{1,0:T(8,128)} %copy.17.pick_ref, f32[512,128]{1,0:T(8,128)} %copy.18.gate_ref, s32[64,128]{1,0:T(8,128)} %get-tuple-element.49.ids_ref, bf16[256,1024]{1,0:T(8,128)(2,1)} %u_ref.1, ...), custom_call_target="tpu_custom_call" | custom-call | flops 12884901888 | bytes 16777216 | tf_op jit(solution)/shard_map/gate_matrix/pallas_call | solution.py:299
  123.4 0.0 copy-done.3
  123.4 1.3 copy.16
  124.8 0.0 copy-start.2
  124.8 104.3 %first_pass.1 = (f32[512,8192]{1,0:T(8,128)}, f32[512,8192]{1,0:T(8,128)}, bf16[8192,1024]{1,0:T(8,128)(2,1)}, bf16[4,4,4,256,1024]{4,3,2,1,0:T(8,128)(2,1)}, bf...) custom-call(bf16[512,1024]{1,0:T(8,128)(2,1)} %tok_ref.1, ...), custom_call_target="tpu_custom_call", output_to_operand_aliasing={{3}: (6, {})} | custom-call | flops 47244640256 | bytes 134217728 | tf_op jit(solution)/shard_map/first_pass/pallas_call | solution.py:372
  229.1 0.0 copy-done.2
  229.1 1.3 copy.19
  230.4 103.3 %second_pass.1 = (f32[512,8192]{1,0:T(8,128)}, bf16[8192,1024]{1,0:T(8,128)(2,1)}, bf16[4,4,4,128,1024]{4,3,2,1,0:T(8,128)(2,1)}, bf16[2,4,4,48,1024]{4,3,2,1,0:...) custom-call(bf16[512,1024]{1,0:T(8,128)(2,1)} %dy_ref.1, ...), custom_call_target="tpu_custom_call" | custom-call | flops 47244640256 | bytes 117440512 | tf_op jit(solution)/shard_map/second_pass/pallas_call | solution.py:568
  333.8 0.0 copy-start.4
  333.8 0.0 copy-start.1
  333.8 71.8 %out_pass.1 = (bf16[512,1024]{1,0:T(8,128)(2,1)}, bf16[512,1024]{1,0:T(8,128)(2,1)}, bf16[128,1024]{1,0:T(8,128)(2,1)}) custom-call(f32[512,8192]{1,0:T(8,128)} %get-tuple-element.30.w_ref, bf16[8192,1024]{1,0:T(8,128)(2,1)} %get-tuple-element.37.v_ref, f32[512,8192]{1,0:T(8,128)} %get-tuple-element.38.c_ref, bf16[8192,1024]{1,0:T(8,128)(2,1)} %get-tuple-element.39.u_ref, ...), custom_call_target="tpu_custom_call" | custom-call | flops 51539607552 | bytes 67108864 | tf_op jit(solution)/shard_map/out_pass/pallas_call | solution.py:621
  405.6 7.4 %all_gather.6 = bf16[256,1024]{1,0:T(8,128)(2,1)S(1)} all-gather(bf16[128,1024]{1,0:T(8,128)(2,1)} %get-tuple-element.46), channel_id=1, replica_groups=mesh['replica'=1,'data'=2,'table'=64] {'data'}, dimensions={0}, use_global_device_ids=true | all-gather | bytes 786432 | tf_op jit(solution)/shard_map/all_gather | solution.py:652
  412.9 0.0 copy-done.4
  412.9 2.2 all_gather.7
  415.1 2.3 copy.25
  417.4 2.3 copy.26
  419.6 0.8 copy.27
  420.4 0.8 copy.28
  421.2 0.0 copy-done.1
  (3 shorter events, 0.0 us)
Async XLA Ops:
  0.6 0.8 copy-start
  6.3 117.1 %copy-start.3 = (bf16[512,1024]{1,0:T(8,128)(2,1)S(1)}, bf16[512,1024]{1,0:T(8,128)(2,1)}, u32[]{:S(2)}) copy-start(bf16[512,1024]{1,0:T(8,128)(2,1)} %dy_ref.1) | copy-start | bytes 3145732
  124.8 104.3 %copy-start.2 = (bf16[512,1024]{1,0:T(8,128)(2,1)S(1)}, bf16[512,1024]{1,0:T(8,128)(2,1)}, u32[]{:S(2)}) copy-start(bf16[512,1024]{1,0:T(8,128)(2,1)} %tok_ref.1) | copy-start | bytes 3145732
  333.8 79.2 %copy-start.4 = (bf16[128,1024]{1,0:T(8,128)(2,1)S(1)}, bf16[128,1024]{1,0:T(8,128)(2,1)}, u32[]{:S(2)}) copy-start(bf16[128,1024]{1,0:T(8,128)(2,1)} %get-tuple-element.47) | copy-start | bytes 786436
  333.8 87.5 %copy-start.1 = (s32[1,8192]{1,0:T(1,128)S(1)}, s32[1,8192]{1,0:T(1,128)}, u32[]{:S(2)}) copy-start(s32[1,8192]{1,0:T(1,128)} %param.11) | copy-start | bytes 98308
